TPU v7x, 32 devices: a whole 2x2x4 slice. The times are simulated.
32 devices in a mesh: dp: 2 (over y), shard: 16 (over z, x, core).
Axes of the slice: x: 2, y: 2, z: 4, core: 2. Of those that a mesh axis runs over, the one named last changes fastest.
Arguments:
- gradients: bfloat16 [2, 16, 2, 786432], P('dp', 'shard'), may hold values from -6 to 6
- tile_table: int32 [16, 96], replicated, may hold values from 0 to 1535, as said below
- master: float32 [16, 2, 786432], P('shard', 'dp'), may hold values from -0.072 to 0.072
- moment: float32 [16, 2, 786432], P('shard', 'dp'), may hold values from -6 to 6
- second: float32 [16, 2, 786432], P('shard', 'dp'), may hold values from 1 to 16
Outputs:
- master_new: float32 [16, 2, 786432], P('shard', 'dp')
- moment_new: float32 [16, 2, 786432], P('shard', 'dp')
- second_new: float32 [16, 2, 786432], P('shard', 'dp')
- tiles_out: bfloat16 [1536, 128, 128], P('shard')
- scales_out: bfloat16 [1536], P('shard')
Inputs may be any that keep to these rules, and one draw needn't show every extreme that they name: tile_table holds each number of 0 to 1535 once; each row holds exactly 6 numbers of every block of 96 consecutive numbers; in any row, the columns d * 48 to (d + 1) * 48 - 1 hold at most 3 numbers of one block, and this most is reached; over all rows together those columns hold exactly 48 numbers of every block.
All inputs are finite; a program needn't handle non-finite values.
Results may differ from a plain program's by a relative error of at most 0.0095.
Values may be sent and summed in bfloat16 or wider, within the bound.
No kernel may reach another device: no remote copies, remote signals or barrier semaphores. Data moves between devices by JAX's collectives and lax.ppermute only.
A program may use at most 64 MiB of HBM per device.

v0:
```python
import jax
import jax.numpy as jnp
from jax import lax
from jax.sharding import PartitionSpec as P

TB = 128


beta_first = 0.9
beta_second = 0.95
learning_rate = 0.002
weight_decay = 0.1
adam_epsilon = 1e-08
scale_epsilon = 1e-06
step_count = 10


def rank_within(owners):
    count = owners.shape[-1]
    position = jnp.arange(count, dtype=jnp.int32)
    same_owner = owners[..., :, None] == owners[..., None, :]
    earlier = position[None, :] < position[:, None]
    return jnp.sum(jnp.logical_and(same_owner, earlier), axis=-1)


def quantize(tile_set):
    largest = jnp.max(jnp.abs(tile_set), axis=(1, 2))
    tile_scale = (largest + scale_epsilon).astype(jnp.bfloat16)
    quantized = (tile_set / tile_scale.astype(jnp.float32)[:, None, None]).astype(jnp.bfloat16)
    return (quantized, tile_scale)


def per_device(gradients, tile_table, master, moment, second):
    summed = lax.psum_scatter(
        gradients.astype(jnp.float32).astype(jnp.bfloat16), "dp", scatter_dimension=2, tiled=True
    ).astype(jnp.float32)
    grad = summed.reshape(master.shape)
    moment_new = beta_first * moment + (1.0 - beta_first) * grad
    second_new = beta_second * second + (1.0 - beta_second) * grad * grad
    first_fix = 1.0 - beta_first**step_count
    second_fix = 1.0 - beta_second**step_count
    update = moment_new / first_fix / (jnp.sqrt(second_new / second_fix) + adam_epsilon)
    master_new = master - learning_rate * (update + weight_decay * master)
    owner_count = lax.axis_size("shard")
    owned = tile_table.shape[1]
    my_index = lax.axis_index("shard")
    all_owner = tile_table // owned
    is_mine = all_owner == my_index
    dp_count = lax.axis_size("dp")
    sub_len = owned // dp_count
    room = (sub_len + owner_count - 1) // owner_count
    my_part = lax.axis_index("dp")
    owner_cube = all_owner.reshape(owner_count, dp_count, sub_len)
    rank_cube = rank_within(owner_cube)
    owner_ids = jnp.arange(owner_count, dtype=jnp.int32)
    counts = jnp.sum((owner_cube[..., None] == owner_ids).astype(jnp.int32), axis=2)
    starts = jnp.cumsum(counts, axis=0) - counts
    compact = jnp.take_along_axis(starts, owner_cube, axis=2) + rank_cube
    my_owners = owner_cube[my_index, my_part]
    my_ranks = rank_cube[my_index, my_part]
    quantized, tile_scale = quantize(master_new.reshape(-1, TB, TB))
    target = my_owners * room + my_ranks
    outgoing_q = jnp.zeros((owner_count * room, TB, TB), jnp.bfloat16).at[target].set(quantized)
    outgoing_s = jnp.zeros((owner_count * room,), jnp.bfloat16).at[target].set(tile_scale)
    arrived_q, arrived_s = (
        lax.all_to_all(
            outgoing_q.reshape(owner_count, room, TB, TB),
            "shard",
            split_axis=0,
            concat_axis=0,
            tiled=True,
        ),
        lax.all_to_all(
            outgoing_s.reshape(owner_count, room), "shard", split_axis=0, concat_axis=0, tiled=True
        ),
    )
    part_owner = owner_cube[:, my_part]
    source_row = owner_ids[:, None] * room + rank_cube[:, my_part]
    pick_slot = jnp.where(part_owner == my_index, compact[:, my_part], sub_len)
    pick_order = jnp.zeros((sub_len,), jnp.int32).at[pick_slot].set(source_row, mode="drop")
    kept_q = arrived_q.reshape(owner_count * room, TB, TB)[pick_order]
    kept_s = arrived_s.reshape(owner_count * room)[pick_order]
    whole_q, whole_s = (
        lax.all_gather(kept_q, "dp", axis=0, tiled=True),
        lax.all_gather(kept_s, "dp", axis=0, tiled=True),
    )
    gathered_index = jnp.arange(dp_count, dtype=jnp.int32)[None, :, None] * sub_len + compact
    place_slot = jnp.where(is_mine, tile_table - my_index * owned, owned)
    place_order = (
        jnp.zeros((owned,), jnp.int32)
        .at[place_slot]
        .set(gathered_index.reshape(owner_count, owned), mode="drop")
    )
    tiles_out = whole_q[place_order]
    scales_out = whole_s[place_order]
    return (master_new, moment_new, second_new, tiles_out, scales_out)


def solution(mesh):
    in_specs = (
        P("dp", "shard", None, None),
        P(),
        P("shard", "dp", None),
        P("shard", "dp", None),
        P("shard", "dp", None),
    )
    out_specs = (
        P("shard", "dp", None),
        P("shard", "dp", None),
        P("shard", "dp", None),
        P("shard", None, None),
        P("shard"),
    )
    return jax.shard_map(
        per_device, mesh=mesh, in_specs=in_specs, out_specs=out_specs, check_vma=False
    )
```

profile of v0, /device:TPU:0, one launch (start us, length us, event | category | flops | bytes accessed | tf_op | source)
XLA Modules:
  0.0 232.8 jit_solution(14788937986147756043)
XLA Ops:
  7.2 0.7 all-reduce.4.cloned.1.call-update
  8.1 0.6 fusion.19
  8.7 0.9 convert_reduce_fusion
  9.6 89.3 %all-reduce.4.cloned.1.call-done = bf16[1,1,2,786432]{3,2,1,0:T(2,128)(2,1)} async-done(((bf16[1,1,2,786432]{3,2,1,0:T(2,128)(2,1)}), bf16[1,1,2,786432]{3,2,1,0:T(2,128)(2,1)}) %all-reduce.4.cloned.1.call-update) | async-done | bytes 3145744
  98.9 24.6 %multiply_subtract_fusion = (f32[1,1,786432]{2,1,0:T(1,128)S(1)}, f32[1,1,786432]{2,1,0:T(1,128)}, f32[1,1,786432]{2,1,0:T(1,128)}) fusion(f32[1,1,786432]{2,1,0:T(1,128)S(1)} %copy-done.1, bf16[1,1,2,786432]{3,2,1,0:T(2,128)(2,1)} %all-reduce.4.cloned.1.call-done, u32[]{:T(128)} %bitcast.2, f32[1,1,786432]{2,1,0:T(1,128)} %param.8, f32[1,1,786432]{2,1,0:T(1,128)} %param.9), kind=kLoop, calls=%fused_computation.15 | loop fusion | flops 12582912 | bytes 20447236 | tf_op jit(solution)/shard_map/sub | solution.py:43
  124.4 0.7 copy-done
  125.2 1.5 broadcast_in_dim.41
  126.7 6.6 %scatter_fusion = bf16[48,128,128]{2,1,0:T(8,128)(2,1)} fusion(bf16[48,128,128]{2,1,0:T(8,128)(2,1)} %broadcast_in_dim.41, s32[48]{0:T(128)S(1)} %fusion.9, bf16[48,128,128]{2,1,0:T(8,128)(2,1)S(1)} %divide_convert_fusion), kind=kCustom, calls=%fused_computation.5 | custom fusion | bytes 4718784 | tf_op jit(solution)/shard_map/scatter | solution.py:63
  133.2 5.6 %all-to-all-start = ((bf16[16,3,128,128]{3,2,1,0:T(8,128)(2,1)}), bf16[16,3,128,128]{3,2,1,0:T(8,128)(2,1)S(1)}, u32[]{:S(2)}, u32[]{:S(2)}) async-start(bf16[16,3,128,128]{3,2,1,0:T(8,128)(2,1)} %bitcast.8), calls=%async_computation | async-start | bytes 3145728 | tf_op jit(solution)/shard_map/all_to_all | solution.py:66
  139.1 0.7 convert_reduce_fusion.1
  139.8 14.4 %gather_fusion.4 = s32[1536]{0:T(1024)S(1)} fusion(s32[16,2,16]{2,1,0:T(2,128)S(1)} %reduce-window_subtract_fusion, s32[1536]{0:T(1024)S(1)} %reshape.250), kind=kCustom, calls=%fused_computation.4 | custom fusion | bytes 30720 | tf_op jit(solution)/shard_map/jit(take_along_axis)/gather | solution.py:58
  154.6 3.4 %scatter_custom_fusion.1 = s32[48]{0:T(128)S(1)} fusion(s32[768]{0:T(1024)S(1)} %reshape.266, s32[768]{0:T(1024)S(1)} %reshape.268, s32[]{:T(128)} %constant.35.clone.1), kind=kCustom, calls=%fused_computation.56 | custom fusion | bytes 196 | tf_op jit(solution)/shard_map/scatter | solution.py:80
  158.0 12.8 %all-to-all-done = bf16[16,3,128,128]{3,2,1,0:T(8,128)(2,1)S(1)} async-done(((bf16[16,3,128,128]{3,2,1,0:T(8,128)(2,1)}), bf16[16,3,128,128]{3,2,1,0:T(8,128)(2,1)S(1)}, u32[]{:S(2)}, u32[]{:S(2)}) %all-to-all-start) | async-done | bytes 1572896 | tf_op jit(solution)/shard_map/all_to_all | solution.py:66
  170.7 1.9 gather_fusion
  173.2 6.2 %scatter_custom_fusion.2 = s32[96]{0:T(128)S(1)} fusion(s32[1536]{0:T(1024)S(1)} %reshape.274, s32[1536]{0:T(1024)S(1)} %reshape.276, s32[]{:T(128)} %constant.35.clone.1), kind=kCustom, calls=%fused_computation.54 | custom fusion | bytes 388 | tf_op jit(solution)/shard_map/scatter | solution.py:92
  179.4 0.9 scatter_custom_fusion.3
  180.2 0.7 all_to_all.12
  180.9 9.1 %all-to-all-start.1 = ((bf16[16,1,3]{2,1,0:T(2,128)(2,1)}), bf16[16,1,3]{2,1,0:T(2,128)(2,1)S(1)}, u32[]{:S(2)}, u32[]{:S(2)}) async-start(bf16[16,1,3]{2,1,0:T(2,128)(2,1)} %all_to_all.12), calls=%async_computation.1 | async-start | bytes 16384 | tf_op jit(solution)/shard_map/all_to_all | solution.py:73
  190.7 5.8 %all-to-all-done.1 = bf16[16,1,3]{2,1,0:T(2,128)(2,1)S(1)} async-done(((bf16[16,1,3]{2,1,0:T(2,128)(2,1)}), bf16[16,1,3]{2,1,0:T(2,128)(2,1)S(1)}, u32[]{:S(2)}, u32[]{:S(2)}) %all-to-all-start.1) | async-done | bytes 128 | tf_op jit(solution)/shard_map/all_to_all | solution.py:73
  196.6 0.8 gather_fusion.2
  197.6 5.1 %all-reduce = bf16[96]{0:T(256)(128)(2,1)S(1)} all-reduce(bf16[96]{0:T(256)(128)(2,1)S(1)} %dynamic-update-slice), channel_id=3, replica_groups=mesh['dp'=2,'shard'=16] {'dp'}, use_global_device_ids=true, to_apply=%add | all-reduce | flops 96 | bytes 384
  202.7 1.7 gather_fusion.3
  204.5 16.9 %all-gather.4.cloned.1.call-done = bf16[96,128,128]{2,1,0:T(8,128)(2,1)} async-done(((bf16[48,128,128]{2,1,0:T(8,128)(2,1)}), bf16[96,128,128]{2,1,0:T(8,128)(2,1)}) %all-gather.4.cloned.1.call-update) | async-done | bytes 3145744 | tf_op jit(solution)/shard_map/all_gather | solution.py:84
  221.4 4.6 %gather_fusion.1 = bf16[96,128,128]{2,1,0:T(8,128)(2,1)} fusion(bf16[96,128,128]{2,1,0:T(8,128)(2,1)} %all-gather.4.cloned.1.call-done, s32[1024]{0:T(1024)S(1)} %pad_clamp_fusion), kind=kCustom, calls=%fused_computation.1 | custom fusion | bytes 6291840 | tf_op jit(solution)/shard_map/gather | solution.py:94
  (44 shorter events, 2.6 us)
Async XLA Ops:
  7.2 0.9 copy-start.3
  7.2 0.8 copy-start.2
  7.2 91.7 %copy-start.1 = (f32[1,1,786432]{2,1,0:T(1,128)S(1)}, f32[1,1,786432]{2,1,0:T(1,128)}, u32[]{:S(2)}) copy-start(f32[1,1,786432]{2,1,0:T(1,128)} %param.7) | copy-start | bytes 9437188
  7.2 91.7 %all-reduce.4.cloned.1.call-start = ((), (), s32[]{:S(2)}) async-start(), calls=%async_computation.3 | async-start | bytes 6291456
  123.5 1.7 copy-start
  133.2 37.5 %all-to-all-start = ((bf16[16,3,128,128]{3,2,1,0:T(8,128)(2,1)}), bf16[16,3,128,128]{3,2,1,0:T(8,128)(2,1)S(1)}, u32[]{:S(2)}, u32[]{:S(2)}) async-start(bf16[16,3,128,128]{3,2,1,0:T(8,128)(2,1)} %bitcast.8), calls=%async_computation | async-start | bytes 3145728 | tf_op jit(solution)/shard_map/all_to_all | solution.py:66
  138.9 82.5 %all-gather.4.cloned.1.call-start = ((), (), s32[]{:S(2)}) async-start(), calls=%async_computation.2 | async-start | bytes 4718592 | tf_op jit(solution)/shard_map/all_gather | solution.py:84
  180.9 15.5 %all-to-all-start.1 = ((bf16[16,1,3]{2,1,0:T(2,128)(2,1)}), bf16[16,1,3]{2,1,0:T(2,128)(2,1)S(1)}, u32[]{:S(2)}, u32[]{:S(2)}) async-start(bf16[16,1,3]{2,1,0:T(2,128)(2,1)} %all_to_all.12), calls=%async_computation.1 | async-start | bytes 16384 | tf_op jit(solution)/shard_map/all_to_all | solution.py:73
Sparse Core Ops, SparseCore 0:
  10.3 88.5 all-reduce.3
  172.8 48.5 all-gather.3
where the time goes:
time: 233 us
  waiting for transfers between devices  125 us (54%)
  local copies, waits for them, and re-layouts  45.2 us (19%)
  other arithmetic  27.3 us (12%)
  between operations  14.9 us (6%)
  starting transfers between devices  14.8 us (6%)
  blocking collectives  5.12 us (2%)
    unnamed x3, waiting for transfers between devices  90 us
    sub x1, other arithmetic, per_device(): master_new = master - learning_rate * (update + weight_decay * master)  24.6 us
    all_gather x1, waiting for transfers between devices, per_device(): lax.all_gather(kept_q, 'dp', axis=0, tiled=True)  16.9 us
    gather x4, local copies, waits for them, and re-layouts, per_device(): compact = jnp.take_along_axis(starts, owner_cube, axis=2) + rank_cube  14.6 us
    all_to_all x1, waiting for transfers between devices, per_device(): lax.all_to_all(outgoing_q.reshape(owner_count, room, TB, TB), 'shard', sp...  12.8 us
    all_to_all x1, starting transfers between devices, per_device(): lax.all_to_all(outgoing_s.reshape(owner_count, room), 'shard', split_axis...  9.11 us
    scatter x1, local copies, waits for them, and re-layouts, per_device(): jnp.zeros((owner_count * room, TB, TB), jnp.bfloat16).at[target]  6.58 us
    scatter x1, local copies, waits for them, and re-layouts, per_device(): place_order = jnp.zeros((owned,), jnp.int32).at[place_slot].set(gathered_...  6.17 us
  transfers between devices with their start and end apart: 4, of which 4 were waited for; matrix products, arithmetic and copies ran while one was open for 13% of the time, Pallas kernels for 0%

commit v1 on v0

v1 whole, which is shorter than its diff:
```python
import functools

import jax
import jax.numpy as jnp
from jax import lax
from jax.experimental import pallas as pl
from jax.experimental.pallas import tpu as pltpu
from jax.sharding import PartitionSpec as P


TB = 128
LANES = 128

beta_first = 0.9
beta_second = 0.95
learning_rate = 0.002
weight_decay = 0.1
adam_epsilon = 1e-08
scale_epsilon = 1e-06
step_count = 10

HBM = pl.BlockSpec(memory_space=pltpu.HBM)
VMEM = pl.BlockSpec(memory_space=pltpu.VMEM)
SMEM = pl.BlockSpec(memory_space=pltpu.SMEM)


def in_hbm(arrays):
    return [pltpu.with_memory_space_constraint(a, pltpu.HBM) for a in arrays]


def rank_within(owners):
    position = jnp.arange(owners.shape[-1], dtype=jnp.int32)
    same_owner = owners[..., :, None] == owners[..., None, :]
    earlier = position[None, :] < position[:, None]
    return jnp.sum((same_owner & earlier).astype(jnp.int32), axis=-1)


def extract(raw, wide, part, parts):
    wide[...] = raw[...].astype(jnp.float32)
    return wide[pl.ds(part, TB, stride=parts), :]


def fill_order(part, table, row, owners, parts, room, owned, order, count):
    sub_len = owned // parts

    def clear(k, carry):
        order[part * room * owners + k] = 0
        return carry

    def zero(k, carry):
        count[k] = 0
        return carry

    def enter(t, carry):
        owner = table[row, part * sub_len + t] // owned
        rank = count[owner]
        count[owner] = rank + 1
        order[(part * room + rank) * owners + owner] = t
        return carry

    if room * owners != sub_len:
        lax.fori_loop(0, room * owners, clear, 0)
    lax.fori_loop(0, owners, zero, 0, unroll=True)
    lax.fori_loop(0, sub_len, enter, 0, unroll=4)


def pack_kernel(chunk, shift, owners, parts, room, owned, lead, *refs):
    if lead:
        table, grads, order, out, raw, wide, sems, count = refs
        row = lax.axis_index("shard")
        fill = functools.partial(
            fill_order,
            table=table,
            row=row,
            owners=owners,
            parts=parts,
            room=room,
            owned=owned,
            order=order,
            count=count,
        )
        fill(lax.rem(lax.axis_index("dp") + shift, parts))
    else:
        order, grads, out, raw, wide, sems = refs
    part = lax.rem(lax.axis_index("dp") + shift, parts)
    base = (part * room + chunk) * owners
    slots = raw.shape[0]

    def fetch(i):
        slot = lax.rem(i, slots)
        return pltpu.make_async_copy(grads.at[order[base + i]], raw.at[slot], sems.at[slot])

    for i in range(min(slots, owners)):
        fetch(i).start()
    if lead:
        for s in range(parts - 1):
            fill(lax.rem(lax.axis_index("dp") + shift + 1 + s, parts))

    def body(i, carry):
        fetch(i).wait()
        out[i] = extract(raw.at[lax.rem(i, slots)], wide, part, parts).astype(out.dtype)

        @pl.when(i + slots < owners)
        def _():
            fetch(i + slots).start()

        return carry

    lax.fori_loop(0, owners, body, 0)


def adam_kernel(chunk, last, owners, parts, room, *refs):
    order, _, grads, master, moment, second = refs[:6]
    refs = refs[6:]
    if chunk:
        sc_in, refs = refs[0], refs[1:]
    arrived = refs[: parts - 1]
    refs = refs[parts - 1 + (3 if chunk else 0) :]
    outs = refs[:3]
    record = refs[3]
    sc_out = refs[4]
    raw, wide, states, news, peak, scale, quant, in_sems, out_sems, quant_sems = refs[5:]
    part = lax.axis_index("dp")
    base = (part * room + chunk) * owners

    def fetches(i):
        tile = order[base + i]
        copies = [pltpu.make_async_copy(grads.at[tile], raw.at[i], in_sems.at[0, i])]
        for k, ref in enumerate((master, moment, second)):
            copies.append(pltpu.make_async_copy(ref.at[tile], states.at[k, i], in_sems.at[k + 1, i]))
        return copies

    def stores(i):
        tile = order[base + i]
        return [pltpu.make_async_copy(news.at[k, i], outs[k].at[tile], out_sems.at[k, i]) for k in range(3)]

    def start_fetch(i, carry):
        for copy in fetches(i):
            copy.start()
        return carry

    lax.fori_loop(0, owners, start_fetch, 0)
    first_fix = 1.0 / (1.0 - beta_first**step_count)
    second_fix = 1.0 / (1.0 - beta_second**step_count)
    rows = 32

    def update(i, carry):
        for copy in fetches(i):
            copy.wait()
        wide[...] = raw[i].astype(jnp.float32)
        top = None
        for b in range(0, TB, rows):
            at = pl.ds(b, rows)
            grad = wide[pl.ds(b * parts + part, rows, stride=parts), :]
            for ref in arrived:
                grad = grad + ref[i, at, :].astype(jnp.float32)
            moment_new = beta_first * states[1, i, at, :] + (1.0 - beta_first) * grad
            second_new = beta_second * states[2, i, at, :] + (1.0 - beta_second) * grad * grad
            old = states[0, i, at, :]
            step = moment_new * first_fix / (jnp.sqrt(second_new * second_fix) + adam_epsilon)
            master_new = old - learning_rate * (step + weight_decay * old)
            news[0, i, at, :] = master_new
            news[1, i, at, :] = moment_new
            news[2, i, at, :] = second_new
            size = jnp.abs(master_new)
            for s in range(0, rows, 8):
                top = size[s : s + 8] if top is None else jnp.maximum(top, size[s : s + 8])
        peak[i] = top
        for copy in stores(i):
            copy.start()
        return carry

    lax.fori_loop(0, owners, update, 0)
    largest = jnp.max(jnp.max(peak[...], axis=2, keepdims=True), axis=1, keepdims=True)
    rounded = (largest + scale_epsilon).astype(jnp.bfloat16).astype(jnp.float32)
    rounded = jnp.broadcast_to(rounded, peak.shape)
    peak[...] = 1.0 / rounded
    row = lax.broadcasted_iota(jnp.int32, scale.shape, 1)
    scale[...] = jnp.where(row == chunk, jnp.broadcast_to(rounded[:, :1], scale.shape), sc_in[...] if chunk else 0.0)

    def send(i):
        return pltpu.make_async_copy(quant.at[i], record.at[i], quant_sems.at[i])

    def quantize(i, carry):
        inverse = peak[i]
        for b in range(0, TB, 16):
            pair = [news[0, i, pl.ds(b + s, 8), :] * inverse for s in (0, 8)]
            quant[i, pl.ds(b, 16), :] = jnp.concatenate(pair, axis=0).astype(quant.dtype)
        if last:
            quant[i, pl.ds(TB, scale.shape[1]), :] = scale[i].astype(quant.dtype)
        send(i).start()
        return carry

    lax.fori_loop(0, owners, quantize, 0)
    sc_out[...] = scale[...]

    def finish(i, carry):
        send(i).wait()
        for copy in stores(i):
            copy.wait()
        return carry

    lax.fori_loop(0, owners, finish, 0)


def place_kernel(sources, scale_sources, owners, room, owned, first, *refs):
    slots = refs[0]
    count = len(sources)
    records = refs[1 : 1 + count]
    scales = refs[1 + count : 1 + count + len(scale_sources)]
    refs = refs[1 + count + len(scale_sources) + (0 if first else 1) :]
    tiles_out = refs[0]
    if scale_sources:
        scales_out = refs[1]
    sems = refs[-1]
    here = lax.axis_index("dp")
    parts = slots.shape[0] // (room * owners)

    def index(chunk, shift, i):
        part = lax.rem(here + parts - shift, parts)
        return slots[(part * room + chunk) * owners + i]

    def copy(n, i, slot):
        return pltpu.make_async_copy(records[n].at[i, pl.ds(0, TB)], tiles_out.at[slot], sems.at[n, i])

    for n, (chunk, shift) in enumerate(sources):

        def start(i, carry, n=n, chunk=chunk, shift=shift):
            slot = index(chunk, shift, i)

            @pl.when(slot >= 0)
            def _():
                copy(n, i, slot).start()

            return carry

        lax.fori_loop(0, owners, start, 0)
    if scale_sources:
        lane = lax.broadcasted_iota(jnp.int32, scales_out.shape, 1)
        scales_out[...] = jnp.zeros(scales_out.shape, scales_out.dtype)
        for n, shift in enumerate(scale_sources):

            def gather(i, carry, n=n, shift=shift):
                block = scales[n][i, pl.ds(TB, scales[n].shape[1] - TB), :].astype(jnp.float32)
                total = scales_out[...]
                for r in range(room):
                    wide = jnp.concatenate([block[r : r + 1]] * (scales_out.shape[1] // LANES), axis=1)
                    total = jnp.where(lane == index(r, shift, i), wide, total)
                scales_out[...] = total
                return carry

            lax.fori_loop(0, owners, gather, 0)
    for n, (chunk, shift) in enumerate(sources):

        def end(i, carry, n=n, chunk=chunk, shift=shift):
            slot = index(chunk, shift, i)

            @pl.when(slot >= 0)
            def _():
                copy(n, i, slot).wait()

            return carry

        lax.fori_loop(0, owners, end, 0)


def per_device(gradients, tile_table, master, moment, second):
    owners = lax.axis_size("shard")
    parts = lax.axis_size("dp")
    owned = tile_table.shape[1]
    sub_len = owned // parts
    room = (sub_len + owners - 1) // owners
    me = lax.axis_index("shard")
    tiles = master.size // (TB * TB)
    pad = (room + 7) // 8 * 8

    cube = tile_table.reshape(owners, parts, sub_len)
    cube_owner = cube // owned
    cube_rank = rank_within(cube_owner)
    chunk_ids = jnp.arange(room, dtype=jnp.int32)
    mine = (cube_owner == me)[:, :, None, :] & (cube_rank[:, :, None, :] == chunk_ids[:, None])
    slots = jnp.sum(jnp.where(mine, cube[:, :, None, :] - me * owned + 1, 0), axis=-1) - 1
    slots = slots.transpose(1, 2, 0).reshape(-1)

    grads = gradients.reshape(parts, tiles, TB, TB).transpose(1, 2, 0, 3).reshape(tiles, TB * parts, TB)
    states = [a.reshape(tiles, TB, TB) for a in (master, moment, second)]
    tile_bytes = TB * TB * 2 * parts
    ring = max(2, min(owners, (4 << 20) // tile_bytes))
    perms = {s: [(d, (d + s) % parts) for d in range(parts)] for s in range(1, parts)}
    f32_tiles = pltpu.HBM((tiles, TB, TB), jnp.float32)

    arrived = []
    for r in range(room):
        got = []
        for s in range(1, parts):
            lead = r == 0 and s == 1
            result = pl.pallas_call(
                functools.partial(pack_kernel, r, s, owners, parts, room, owned, lead),
                out_shape=[jax.ShapeDtypeStruct((parts * room * owners,), jnp.int32)] * lead
                + [jax.ShapeDtypeStruct((owners, TB, TB), jnp.bfloat16)],
                in_specs=[SMEM, HBM],
                out_specs=[SMEM] * lead + [VMEM],
                scratch_shapes=[
                    pltpu.VMEM((ring, TB * parts, TB), jnp.bfloat16),
                    pltpu.VMEM((TB * parts, TB), jnp.float32),
                    pltpu.SemaphoreType.DMA((ring,)),
                ]
                + [pltpu.SMEM((owners,), jnp.int32)] * lead,
                compiler_params=pltpu.CompilerParams(vmem_limit_bytes=16 << 20),
                cost_estimate=pl.CostEstimate(flops=6000000, bytes_accessed=2 << 20, transcendentals=0),
            )(tile_table if lead else order, *in_hbm([grads]))
            if lead:
                order, packed = result
            else:
                (packed,) = result
            got.append(lax.ppermute(packed, "dp", perms[s]))
        arrived.append(got)

    news = []
    sc = []
    mine_r, theirs_r = [], []
    for r in range(room):
        last = r == room - 1
        height = TB + (pad if last else 0)
        count = 6 + len(sc) + parts - 1
        *news, record, scale_rows = pl.pallas_call(
            functools.partial(adam_kernel, r, last, owners, parts, room),
            out_shape=[f32_tiles] * 3
            + [pltpu.HBM((owners, height, TB), jnp.bfloat16), jax.ShapeDtypeStruct((owners, pad, LANES), jnp.float32)],
            in_specs=[SMEM, SMEM, HBM, HBM, HBM, HBM] + [VMEM] * (len(sc) + parts - 1) + [HBM] * len(news),
            out_specs=[HBM] * 4 + [VMEM],
            input_output_aliases={count + k: k for k in range(len(news))},
            scratch_shapes=[
                pltpu.VMEM((owners, TB * parts, TB), jnp.bfloat16),
                pltpu.VMEM((TB * parts, TB), jnp.float32),
                pltpu.VMEM((3, owners, TB, TB), jnp.float32),
                pltpu.VMEM((3, owners, TB, TB), jnp.float32),
                pltpu.VMEM((owners, 8, LANES), jnp.float32),
                pltpu.VMEM((owners, pad, LANES), jnp.float32),
                pltpu.VMEM((owners, height, TB), jnp.bfloat16),
                pltpu.SemaphoreType.DMA((4, owners)),
                pltpu.SemaphoreType.DMA((3, owners)),
                pltpu.SemaphoreType.DMA((owners,)),
            ],
            compiler_params=pltpu.CompilerParams(vmem_limit_bytes=40 << 20),
            cost_estimate=pl.CostEstimate(flops=30000000, bytes_accessed=8 << 20, transcendentals=0),
        )(order, slots, *in_hbm([grads, *states]), *sc, *arrived[r], *in_hbm(news))
        kept = lax.all_to_all(record, "shard", split_axis=0, concat_axis=0, tiled=True)
        sc = [scale_rows]
        mine_r.append(kept)
        theirs_r.append([])
        for s in range(1, parts):
            theirs_r[r].append(lax.ppermute(kept, "dp", perms[s]))

    early = [((r, 0), mine_r[r]) for r in range(room)]
    early += [((r, s), theirs_r[r][s - 1]) for r in range(room - 1) for s in range(1, parts)]
    late = [((room - 1, s), theirs_r[room - 1][s - 1]) for s in range(1, parts)]
    tiles_shape = pltpu.HBM((owned, TB, TB), jnp.bfloat16)
    width = (owned + LANES - 1) // LANES * LANES

    def place(group, scale_group, previous):
        outs = [tiles_shape]
        out_specs = [HBM]
        if scale_group:
            outs.append(jax.ShapeDtypeStruct((1, width), jnp.float32))
            out_specs.append(VMEM)
        count = 1 + len(group) + len(scale_group)
        return pl.pallas_call(
            functools.partial(
                place_kernel,
                [k for k, _ in group],
                [k for k, _ in scale_group],
                owners,
                room,
                owned,
                not previous,
            ),
            out_shape=outs,
            in_specs=[SMEM] + [VMEM] * (count - 1) + [HBM] * len(previous),
            out_specs=out_specs,
            input_output_aliases={count: 0} if previous else {},
            scratch_shapes=[pltpu.SemaphoreType.DMA((len(group), owners))],
            compiler_params=pltpu.CompilerParams(vmem_limit_bytes=16 << 20),
            name="place_late" if previous else "place_early",
        )(slots, *[a for _, a in group], *[a for _, a in scale_group], *in_hbm(previous))

    (tiles_out,) = place(early, [], [])
    scale_group = [(0, mine_r[-1])] + [(s, theirs_r[-1][s - 1]) for s in range(1, parts)]
    tiles_out, scales = place(late, scale_group, [tiles_out])
    scales_out = scales[0, :owned].astype(jnp.bfloat16)
    return (*[a.reshape(master.shape) for a in news], tiles_out, scales_out)


def solution(mesh):
    in_specs = (
        P("dp", "shard", None, None),
        P(),
        P("shard", "dp", None),
        P("shard", "dp", None),
        P("shard", "dp", None),
    )
    out_specs = (
        P("shard", "dp", None),
        P("shard", "dp", None),
        P("shard", "dp", None),
        P("shard", None, None),
        P("shard"),
    )

    return jax.shard_map(per_device, mesh=mesh, in_specs=in_specs, out_specs=out_specs, check_vma=False)
```

time: 233 us -> 134 us (0.58)
  waiting for transfers between devices: 125 us -> 60 us
  local copies, waits for them, and re-layouts: 45.2 us -> 1.55 us
  Pallas kernels: 0 us -> 28.7 us
  other arithmetic: 27.3 us -> 1.13 us
  blocking collectives: 5.12 us -> 22.4 us
  between operations: 14.9 us -> 0.78 us
  starting transfers between devices: 14.8 us -> 18.5 us
    unnamed x3 -> x0, waiting for transfers between devices: 90 us -> none
    ppermute x0 -> x6, waiting for transfers between devices: none -> 47.8 us  [the longest x3 26.3 us: per_device(): got.append(lax.ppermute(packed, 'dp', perms[s]))]
    pallas_call x0 -> x8, Pallas kernels: none -> 28.7 us  [the longest x3 17.3 us: per_device(): pl.pallas_call(functools.partial(adam_kernel, r, last, owners, parts, roo...]
    sub x1, other arithmetic: 24.6 us -> 0.01 us  [per_device(): jnp.sum(jnp.where(mine, cube[:, :, None, :] - me * owned + 1, 0), axis=-1)]
    gather x8 -> x0, local copies, waits for them, and re-layouts: 23.7 us -> none  [the longest x4 14.6 us: per_device(): compact = jnp.take_along_axis(starts, owner_cube, axis=2) + rank_cube]
    all_to_all x0 -> x1, blocking collectives: none -> 22.4 us  [per_device(): lax.all_to_all(record, 'shard', split_axis=0, concat_axis=0, tiled=True)]
    scatter x4 -> x0, local copies, waits for them, and re-layouts: 17 us -> none  [the longest x1 6.58 us: per_device(): jnp.zeros((owner_count * room, TB, TB), jnp.bfloat16).at[target]]
    all_gather x1 -> x0, waiting for transfers between devices: 16.9 us -> none  [per_device(): lax.all_gather(kept_q, 'dp', axis=0, tiled=True)]
  transfers between devices with their start and end apart: 4 -> 8, of which waited for: 4 -> 6; matrix products, arithmetic and copies ran while one was open for 13% -> 1% of each run, Pallas kernels for 0% -> 14%
where the time goes in v1:
time: 134 us; the launch traced here: 133 us
  waiting for transfers between devices  60 us (45%)
  Pallas kernels  28.7 us (21%)
  blocking collectives  22.4 us (17%)
  starting transfers between devices  18.5 us (14%)
  local copies, waits for them, and re-layouts  1.55 us (1%)
    ppermute x3, waiting for transfers between devices, per_device(): got.append(lax.ppermute(packed, 'dp', perms[s]))  26.3 us
    all_to_all x1, blocking collectives, per_device(): lax.all_to_all(record, 'shard', split_axis=0, concat_axis=0, tiled=True)  22.4 us
    ppermute x3, waiting for transfers between devices, per_device(): theirs_r[r].append(lax.ppermute(kept, 'dp', perms[s]))  21.5 us
    pallas_call x3, Pallas kernels, per_device(): pl.pallas_call(functools.partial(adam_kernel, r, last, owners, parts, roo...  17.3 us
    all_to_all x2, waiting for transfers between devices, per_device(): lax.all_to_all(record, 'shard', split_axis=0, concat_axis=0, tiled=True)  12.1 us
    all_to_all x2, starting transfers between devices, per_device(): lax.all_to_all(record, 'shard', split_axis=0, concat_axis=0, tiled=True)  9.71 us
    pallas_call x3, Pallas kernels, per_device(): pl.pallas_call(functools.partial(pack_kernel, r, s, owners, parts, room,...  7.12 us
    ppermute x3, starting transfers between devices, per_device(): got.append(lax.ppermute(packed, 'dp', perms[s]))  5.22 us
  transfers between devices with their start and end apart: 8, of which 6 were waited for; matrix products, arithmetic and copies ran while one was open for 1% of the time, Pallas kernels for 14%

profile of v1, /device:TPU:0, one launch (start us, length us, event | category | flops | bytes accessed | tf_op | source)
XLA Modules:
  0.0 133.0 jit_solution(7667591504801279342)
XLA Ops:
  0.6 0.7 copy-done
  1.3 3.2 %shard_map.92 = (s32[96]{0:T(128)S(1)}, bf16[16,128,128]{2,1,0:T(8,128)(2,1)S(1)}) custom-call(s32[16,96]{1,0:T(8,128)S(1)} %copy-done, bf16[48,256,128]{2,1,0:T(8,128)(2,1)} %bitcast.15), custom_call_target="tpu_custom_call" | custom-call | flops 6000000 | bytes 2097152 | tf_op jit(solution)/shard_map/pallas_call | solution.py:297
  4.6 3.1 %collective-permute-start = (bf16[16,128,128]{2,1,0:T(8,128)(2,1)S(1)}, bf16[16,128,128]{2,1,0:T(8,128)(2,1)S(1)}, u32[]{:S(2)}, u32[]{:S(2)}) collective-permute-start(bf16[16,128,128]{2,1,0:T(8,128)(2,1)S(1)} %get-tuple-element.24), channel_id=1, source_target_pairs={{0,16},{16,0},{1,17},{17,1},{2,18},{18,2},{3,19},{19,3},{4,20},{20... | collective-permute-start | bytes 1572872 | tf_op jit(solution)/shard_map/ppermute | solution.py:316
  7.9 0.9 convert_reduce_fusion
  9.1 10.4 %collective-permute-done.refs_6_ = bf16[16,128,128]{2,1,0:T(8,128)(2,1)S(1)} collective-permute-done((bf16[16,128,128]{2,1,0:T(8,128)(2,1)S(1)}, bf16[16,128,128]{2,1,0:T(8,128)(2,1)S(1)}, u32[]{:S(2)}, u32[]{:S(2)}) %collective-permute-start) | collective-permute-done | bytes 524320 | tf_op jit(solution)/shard_map/ppermute | solution.py:316
  19.5 5.6 %shard_map.93 = (f32[48,128,128]{2,1,0:T(8,128)}, f32[48,128,128]{2,1,0:T(8,128)}, f32[48,128,128]{2,1,0:T(8,128)}, bf16[16,128,128]{2,1,0:T(8,128)(2,1)}, f32[16,8,128]{2,1,0:T(8,128)S(1)}) custom-call(s32[96]{0:T(128)S(1)} %get-tuple-element.23.refs_0_, s32[96]{0:T(128)S(1)} %reshape.121.refs_1_.refs_0_, bf16[48,256,128]{2,1,0:T(8,128)(2,1)} %bitcast.16, ...), custom_call_target="tpu_custom_call" | custom-call | flops 30000000 | bytes 8388608 | tf_op jit(solution)/shard_map/pallas_call | solution.py:326
  25.1 6.1 %all-to-all-start.1 = ((bf16[16,128,128]{2,1,0:T(8,128)(2,1)}), bf16[16,128,128]{2,1,0:T(8,128)(2,1)S(1)}, u32[]{:S(2)}, u32[]{:S(2)}) async-start(bf16[16,128,128]{2,1,0:T(8,128)(2,1)} %get-tuple-element.37), calls=%async_computation.1 | async-start | bytes 1048576 | tf_op jit(solution)/shard_map/all_to_all | solution.py:348
  31.3 2.0 %shard_map.94 = bf16[16,128,128]{2,1,0:T(8,128)(2,1)S(1)} custom-call(s32[96]{0:T(128)S(1)} %get-tuple-element.23.refs_0_, bf16[48,256,128]{2,1,0:T(8,128)(2,1)} %bitcast.17), custom_call_target="tpu_custom_call" | custom-call | flops 6000000 | bytes 2097152 | tf_op jit(solution)/shard_map/pallas_call | solution.py:297
  33.2 1.6 %collective-permute-start.1 = (bf16[16,128,128]{2,1,0:T(8,128)(2,1)S(1)}, bf16[16,128,128]{2,1,0:T(8,128)(2,1)S(1)}, u32[]{:S(2)}, u32[]{:S(2)}) collective-permute-start(bf16[16,128,128]{2,1,0:T(8,128)(2,1)S(1)} %shard_map.94), channel_id=1, source_target_pairs={{0,16},{16,0},{1,17},{17,1},{2,18},{18,2},{3,19},{19,3},{4,20},{20... | collective-permute-start | bytes 1572872 | tf_op jit(solution)/shard_map/ppermute | solution.py:316
  34.8 1.9 %shard_map.96 = bf16[16,128,128]{2,1,0:T(8,128)(2,1)S(1)} custom-call(s32[96]{0:T(128)S(1)} %get-tuple-element.23.refs_0_, bf16[48,256,128]{2,1,0:T(8,128)(2,1)} %bitcast.18), custom_call_target="tpu_custom_call" | custom-call | flops 6000000 | bytes 2097152 | tf_op jit(solution)/shard_map/pallas_call | solution.py:297
  36.8 0.6 collective-permute-start.2
  37.3 10.7 %collective-permute-done.1.refs_7_ = bf16[16,128,128]{2,1,0:T(8,128)(2,1)S(1)} collective-permute-done((bf16[16,128,128]{2,1,0:T(8,128)(2,1)S(1)}, bf16[16,128,128]{2,1,0:T(8,128)(2,1)S(1)}, u32[]{:S(2)}, u32[]{:S(2)}) %collective-permute-start.1) | collective-permute-done | bytes 524320 | tf_op jit(solution)/shard_map/ppermute | solution.py:316
  48.1 5.6 %shard_map.95 = (f32[48,128,128]{2,1,0:T(8,128)}, f32[48,128,128]{2,1,0:T(8,128)}, f32[48,128,128]{2,1,0:T(8,128)}, bf16[16,128,128]{2,1,0:T(8,128)(2,1)}, f32[16,8,128]{2,1,0:T(8,128)S(1)}) custom-call(s32[96]{0:T(128)S(1)} %get-tuple-element.23.refs_0_, ...), custom_call_target="tpu_custom_call", output_to_operand_aliasing={{0}: (8, {}), {1}: (9, {}), {2}: (10, {})} | custom-call | flops 30000000 | bytes 8388608 | tf_op jit(solution)/shard_map/pallas_call | solution.py:326
  53.7 5.1 %collective-permute-done.2.refs_7_ = bf16[16,128,128]{2,1,0:T(8,128)(2,1)S(1)} collective-permute-done((bf16[16,128,128]{2,1,0:T(8,128)(2,1)S(1)}, bf16[16,128,128]{2,1,0:T(8,128)(2,1)S(1)}, u32[]{:S(2)}, u32[]{:S(2)}) %collective-permute-start.2) | collective-permute-done | bytes 524320 | tf_op jit(solution)/shard_map/ppermute | solution.py:316
  58.8 6.2 %shard_map.97 = (f32[48,128,128]{2,1,0:T(8,128)}, f32[48,128,128]{2,1,0:T(8,128)}, f32[48,128,128]{2,1,0:T(8,128)}, bf16[16,136,128]{2,1,0:T(8,128)(2,1)}, f32[16,8,128]{2,1,0:T(8,128)}) custom-call(s32[96]{0:T(128)S(1)} %get-tuple-element.23.refs_0_, s32[96]{0:T(128)S(1)} %reshape.121.refs_1_.refs_0_, ...), custom_call_target="tpu_custom_call", output_to_operand_aliasing={{0}: (8, {}), {1}: (9, {}), {2}: (10, {})} | custom-call | flops 30000000 | bytes 8388608 | tf_op jit(solution)/shard_map/pallas_call | solution.py:326
  65.0 22.4 %all_to_all.15.refs_3_.refs_2_ = bf16[16,136,128]{2,1,0:T(8,128)(2,1)S(1)} all-to-all(bf16[16,136,128]{2,1,0:T(8,128)(2,1)} %get-tuple-element.36), channel_id=1, replica_groups=mesh['dp'=2,'shard'=16] {'shard'}, dimensions={0} | all-to-all | bytes 1114112 | tf_op jit(solution)/shard_map/all_to_all | solution.py:348
  87.4 3.6 %all-to-all-start.2 = ((bf16[16,128,128]{2,1,0:T(8,128)(2,1)}), bf16[16,128,128]{2,1,0:T(8,128)(2,1)S(1)}, u32[]{:S(2)}, u32[]{:S(2)}) async-start(bf16[16,128,128]{2,1,0:T(8,128)(2,1)} %get-tuple-element.38), calls=%async_computation.2 | async-start | bytes 1048576 | tf_op jit(solution)/shard_map/all_to_all | solution.py:348
  91.0 1.6 %collective-permute-start.3 = (bf16[16,136,128]{2,1,0:T(8,128)(2,1)S(1)}, bf16[16,136,128]{2,1,0:T(8,128)(2,1)S(1)}, u32[]{:S(2)}, u32[]{:S(2)}) collective-permute-start(bf16[16,136,128]{2,1,0:T(8,128)(2,1)S(1)} %all_to_all.15.refs_3_.refs_2_), channel_id=1, source_target_pairs={{0,16},{16,0},{1,17},{17,1},{2,18},{18,2},{3,19},{19,3},{4,20},{20... | collective-permute-start | bytes 1671176 | tf_op jit(solution)/shard_map/ppermute | solution.py:353
  93.1 12.1 %all-to-all-done.2.refs_2_ = bf16[16,128,128]{2,1,0:T(8,128)(2,1)S(1)} async-done(((bf16[16,128,128]{2,1,0:T(8,128)(2,1)}), bf16[16,128,128]{2,1,0:T(8,128)(2,1)S(1)}, u32[]{:S(2)}, u32[]{:S(2)}) %all-to-all-start.2) | async-done | bytes 524320 | tf_op jit(solution)/shard_map/all_to_all | solution.py:348
  105.2 1.5 %collective-permute-start.5 = (bf16[16,128,128]{2,1,0:T(8,128)(2,1)S(1)}, bf16[16,128,128]{2,1,0:T(8,128)(2,1)S(1)}, u32[]{:S(2)}, u32[]{:S(2)}) collective-permute-start(bf16[16,128,128]{2,1,0:T(8,128)(2,1)S(1)} %all-to-all-done.2.refs_2_), channel_id=1, source_target_pairs={{0,16},{16,0},{1,17},{17,1},{2,18},{18,2},{3,19},{19,3},{4,20},{20... | collective-permute-start | bytes 1572872 | tf_op jit(solution)/shard_map/ppermute | solution.py:353
  106.7 11.0 %collective-permute-done.4.refs_4_ = bf16[16,128,128]{2,1,0:T(8,128)(2,1)S(1)} collective-permute-done((bf16[16,128,128]{2,1,0:T(8,128)(2,1)S(1)}, bf16[16,128,128]{2,1,0:T(8,128)(2,1)S(1)}, u32[]{:S(2)}, u32[]{:S(2)}) %collective-permute-start.4) | collective-permute-done | bytes 524320 | tf_op jit(solution)/shard_map/ppermute | solution.py:353
  117.8 10.5 %collective-permute-done.5.refs_5_ = bf16[16,128,128]{2,1,0:T(8,128)(2,1)S(1)} collective-permute-done((bf16[16,128,128]{2,1,0:T(8,128)(2,1)S(1)}, bf16[16,128,128]{2,1,0:T(8,128)(2,1)S(1)}, u32[]{:S(2)}, u32[]{:S(2)}) %collective-permute-start.5) | collective-permute-done | bytes 524320 | tf_op jit(solution)/shard_map/ppermute | solution.py:353
  128.3 2.7 %place_early.1.refs_4_ = bf16[96,128,128]{2,1,0:T(8,128)(2,1)} custom-call(s32[96]{0:T(128)S(1)} %reshape.121.refs_1_.refs_0_, bf16[16,128,128]{2,1,0:T(8,128)(2,1)S(1)} %all-to-all-done.1.refs_1_, bf16[16,128,128]{2,1,0:T(8,128)(2,1)S(1)} %all-to-all-done.2.refs_2_, bf16[16,136,128]{2,1,0:T(8,128)(2,1)S(1)} %all_to_all.15.refs_3_.refs_2_, ...), custom_call_target="tpu_custom_call" | custom-call | tf_op jit(solution)/shard_map/place_early/pallas_call | solution.py:368
  131.0 1.5 %place_late.1 = (bf16[96,128,128]{2,1,0:T(8,128)(2,1)}, f32[1,128]{1,0:T(1,128)S(1)}) custom-call(s32[96]{0:T(128)S(1)} %reshape.121.refs_1_.refs_0_, bf16[16,136,128]{2,1,0:T(8,128)(2,1)S(1)} %collective-permute-done.3.refs_1_.refs_3_, bf16[16,136,128]{2,1,0:T(8,128)(2,1)S(1)} %all_to_all.15.refs_3_.refs_2_, ...), custom_call_target="tpu_custom_call", output_to_operand_aliasing={{0}: (4, {})} | custom-call | tf_op jit(solution)/shard_map/place_late/pallas_call | solution.py:368
  (21 shorter events, 1.6 us)
Async XLA Ops:
  0.6 0.7 copy-start
  1.3 6.4 %copy-start.1 = (s32[16,96]{1,0:T(8,128)S(1)}, s32[16,96]{1,0:T(8,128)}, u32[]{:S(2)}) copy-start(s32[16,96]{1,0:T(8,128)} %refs_0_.1) | copy-start | bytes 18436
  4.6 15.0 %collective-permute-start = (bf16[16,128,128]{2,1,0:T(8,128)(2,1)S(1)}, bf16[16,128,128]{2,1,0:T(8,128)(2,1)S(1)}, u32[]{:S(2)}, u32[]{:S(2)}) collective-permute-start(bf16[16,128,128]{2,1,0:T(8,128)(2,1)S(1)} %get-tuple-element.24), channel_id=1, source_target_pairs={{0,16},{16,0},{1,17},{17,1},{2,18},{18,2},{3,19},{19,3},{4,20},{20... | collective-permute-start | bytes 1572872 | tf_op jit(solution)/shard_map/ppermute | solution.py:316
  25.1 39.9 %all-to-all-start.1 = ((bf16[16,128,128]{2,1,0:T(8,128)(2,1)}), bf16[16,128,128]{2,1,0:T(8,128)(2,1)S(1)}, u32[]{:S(2)}, u32[]{:S(2)}) async-start(bf16[16,128,128]{2,1,0:T(8,128)(2,1)} %get-tuple-element.37), calls=%async_computation.1 | async-start | bytes 1048576 | tf_op jit(solution)/shard_map/all_to_all | solution.py:348
  33.2 14.9 %collective-permute-start.1 = (bf16[16,128,128]{2,1,0:T(8,128)(2,1)S(1)}, bf16[16,128,128]{2,1,0:T(8,128)(2,1)S(1)}, u32[]{:S(2)}, u32[]{:S(2)}) collective-permute-start(bf16[16,128,128]{2,1,0:T(8,128)(2,1)S(1)} %shard_map.94), channel_id=1, source_target_pairs={{0,16},{16,0},{1,17},{17,1},{2,18},{18,2},{3,19},{19,3},{4,20},{20... | collective-permute-start | bytes 1572872 | tf_op jit(solution)/shard_map/ppermute | solution.py:316
  36.8 22.0 %collective-permute-start.2 = (bf16[16,128,128]{2,1,0:T(8,128)(2,1)S(1)}, bf16[16,128,128]{2,1,0:T(8,128)(2,1)S(1)}, u32[]{:S(2)}, u32[]{:S(2)}) collective-permute-start(bf16[16,128,128]{2,1,0:T(8,128)(2,1)S(1)} %shard_map.96), channel_id=1, source_target_pairs={{0,16},{16,0},{1,17},{17,1},{2,18},{18,2},{3,19},{19,3},{4,20},{20... | collective-permute-start | bytes 1572872 | tf_op jit(solution)/shard_map/ppermute | solution.py:316
  87.4 17.8 %all-to-all-start.2 = ((bf16[16,128,128]{2,1,0:T(8,128)(2,1)}), bf16[16,128,128]{2,1,0:T(8,128)(2,1)S(1)}, u32[]{:S(2)}, u32[]{:S(2)}) async-start(bf16[16,128,128]{2,1,0:T(8,128)(2,1)} %get-tuple-element.38), calls=%async_computation.2 | async-start | bytes 1048576 | tf_op jit(solution)/shard_map/all_to_all | solution.py:348
  91.0 40.0 %collective-permute-start.3 = (bf16[16,136,128]{2,1,0:T(8,128)(2,1)S(1)}, bf16[16,136,128]{2,1,0:T(8,128)(2,1)S(1)}, u32[]{:S(2)}, u32[]{:S(2)}) collective-permute-start(bf16[16,136,128]{2,1,0:T(8,128)(2,1)S(1)} %all_to_all.15.refs_3_.refs_2_), channel_id=1, source_target_pairs={{0,16},{16,0},{1,17},{17,1},{2,18},{18,2},{3,19},{19,3},{4,20},{20... | collective-permute-start | bytes 1671176 | tf_op jit(solution)/shard_map/ppermute | solution.py:353
  92.6 25.2 %collective-permute-start.4 = (bf16[16,128,128]{2,1,0:T(8,128)(2,1)S(1)}, bf16[16,128,128]{2,1,0:T(8,128)(2,1)S(1)}, u32[]{:S(2)}, u32[]{:S(2)}) collective-permute-start(bf16[16,128,128]{2,1,0:T(8,128)(2,1)S(1)} %all-to-all-done.1.refs_1_), channel_id=1, source_target_pairs={{0,16},{16,0},{1,17},{17,1},{2,18},{18,2},{3,19},{19,3},{4,20},{20... | collective-permute-start | bytes 1572872 | tf_op jit(solution)/shard_map/ppermute | solution.py:353
  105.2 23.1 %collective-permute-start.5 = (bf16[16,128,128]{2,1,0:T(8,128)(2,1)S(1)}, bf16[16,128,128]{2,1,0:T(8,128)(2,1)S(1)}, u32[]{:S(2)}, u32[]{:S(2)}) collective-permute-start(bf16[16,128,128]{2,1,0:T(8,128)(2,1)S(1)} %all-to-all-done.2.refs_2_), channel_id=1, source_target_pairs={{0,16},{16,0},{1,17},{17,1},{2,18},{18,2},{3,19},{19,3},{4,20},{20... | collective-permute-start | bytes 1572872 | tf_op jit(solution)/shard_map/ppermute | solution.py:353

commit v2 on v0

v2 whole, which is shorter than its diff:
```python
import functools

import jax
import jax.numpy as jnp
from jax import lax
from jax.experimental import pallas as pl
from jax.experimental.pallas import tpu as pltpu
from jax.sharding import PartitionSpec as P


TB = 128
LANES = 128
UNROLL = 2
PACK_MIB = 4
ADAM_MIB = 4


beta_first = 0.9
beta_second = 0.95
learning_rate = 0.002
weight_decay = 0.1
adam_epsilon = 1e-08
scale_epsilon = 1e-06
step_count = 10

HBM = pl.BlockSpec(memory_space=pltpu.HBM)
VMEM = pl.BlockSpec(memory_space=pltpu.VMEM)
SMEM = pl.BlockSpec(memory_space=pltpu.SMEM)


def in_hbm(arrays):
    return [pltpu.with_memory_space_constraint(a, pltpu.HBM) for a in arrays]


def in_vmem(arrays):
    return [pltpu.with_memory_space_constraint(a, pltpu.VMEM) for a in arrays]


def extract(raw, wide, part, parts):
    wide[...] = raw[...].astype(jnp.float32)
    return wide[pl.ds(part, TB, stride=parts), :]


def other(index, step, size):
    if size & (size - 1) == 0:
        return index ^ step
    return (index + step) % size


def back(index, step, size):
    if size & (size - 1) == 0:
        return index ^ step
    return (index + size - step) % size


class Plan:
    def __init__(self, parts, owners, owned, tiles):
        self.parts, self.owners, self.owned, self.tiles = parts, owners, owned, tiles
        self.sub_len = owned // parts
        self.room = (self.sub_len + owners - 1) // owners
        self.far = 4 if owners % 4 == 0 and owners > 4 else 1
        self.near = owners // self.far
        self.chunks = [self.far - 1] + list(range(1, self.far - 1)) + [0] if self.far > 1 else [0]
        self.per_chunk = self.near * self.room
        self.pad = (self.room + 7) // 8 * 8
        self.height = self.room * TB + self.pad

    def pattern(self, k, q):
        pairs = []
        for i in range(self.owners):
            far, near = divmod(i, self.near)
            pairs.append((i, other(far, k, self.far) * self.near + other(near, q, self.near)))
        return pairs

    def source(self, me, k, q):
        return back(me // self.near, k, self.far) * self.near + back(me % self.near, q, self.near)


def step_between(here, there, size):
    if size & (size - 1) == 0:
        return here ^ there
    return lax.rem(there + size - here, size)


def fill_order(part, plan, table, order, count):
    me = lax.axis_index("shard")
    entries = plan.owners * plan.room

    def clear(j, carry):
        order[part * entries + j] = 0
        return carry

    def zero(j, carry):
        count[j] = 0
        return carry

    def enter(t, carry):
        owner = table[me, part * plan.sub_len + t] // plan.owned
        rank = count[owner]
        count[owner] = rank + 1
        k = step_between(me // plan.near, owner // plan.near, plan.far)
        q = step_between(me % plan.near, owner % plan.near, plan.near)
        order[part * entries + (k * plan.near + q) * plan.room + rank] = t
        return carry

    if entries != plan.sub_len:
        lax.fori_loop(0, entries, clear, 0)
    lax.fori_loop(0, plan.owners, zero, 0, unroll=True)
    lax.fori_loop(0, plan.sub_len, enter, 0, unroll=4)


def pack_kernel(plan, chunk, shift, lead, loads, *refs):
    parts, entries = plan.parts, plan.per_chunk
    part = lax.rem(lax.axis_index("dp") + shift, parts)
    base = part * plan.owners * plan.room + chunk * entries
    if lead:
        table, source = refs[:2]
        order, out, grads, wide, rows, count, sems = refs[2:]
        copies = [pltpu.make_async_copy(table, rows, sems.at[0]), pltpu.make_async_copy(source, grads, sems.at[1])]
    else:
        order, grads = refs[:2]
        sources, out = refs[2 : 2 + loads], refs[2 + loads]
        targets, wide = refs[3 + loads : 3 + 2 * loads], refs[3 + 2 * loads]
        copies = [pltpu.make_async_copy(a, b, refs[-1].at[n]) for n, (a, b) in enumerate(zip(sources, targets))]
    for copy in copies:
        copy.start()
    if lead:
        copies[0].wait()
        fill_order(part, plan, rows, order, count)
        copies[1].wait()

    def body(i, carry):
        out[i] = extract(grads.at[order[base + i]], wide, part, parts).astype(out.dtype)
        return carry

    lax.fori_loop(0, entries, body, 0)
    if lead:
        for s in range(1, parts):
            fill_order(lax.rem(part + s, parts), plan, rows, order, count)
    else:
        for copy in copies:
            copy.wait()


def adam_kernel(plan, chunk, first, *refs):
    parts, entries, room = plan.parts, plan.per_chunk, plan.room
    order, grads, master, moment, second = refs[:5]
    arrived = refs[5 : 4 + parts]
    refs = refs[4 + parts + (0 if first else 3) :]
    master_out, moment_out, second_out = refs[:3]
    blocks = refs[3 : 3 + plan.near]
    wide, peak = refs[3 + plan.near :]
    part = lax.axis_index("dp")
    base = part * plan.owners * room + chunk * entries
    first_fix = 1.0 / (1.0 - beta_first**step_count)
    second_fix = 1.0 / (1.0 - beta_second**step_count)
    rows = 32

    def update(i, carry):
        tile = order[base + i]
        wide[...] = grads[tile].astype(jnp.float32)
        top = None
        for b in range(0, TB, rows):
            at = pl.ds(b, rows)
            grad = wide[pl.ds(b * parts + part, rows, stride=parts), :]
            for ref in arrived:
                grad = grad + ref[i, at, :].astype(jnp.float32)
            moment_new = beta_first * moment[tile, at, :] + (1.0 - beta_first) * grad
            second_new = beta_second * second[tile, at, :] + (1.0 - beta_second) * grad * grad
            old = master[tile, at, :]
            step = moment_new * first_fix / (jnp.sqrt(second_new * second_fix) + adam_epsilon)
            master_new = old - learning_rate * (step + weight_decay * old)
            master_out[tile, at, :] = master_new
            moment_out[tile, at, :] = moment_new
            second_out[tile, at, :] = second_new
            size = jnp.abs(master_new)
            for s in range(0, rows, 8):
                top = size[s : s + 8] if top is None else jnp.maximum(top, size[s : s + 8])
        peak[i] = top
        return carry

    lax.fori_loop(0, entries, update, 0, unroll=UNROLL)
    largest = jnp.max(jnp.max(peak[...], axis=2, keepdims=True), axis=1, keepdims=True)
    rounded = (largest + scale_epsilon).astype(jnp.bfloat16).astype(jnp.float32)
    peak[...] = jnp.broadcast_to(rounded, peak.shape)
    row = lax.broadcasted_iota(jnp.int32, (plan.pad, LANES), 0)
    for q, block in enumerate(blocks):
        tail = jnp.zeros((plan.pad, LANES), jnp.float32)
        for r in range(room):
            i = q * room + r
            tile = order[base + i]
            scale = peak[i]
            inverse = 1.0 / scale
            tail = jnp.where(row == r, jnp.concatenate([scale] * (plan.pad // 8), axis=0), tail)
            for b in range(0, TB, 16):
                pair = [master_out[tile, pl.ds(b + s, 8), :] * inverse for s in (0, 8)]
                block[pl.ds(r * TB + b, 16), :] = jnp.concatenate(pair, axis=0).astype(block.dtype)
        block[pl.ds(room * TB, plan.pad), :] = tail.astype(block.dtype)


def slots_kernel(plan, table, out):
    me = lax.axis_index("shard")
    owned, sub_len = plan.owned, plan.sub_len
    local = table[...] - me * owned
    mine = (local >= 0) & (local < owned)
    before = lax.broadcasted_iota(jnp.int32, (owned, owned), 0)
    after = lax.broadcasted_iota(jnp.int32, (owned, owned), 1)
    same = before // sub_len == after // sub_len
    counts = jnp.where((before < after) & same, 1.0, 0.0).astype(jnp.bfloat16)
    flags = jnp.where(mine, 1.0, 0.0).astype(jnp.bfloat16)
    rank = jnp.dot(flags, counts, preferred_element_type=jnp.float32)
    column = lax.broadcasted_iota(jnp.int32, local.shape, 1) // sub_len
    lane = lax.broadcasted_iota(jnp.int32, out.shape, 1)
    value = jnp.where(mine, local + 1, 0).astype(jnp.float32)
    total = jnp.zeros(out.shape, jnp.float32)
    for part in range(plan.parts):
        for r in range(plan.room):
            chosen = jnp.where((column == part) & (rank == float(r)), value, 0.0)
            found = jnp.sum(chosen, axis=1, keepdims=True)
            total = jnp.where(lane == part * plan.room + r, found, total)
    out[...] = total.astype(jnp.int32) - 1


def store_kernel(*refs):
    sems = refs[-1]
    count = (len(refs) - 1) // 2
    copies = [pltpu.make_async_copy(refs[n], refs[count + n], sems.at[n]) for n in range(count)]
    for copy in copies:
        copy.start()
    for copy in copies:
        copy.wait()


def place_kernel(plan, sources, count, first, *refs):
    room = plan.room
    slots, blocks = refs[0], refs[1 : 1 + count]
    if first:
        tiles_out, scales_out, sems = refs[1 + count :]
    else:
        scales_in, _, tiles_out, scales_out, sems = refs[1 + count :]
    here, me = lax.axis_index("dp"), lax.axis_index("shard")
    lane = lax.broadcasted_iota(jnp.int32, scales_out.shape, 1)
    total = jnp.zeros(scales_out.shape, jnp.float32) if first else scales_in[...]
    entries, views = [], []
    for n, (ref, k, q, shift, at) in enumerate(sources):
        views.append(blocks[ref] if at is None else blocks[ref].at[at])
        part = lax.rem(here + plan.parts - shift, plan.parts)
        row = plan.source(me, k, q)
        for r in range(room):
            slot = slots[row, part * room + r]
            copy = pltpu.make_async_copy(views[n].at[pl.ds(r * TB, TB)], tiles_out.at[slot], sems.at[n * room + r])
            entries.append((slot, copy))
            if room * plan.owners == plan.sub_len:
                copy.start()
            else:
                pl.when(slot >= 0)(copy.start)
    for n in range(len(views)):
        tail = views[n][pl.ds(room * TB, plan.pad), :].astype(jnp.float32)
        for r in range(room):
            wide = jnp.concatenate([tail[r : r + 1]] * (scales_out.shape[1] // LANES), axis=1)
            total = jnp.where(lane == entries[n * room + r][0], wide, total)
    scales_out[...] = total
    for slot, copy in entries:
        if room * plan.owners == plan.sub_len:
            copy.wait()
        else:
            pl.when(slot >= 0)(copy.wait)


def per_device(gradients, tile_table, master, moment, second):
    owners = lax.axis_size("shard")
    parts = lax.axis_size("dp")
    owned = tile_table.shape[1]
    tiles = master.size // (TB * TB)
    plan = Plan(parts, owners, owned, tiles)
    room, entries = plan.room, plan.per_chunk

    slots = pl.pallas_call(
        functools.partial(slots_kernel, plan),
        out_shape=jax.ShapeDtypeStruct((owners, (parts * room + LANES - 1) // LANES * LANES), jnp.int32),
        in_specs=[VMEM],
        out_specs=VMEM,
        compiler_params=pltpu.CompilerParams(vmem_limit_bytes=2 << 20),
        cost_estimate=pl.CostEstimate(flops=5000000, bytes_accessed=2 << 20, transcendentals=0),
        name="slots",
    )(*in_hbm([tile_table]))

    grads = gradients.reshape(parts, tiles, TB, TB).transpose(1, 2, 0, 3).reshape(tiles, TB * parts, TB)
    states = [a.reshape(tiles, TB, TB) for a in (master, moment, second)]
    cycles = {s: [(d, (d + s) % parts) for d in range(parts)] for s in range(1, parts)}
    f32_tiles = pltpu.VMEM((tiles, TB, TB), jnp.float32)
    block_shape = pltpu.VMEM((plan.height, TB), jnp.bfloat16)

    order = None
    waiting = list(states)
    states = []
    arrived = {}
    calls = [(k, s) for k in plan.chunks for s in range(1, parts)]
    packed_shape = pltpu.VMEM((entries, TB, TB), jnp.bfloat16)
    wide_shape = pltpu.VMEM((TB * parts, TB), jnp.float32)
    for n, (k, s) in enumerate(calls):
        lead = n == 0
        loading = [] if lead else waiting[: len(waiting) if n == len(calls) - 1 else 1]
        if lead:
            operands = in_hbm([tile_table, grads])
            in_specs, out_specs = [HBM, HBM], [SMEM, VMEM, VMEM]
            out_shape = [
                jax.ShapeDtypeStruct((parts * room * owners,), jnp.int32),
                packed_shape,
                pltpu.VMEM(grads.shape, grads.dtype),
            ]
            scratch = [
                wide_shape,
                pltpu.SMEM(tile_table.shape, jnp.int32),
                pltpu.SMEM((owners,), jnp.int32),
                pltpu.SemaphoreType.DMA((2,)),
            ]
        else:
            operands = [order, *in_vmem([grads]), *in_hbm(loading)]
            in_specs, out_specs = [SMEM, VMEM] + [HBM] * len(loading), [VMEM] * (1 + len(loading))
            out_shape = [packed_shape] + [f32_tiles] * len(loading)
            scratch = [wide_shape] + [pltpu.SemaphoreType.DMA((len(loading),))] * bool(loading)
        result = pl.pallas_call(
            functools.partial(pack_kernel, plan, k, s, lead, len(loading)),
            out_shape=out_shape,
            in_specs=in_specs,
            out_specs=out_specs,
            scratch_shapes=scratch,
            compiler_params=pltpu.CompilerParams(vmem_limit_bytes=PACK_MIB << 20),
            cost_estimate=pl.CostEstimate(flops=6000000, bytes_accessed=2 << 20, transcendentals=0),
        )(*operands)
        if lead:
            order, packed, grads = result
        else:
            packed = result[0]
            states += result[1:]
            waiting = waiting[len(loading) :]
        arrived.setdefault(k, []).append(lax.ppermute(packed, "dp", cycles[s]))
    states += waiting

    news = []
    groups = {}
    for k in plan.chunks:
        count = 5 + parts - 1
        results = pl.pallas_call(
            functools.partial(adam_kernel, plan, k, not news),
            out_shape=[f32_tiles] * 3 + [block_shape] * plan.near,
            in_specs=[SMEM] + [VMEM] * (3 + parts) + [VMEM] * len(news),
            out_specs=[VMEM] * (3 + plan.near),
            input_output_aliases={count + j: j for j in range(len(news))},
            scratch_shapes=[pltpu.VMEM((TB * parts, TB), jnp.float32), pltpu.VMEM((entries, 8, LANES), jnp.float32)],
            compiler_params=pltpu.CompilerParams(vmem_limit_bytes=ADAM_MIB << 20),
            cost_estimate=pl.CostEstimate(flops=25000000, bytes_accessed=6 << 20, transcendentals=0),
        )(order, *in_vmem([grads, *states]), *arrived[k], *in_vmem(news))
        news, blocks = results[:3], results[3:]
        groups[k] = []
        for q, block in enumerate(blocks):
            if k or q:
                block = lax.ppermute(block, "shard", plan.pattern(k, q))
            groups[k].append(block)

    entries = []
    if parts == 2:
        for k in plan.chunks:
            for q, block in enumerate(groups[k]):
                passed = lax.ppermute(block, "dp", cycles[1])
                entries += [((k, q, 0, None), block), ((k, q, 1, None), passed)]
        late_chunk = plan.chunks[-2 % len(plan.chunks)]
        is_late = [key[0] == late_chunk and key[1] >= plan.near // 2 and key[2] for key, _ in entries]
    else:
        keys = [(k, q) for k in plan.chunks for q in range(plan.near)]
        stacked = jnp.stack([block for k in plan.chunks for block in groups[k]])
        for s in range(parts):
            passed = lax.ppermute(stacked, "dp", cycles[s]) if s else stacked
            entries.append(([(k, q, s, n) for n, (k, q) in enumerate(keys)], passed))
        is_late = [n == len(entries) - 1 for n in range(len(entries))]
    early = [e for e, flag in zip(entries, is_late) if not flag]
    late = [e for e, flag in zip(entries, is_late) if flag]

    news = pl.pallas_call(
        store_kernel,
        out_shape=[pltpu.HBM((tiles, TB, TB), jnp.float32)] * 3,
        in_specs=[VMEM] * 3,
        out_specs=[HBM] * 3,
        scratch_shapes=[pltpu.SemaphoreType.DMA((3,))],
        compiler_params=pltpu.CompilerParams(vmem_limit_bytes=1 << 20),
        cost_estimate=pl.CostEstimate(flops=5000000, bytes_accessed=2 << 20, transcendentals=0),
        name="store",
    )(*in_vmem(news))

    tiles_shape = pltpu.HBM((owned, TB, TB), jnp.bfloat16)
    width = (owned + LANES - 1) // LANES * LANES

    def place(group, previous):
        count = 1 + len(group)
        sources = []
        for n, (key, _) in enumerate(group):
            sources += [(n, *each) for each in (key if isinstance(key, list) else [key])]
        return pl.pallas_call(
            functools.partial(place_kernel, plan, sources, len(group), not previous),
            out_shape=[tiles_shape, jax.ShapeDtypeStruct((1, width), jnp.float32)],
            in_specs=[SMEM] + [VMEM] * len(group) + ([VMEM, HBM] if previous else []),
            out_specs=[HBM, VMEM],
            input_output_aliases={count + 1: 0} if previous else {},
            scratch_shapes=[pltpu.SemaphoreType.DMA((len(sources) * room,))],
            compiler_params=pltpu.CompilerParams(vmem_limit_bytes=24 << 20),
            cost_estimate=pl.CostEstimate(flops=5000000, bytes_accessed=2 << 20, transcendentals=0),
        )(slots, *[a for _, a in group], *([previous[1], *in_hbm([previous[0]])] if previous else []))

    placed = place(early, None)
    tiles_out, scales = place(late, placed)
    scales_out = scales[0, :owned].astype(jnp.bfloat16)
    return (*[a.reshape(master.shape) for a in news], tiles_out, scales_out)


def solution(mesh):
    in_specs = (
        P("dp", "shard", None, None),
        P(),
        P("shard", "dp", None),
        P("shard", "dp", None),
        P("shard", "dp", None),
    )
    out_specs = (
        P("shard", "dp", None),
        P("shard", "dp", None),
        P("shard", "dp", None),
        P("shard", None, None),
        P("shard"),
    )

    return jax.shard_map(per_device, mesh=mesh, in_specs=in_specs, out_specs=out_specs, check_vma=False)
```

time: 233 us -> 119 us (0.51)
  the two profiles are of different devices: /device:TPU:0 before, /device:TPU:24 now
where the time goes in v2:
time: 119 us
  waiting for transfers between devices  59 us (50%)
  starting transfers between devices  32.3 us (27%)
  Pallas kernels  26.4 us (22%)
    ppermute x15, waiting for transfers between devices, per_device(): block = lax.ppermute(block, 'shard', plan.pattern(k, q))  21.7 us
    ppermute x4, waiting for transfers between devices, per_device(): arrived.setdefault(k, []).append(lax.ppermute(packed, 'dp', cycles[s]))  19.7 us
    ppermute x16, waiting for transfers between devices, per_device(): passed = lax.ppermute(block, 'dp', cycles[1])  17.5 us
    ppermute x15, starting transfers between devices, per_device(): block = lax.ppermute(block, 'shard', plan.pattern(k, q))  16.8 us
    ppermute x16, starting transfers between devices, per_device(): passed = lax.ppermute(block, 'dp', cycles[1])  11.1 us
    pallas_call x4, Pallas kernels, per_device(): pl.pallas_call(functools.partial(pack_kernel, plan, k, s, lead, len(loadi...  10.9 us
    pallas_call x4, Pallas kernels, per_device(): pl.pallas_call(functools.partial(adam_kernel, plan, k, not news), out_sha...  6.43 us
    pallas_call x2, Pallas kernels, place(): pl.pallas_call(functools.partial(place_kernel, plan, sources, len(group),...  4.45 us
  transfers between devices with their start and end apart: 35, of which 23 were waited for; matrix products, arithmetic and copies ran while one was open for 0% of the time, Pallas kernels for 17%

profile of v2, /device:TPU:24, one launch (start us, length us, event | category | flops | bytes accessed | tf_op | source)
XLA Modules:
  0.0 119.0 jit_solution(9264742819825153573)
XLA Ops:
  0.6 3.5 %shard_map.92 = (s32[96]{0:T(128)S(1)}, bf16[12,128,128]{2,1,0:T(8,128)(2,1)S(1)}, bf16[48,256,128]{2,1,0:T(8,128)(2,1)S(1)}) custom-call(s32[16,96]{1,0:T(8,128)} %table.1, bf16[48,256,128]{2,1,0:T(8,128)(2,1)} %bitcast.13), custom_call_target="tpu_custom_call" | custom-call | flops 6000000 | bytes 2097152 | tf_op jit(solution)/shard_map/pallas_call | solution.py:323
  5.8 2.4 %shard_map.93 = (bf16[12,128,128]{2,1,0:T(8,128)(2,1)S(1)}, f32[48,128,128]{2,1,0:T(8,128)S(1)}) custom-call(s32[96]{0:T(128)S(1)} %get-tuple-element.49.refs_0_, bf16[48,256,128]{2,1,0:T(8,128)(2,1)S(1)} %get-tuple-element.50.refs_1_, f32[48,128,128]{2,1,0:T(8,128)} %bitcast.14), custom_call_target="tpu_custom_call" | custom-call | flops 6000000 | bytes 2097152 | tf_op jit(solution)/shard_map/pallas_call | solution.py:323
  8.8 2.4 %shard_map.94 = (bf16[12,128,128]{2,1,0:T(8,128)(2,1)S(1)}, f32[48,128,128]{2,1,0:T(8,128)S(1)}) custom-call(s32[96]{0:T(128)S(1)} %get-tuple-element.49.refs_0_, bf16[48,256,128]{2,1,0:T(8,128)(2,1)S(1)} %get-tuple-element.50.refs_1_, f32[48,128,128]{2,1,0:T(8,128)} %bitcast.15), custom_call_target="tpu_custom_call" | custom-call | flops 6000000 | bytes 2097152 | tf_op jit(solution)/shard_map/pallas_call | solution.py:323
  12.8 2.4 %shard_map.95 = (bf16[12,128,128]{2,1,0:T(8,128)(2,1)S(1)}, f32[48,128,128]{2,1,0:T(8,128)S(1)}) custom-call(s32[96]{0:T(128)S(1)} %get-tuple-element.49.refs_0_, bf16[48,256,128]{2,1,0:T(8,128)(2,1)S(1)} %get-tuple-element.50.refs_1_, f32[48,128,128]{2,1,0:T(8,128)} %bitcast.16), custom_call_target="tpu_custom_call" | custom-call | flops 6000000 | bytes 2097152 | tf_op jit(solution)/shard_map/pallas_call | solution.py:323
  17.9 6.8 %collective-permute-done.2.refs_5_ = bf16[12,128,128]{2,1,0:T(8,128)(2,1)S(1)} collective-permute-done((bf16[12,128,128]{2,1,0:T(8,128)(2,1)S(1)}, bf16[12,128,128]{2,1,0:T(8,128)(2,1)S(1)}, u32[]{:S(2)}, u32[]{:S(2)}) %collective-permute-start.2) | collective-permute-done | bytes 393248 | tf_op jit(solution)/shard_map/ppermute | solution.py:338
  26.3 6.8 %collective-permute-done.1.refs_5_ = bf16[12,128,128]{2,1,0:T(8,128)(2,1)S(1)} collective-permute-done((bf16[12,128,128]{2,1,0:T(8,128)(2,1)S(1)}, bf16[12,128,128]{2,1,0:T(8,128)(2,1)S(1)}, u32[]{:S(2)}, u32[]{:S(2)}) %collective-permute-start.1) | collective-permute-done | bytes 393248 | tf_op jit(solution)/shard_map/ppermute | solution.py:338
  34.7 5.7 %collective-permute-done.refs_5_ = bf16[12,128,128]{2,1,0:T(8,128)(2,1)S(1)} collective-permute-done((bf16[12,128,128]{2,1,0:T(8,128)(2,1)S(1)}, bf16[12,128,128]{2,1,0:T(8,128)(2,1)S(1)}, u32[]{:S(2)}, u32[]{:S(2)}) %collective-permute-start) | collective-permute-done | bytes 393248 | tf_op jit(solution)/shard_map/ppermute | solution.py:338
  45.8 2.0 %collective-permute-start.26 = (bf16[392,128]{1,0:T(8,128)(2,1)S(1)}, bf16[392,128]{1,0:T(8,128)(2,1)S(1)}, u32[]{:S(2)}, u32[]{:S(2)}) collective-permute-start(bf16[392,128]{1,0:T(8,128)(2,1)S(1)} %get-tuple-element.84), channel_id=1, source_target_pairs={{0,9},{1,8},{2,11},{3,10},{4,13},{5,12},{6,15},{7,14},{8,1},{9,0},... | collective-permute-start | bytes 301064 | tf_op jit(solution)/shard_map/ppermute | solution.py:359
  49.4 2.3 %collective-permute-start.6 = (bf16[392,128]{1,0:T(8,128)(2,1)S(1)}, bf16[392,128]{1,0:T(8,128)(2,1)S(1)}, u32[]{:S(2)}, u32[]{:S(2)}) collective-permute-start(bf16[392,128]{1,0:T(8,128)(2,1)S(1)} %get-tuple-element.74), channel_id=1, source_target_pairs={{0,11},{1,10},{2,9},{3,8},{4,15},{5,14},{6,13},{7,12},{8,3},{9,2},... | collective-permute-start | bytes 301064 | tf_op jit(solution)/shard_map/ppermute | solution.py:359
  52.1 7.6 %collective-permute-done.24.refs_17_ = bf16[392,128]{1,0:T(8,128)(2,1)S(1)} collective-permute-done((bf16[392,128]{1,0:T(8,128)(2,1)S(1)}, bf16[392,128]{1,0:T(8,128)(2,1)S(1)}, u32[]{:S(2)}, u32[]{:S(2)}) %collective-permute-start.24) | collective-permute-done | bytes 100384 | tf_op jit(solution)/shard_map/ppermute | solution.py:359
  59.7 2.0 %collective-permute-done.26.refs_19_ = bf16[392,128]{1,0:T(8,128)(2,1)S(1)} collective-permute-done((bf16[392,128]{1,0:T(8,128)(2,1)S(1)}, bf16[392,128]{1,0:T(8,128)(2,1)S(1)}, u32[]{:S(2)}, u32[]{:S(2)}) %collective-permute-start.26) | collective-permute-done | bytes 100384 | tf_op jit(solution)/shard_map/ppermute | solution.py:359
  62.2 2.8 %collective-permute-done.4.refs_21_ = bf16[392,128]{1,0:T(8,128)(2,1)S(1)} collective-permute-done((bf16[392,128]{1,0:T(8,128)(2,1)S(1)}, bf16[392,128]{1,0:T(8,128)(2,1)S(1)}, u32[]{:S(2)}, u32[]{:S(2)}) %collective-permute-start.4) | collective-permute-done | bytes 100384 | tf_op jit(solution)/shard_map/ppermute | solution.py:359
  65.1 2.0 %collective-permute-done.6.refs_22_ = bf16[392,128]{1,0:T(8,128)(2,1)S(1)} collective-permute-done((bf16[392,128]{1,0:T(8,128)(2,1)S(1)}, bf16[392,128]{1,0:T(8,128)(2,1)S(1)}, u32[]{:S(2)}, u32[]{:S(2)}) %collective-permute-start.6) | collective-permute-done | bytes 100384 | tf_op jit(solution)/shard_map/ppermute | solution.py:359
  67.1 3.5 %collective-permute-start.12 = (bf16[392,128]{1,0:T(8,128)(2,1)S(1)}, bf16[392,128]{1,0:T(8,128)(2,1)S(1)}, u32[]{:S(2)}, u32[]{:S(2)}) collective-permute-start(bf16[392,128]{1,0:T(8,128)(2,1)S(1)} %get-tuple-element.77), channel_id=1, source_target_pairs={{0,14},{1,15},{2,12},{3,13},{4,10},{5,11},{6,8},{7,9},{8,6},{9,7},... | collective-permute-start | bytes 301064 | tf_op jit(solution)/shard_map/ppermute | solution.py:359
  71.3 3.7 %collective-permute-start.8 = (bf16[392,128]{1,0:T(8,128)(2,1)S(1)}, bf16[392,128]{1,0:T(8,128)(2,1)S(1)}, u32[]{:S(2)}, u32[]{:S(2)}) collective-permute-start(bf16[392,128]{1,0:T(8,128)(2,1)S(1)} %get-tuple-element.75), channel_id=1, source_target_pairs={{0,12},{1,13},{2,14},{3,15},{4,8},{5,9},{6,10},{7,11},{8,4},{9,5},... | collective-permute-start | bytes 301064 | tf_op jit(solution)/shard_map/ppermute | solution.py:359
  75.0 7.0 %collective-permute-done.22.refs_15_ = bf16[392,128]{1,0:T(8,128)(2,1)S(1)} collective-permute-done((bf16[392,128]{1,0:T(8,128)(2,1)S(1)}, bf16[392,128]{1,0:T(8,128)(2,1)S(1)}, u32[]{:S(2)}, u32[]{:S(2)}) %collective-permute-start.22) | collective-permute-done | bytes 100384 | tf_op jit(solution)/shard_map/ppermute | solution.py:359
  88.3 1.6 %collective-permute-done.32.refs_28_ = bf16[392,128]{1,0:T(8,128)(2,1)S(1)} collective-permute-done((bf16[392,128]{1,0:T(8,128)(2,1)S(1)}, bf16[392,128]{1,0:T(8,128)(2,1)S(1)}, u32[]{:S(2)}, u32[]{:S(2)}) %collective-permute-start.32) | collective-permute-done | bytes 100384 | tf_op jit(solution)/shard_map/ppermute | solution.py:366
  92.6 1.6 %collective-permute-done.25.refs_18_ = bf16[392,128]{1,0:T(8,128)(2,1)S(1)} collective-permute-done((bf16[392,128]{1,0:T(8,128)(2,1)S(1)}, bf16[392,128]{1,0:T(8,128)(2,1)S(1)}, u32[]{:S(2)}, u32[]{:S(2)}) %collective-permute-start.25) | collective-permute-done | bytes 100384 | tf_op jit(solution)/shard_map/ppermute | solution.py:366
  94.7 1.6 %collective-permute-done.27.refs_20_ = bf16[392,128]{1,0:T(8,128)(2,1)S(1)} collective-permute-done((bf16[392,128]{1,0:T(8,128)(2,1)S(1)}, bf16[392,128]{1,0:T(8,128)(2,1)S(1)}, u32[]{:S(2)}, u32[]{:S(2)}) %collective-permute-start.27) | collective-permute-done | bytes 100384 | tf_op jit(solution)/shard_map/ppermute | solution.py:366
  96.9 1.6 %collective-permute-done.17.refs_10_ = bf16[392,128]{1,0:T(8,128)(2,1)S(1)} collective-permute-done((bf16[392,128]{1,0:T(8,128)(2,1)S(1)}, bf16[392,128]{1,0:T(8,128)(2,1)S(1)}, u32[]{:S(2)}, u32[]{:S(2)}) %collective-permute-start.17) | collective-permute-done | bytes 100384 | tf_op jit(solution)/shard_map/ppermute | solution.py:366
  99.0 1.6 %collective-permute-done.19.refs_12_ = bf16[392,128]{1,0:T(8,128)(2,1)S(1)} collective-permute-done((bf16[392,128]{1,0:T(8,128)(2,1)S(1)}, bf16[392,128]{1,0:T(8,128)(2,1)S(1)}, u32[]{:S(2)}, u32[]{:S(2)}) %collective-permute-start.19) | collective-permute-done | bytes 100384 | tf_op jit(solution)/shard_map/ppermute | solution.py:366
  101.2 1.6 %collective-permute-done.21.refs_14_ = bf16[392,128]{1,0:T(8,128)(2,1)S(1)} collective-permute-done((bf16[392,128]{1,0:T(8,128)(2,1)S(1)}, bf16[392,128]{1,0:T(8,128)(2,1)S(1)}, u32[]{:S(2)}, u32[]{:S(2)}) %collective-permute-start.21) | collective-permute-done | bytes 100384 | tf_op jit(solution)/shard_map/ppermute | solution.py:366
  108.6 3.8 %store.1 = (f32[48,128,128]{2,1,0:T(8,128)}, f32[48,128,128]{2,1,0:T(8,128)}, f32[48,128,128]{2,1,0:T(8,128)}) custom-call(f32[48,128,128]{2,1,0:T(8,128)S(1)} %get-tuple-element.67.refs_0_, f32[48,128,128]{2,1,0:T(8,128)S(1)} %get-tuple-element.68.refs_1_, f32[48,128,128]{2,1,0:T(8,128)S(1)} %get-tuple-element.69.refs_2_), custom_call_target="tpu_custom_call" | custom-call | flops 5000000 | bytes 2097152 | tf_op jit(solution)/shard_map/store/pallas_call | solution.py:380
  113.6 3.0 %shard_map.100 = (bf16[96,128,128]{2,1,0:T(8,128)(2,1)}, f32[1,128]{1,0:T(1,128)S(1)}) custom-call(s32[16,128]{1,0:T(8,128)S(1)} %slots.1.refs_0_, bf16[392,128]{1,0:T(8,128)(2,1)S(1)} %collective-permute-done.8.refs_1_, bf16[392,128]{1,0:T(8,128)(2,1)S(1)} %collective-permute-done.9.refs_2_, bf16[392,128]{1,0:T(8,128)(2,1)S(1)} %collective-permute-done.10.refs_3_, ...), custom_call_target="tpu_custom_call" | custom-call | flops 5000000 | bytes 2097152 | tf_op jit(solution)/shard_map/pallas_call | solution.py:399
  (60 shorter events, 38.5 us)
Async XLA Ops:
  4.2 12.1 %collective-permute-start.3 = (bf16[12,128,128]{2,1,0:T(8,128)(2,1)S(1)}, bf16[12,128,128]{2,1,0:T(8,128)(2,1)S(1)}, u32[]{:S(2)}, u32[]{:S(2)}) collective-permute-start(bf16[12,128,128]{2,1,0:T(8,128)(2,1)S(1)} %get-tuple-element.57), channel_id=1, source_target_pairs={{0,16},{16,0},{1,17},{17,1},{2,18},{18,2},{3,19},{19,3},{4,20},{20... | collective-permute-start | bytes 1179656 | tf_op jit(solution)/shard_map/ppermute | solution.py:338
  8.2 16.4 %collective-permute-start.2 = (bf16[12,128,128]{2,1,0:T(8,128)(2,1)S(1)}, bf16[12,128,128]{2,1,0:T(8,128)(2,1)S(1)}, u32[]{:S(2)}, u32[]{:S(2)}) collective-permute-start(bf16[12,128,128]{2,1,0:T(8,128)(2,1)S(1)} %get-tuple-element.56), channel_id=1, source_target_pairs={{0,16},{16,0},{1,17},{17,1},{2,18},{18,2},{3,19},{19,3},{4,20},{20... | collective-permute-start | bytes 1179656 | tf_op jit(solution)/shard_map/ppermute | solution.py:338
  11.2 21.9 %collective-permute-start.1 = (bf16[12,128,128]{2,1,0:T(8,128)(2,1)S(1)}, bf16[12,128,128]{2,1,0:T(8,128)(2,1)S(1)}, u32[]{:S(2)}, u32[]{:S(2)}) collective-permute-start(bf16[12,128,128]{2,1,0:T(8,128)(2,1)S(1)} %get-tuple-element.55), channel_id=1, source_target_pairs={{0,16},{16,0},{1,17},{17,1},{2,18},{18,2},{3,19},{19,3},{4,20},{20... | collective-permute-start | bytes 1179656 | tf_op jit(solution)/shard_map/ppermute | solution.py:338
  15.3 25.1 %collective-permute-start = (bf16[12,128,128]{2,1,0:T(8,128)(2,1)S(1)}, bf16[12,128,128]{2,1,0:T(8,128)(2,1)S(1)}, u32[]{:S(2)}, u32[]{:S(2)}) collective-permute-start(bf16[12,128,128]{2,1,0:T(8,128)(2,1)S(1)} %get-tuple-element.54), channel_id=1, source_target_pairs={{0,16},{16,0},{1,17},{17,1},{2,18},{18,2},{3,19},{19,3},{4,20},{20... | collective-permute-start | bytes 1179656 | tf_op jit(solution)/shard_map/ppermute | solution.py:338
  45.4 14.3 %collective-permute-start.24 = (bf16[392,128]{1,0:T(8,128)(2,1)S(1)}, bf16[392,128]{1,0:T(8,128)(2,1)S(1)}, u32[]{:S(2)}, u32[]{:S(2)}) collective-permute-start(bf16[392,128]{1,0:T(8,128)(2,1)S(1)} %get-tuple-element.83), channel_id=1, source_target_pairs={{0,8},{1,9},{2,10},{3,11},{4,12},{5,13},{6,14},{7,15},{8,0},{9,1},... | collective-permute-start | bytes 301064 | tf_op jit(solution)/shard_map/ppermute | solution.py:359
  45.8 15.9 %collective-permute-start.26 = (bf16[392,128]{1,0:T(8,128)(2,1)S(1)}, bf16[392,128]{1,0:T(8,128)(2,1)S(1)}, u32[]{:S(2)}, u32[]{:S(2)}) collective-permute-start(bf16[392,128]{1,0:T(8,128)(2,1)S(1)} %get-tuple-element.84), channel_id=1, source_target_pairs={{0,9},{1,8},{2,11},{3,10},{4,13},{5,12},{6,15},{7,14},{8,1},{9,0},... | collective-permute-start | bytes 301064 | tf_op jit(solution)/shard_map/ppermute | solution.py:359
  47.9 17.2 %collective-permute-start.4 = (bf16[392,128]{1,0:T(8,128)(2,1)S(1)}, bf16[392,128]{1,0:T(8,128)(2,1)S(1)}, u32[]{:S(2)}, u32[]{:S(2)}) collective-permute-start(bf16[392,128]{1,0:T(8,128)(2,1)S(1)} %get-tuple-element.73), channel_id=1, source_target_pairs={{0,10},{1,11},{2,8},{3,9},{4,14},{5,15},{6,12},{7,13},{8,2},{9,3},... | collective-permute-start | bytes 301064 | tf_op jit(solution)/shard_map/ppermute | solution.py:359
  49.4 17.7 %collective-permute-start.6 = (bf16[392,128]{1,0:T(8,128)(2,1)S(1)}, bf16[392,128]{1,0:T(8,128)(2,1)S(1)}, u32[]{:S(2)}, u32[]{:S(2)}) collective-permute-start(bf16[392,128]{1,0:T(8,128)(2,1)S(1)} %get-tuple-element.74), channel_id=1, source_target_pairs={{0,11},{1,10},{2,9},{3,8},{4,15},{5,14},{6,13},{7,12},{8,3},{9,2},... | collective-permute-start | bytes 301064 | tf_op jit(solution)/shard_map/ppermute | solution.py:359
  51.6 15.4 %collective-permute-start.16 = (bf16[392,128]{1,0:T(8,128)(2,1)S(1)}, bf16[392,128]{1,0:T(8,128)(2,1)S(1)}, u32[]{:S(2)}, u32[]{:S(2)}) collective-permute-start(bf16[392,128]{1,0:T(8,128)(2,1)S(1)} %get-tuple-element.79), channel_id=1, source_target_pairs={{0,4},{1,5},{2,6},{3,7},{4,0},{5,1},{6,2},{7,3},{8,12},{9,13},{10,... | collective-permute-start | bytes 301064 | tf_op jit(solution)/shard_map/ppermute | solution.py:359
  59.7 10.8 %collective-permute-start.18 = (bf16[392,128]{1,0:T(8,128)(2,1)S(1)}, bf16[392,128]{1,0:T(8,128)(2,1)S(1)}, u32[]{:S(2)}, u32[]{:S(2)}) collective-permute-start(bf16[392,128]{1,0:T(8,128)(2,1)S(1)} %get-tuple-element.80), channel_id=1, source_target_pairs={{0,5},{1,4},{2,7},{3,6},{4,1},{5,0},{6,3},{7,2},{8,13},{9,12},{10,... | collective-permute-start | bytes 301064 | tf_op jit(solution)/shard_map/ppermute | solution.py:359
  65.1 17.0 %collective-permute-start.22 = (bf16[392,128]{1,0:T(8,128)(2,1)S(1)}, bf16[392,128]{1,0:T(8,128)(2,1)S(1)}, u32[]{:S(2)}, u32[]{:S(2)}) collective-permute-start(bf16[392,128]{1,0:T(8,128)(2,1)S(1)} %get-tuple-element.82), channel_id=1, source_target_pairs={{0,7},{1,6},{2,5},{3,4},{4,3},{5,2},{6,1},{7,0},{8,15},{9,14},{10,... | collective-permute-start | bytes 301064 | tf_op jit(solution)/shard_map/ppermute | solution.py:359
  67.0 15.5 %collective-permute-start.10 = (bf16[392,128]{1,0:T(8,128)(2,1)S(1)}, bf16[392,128]{1,0:T(8,128)(2,1)S(1)}, u32[]{:S(2)}, u32[]{:S(2)}) collective-permute-start(bf16[392,128]{1,0:T(8,128)(2,1)S(1)} %get-tuple-element.76), channel_id=1, source_target_pairs={{0,13},{1,12},{2,15},{3,14},{4,9},{5,8},{6,11},{7,10},{8,5},{9,4},... | collective-permute-start | bytes 301064 | tf_op jit(solution)/shard_map/ppermute | solution.py:359
  67.1 17.1 %collective-permute-start.12 = (bf16[392,128]{1,0:T(8,128)(2,1)S(1)}, bf16[392,128]{1,0:T(8,128)(2,1)S(1)}, u32[]{:S(2)}, u32[]{:S(2)}) collective-permute-start(bf16[392,128]{1,0:T(8,128)(2,1)S(1)} %get-tuple-element.77), channel_id=1, source_target_pairs={{0,14},{1,15},{2,12},{3,13},{4,10},{5,11},{6,8},{7,9},{8,6},{9,7},... | collective-permute-start | bytes 301064 | tf_op jit(solution)/shard_map/ppermute | solution.py:359
  70.5 14.1 %collective-permute-start.14 = (bf16[392,128]{1,0:T(8,128)(2,1)S(1)}, bf16[392,128]{1,0:T(8,128)(2,1)S(1)}, u32[]{:S(2)}, u32[]{:S(2)}) collective-permute-start(bf16[392,128]{1,0:T(8,128)(2,1)S(1)} %get-tuple-element.78), channel_id=1, source_target_pairs={{0,15},{1,14},{2,13},{3,12},{4,11},{5,10},{6,9},{7,8},{8,7},{9,6},... | collective-permute-start | bytes 301064 | tf_op jit(solution)/shard_map/ppermute | solution.py:359
  71.3 14.8 %collective-permute-start.8 = (bf16[392,128]{1,0:T(8,128)(2,1)S(1)}, bf16[392,128]{1,0:T(8,128)(2,1)S(1)}, u32[]{:S(2)}, u32[]{:S(2)}) collective-permute-start(bf16[392,128]{1,0:T(8,128)(2,1)S(1)} %get-tuple-element.75), channel_id=1, source_target_pairs={{0,12},{1,13},{2,14},{3,15},{4,8},{5,9},{6,10},{7,11},{8,4},{9,5},... | collective-permute-start | bytes 301064 | tf_op jit(solution)/shard_map/ppermute | solution.py:359
  87.8 10.8 %collective-permute-start.17 = (bf16[392,128]{1,0:T(8,128)(2,1)S(1)}, bf16[392,128]{1,0:T(8,128)(2,1)S(1)}, u32[]{:S(2)}, u32[]{:S(2)}) collective-permute-start(bf16[392,128]{1,0:T(8,128)(2,1)S(1)} %collective-permute-done.16.refs_9_), channel_id=1, source_target_pairs={{0,16},{16,0},{1,17},{17,1},{2,18},{18,2},{3,19},{19,3},{4,20},{20... | collective-permute-start | bytes 301064 | tf_op jit(solution)/shard_map/ppermute | solution.py:366
  89.9 10.8 %collective-permute-start.19 = (bf16[392,128]{1,0:T(8,128)(2,1)S(1)}, bf16[392,128]{1,0:T(8,128)(2,1)S(1)}, u32[]{:S(2)}, u32[]{:S(2)}) collective-permute-start(bf16[392,128]{1,0:T(8,128)(2,1)S(1)} %collective-permute-done.18.refs_11_), channel_id=1, source_target_pairs={{0,16},{16,0},{1,17},{17,1},{2,18},{18,2},{3,19},{19,3},{4,20},{20... | collective-permute-start | bytes 301064 | tf_op jit(solution)/shard_map/ppermute | solution.py:366
  92.1 10.8 %collective-permute-start.21 = (bf16[392,128]{1,0:T(8,128)(2,1)S(1)}, bf16[392,128]{1,0:T(8,128)(2,1)S(1)}, u32[]{:S(2)}, u32[]{:S(2)}) collective-permute-start(bf16[392,128]{1,0:T(8,128)(2,1)S(1)} %collective-permute-done.20.refs_13_), channel_id=1, source_target_pairs={{0,16},{16,0},{1,17},{17,1},{2,18},{18,2},{3,19},{19,3},{4,20},{20... | collective-permute-start | bytes 301064 | tf_op jit(solution)/shard_map/ppermute | solution.py:366
  94.2 10.8 %collective-permute-start.23 = (bf16[392,128]{1,0:T(8,128)(2,1)S(1)}, bf16[392,128]{1,0:T(8,128)(2,1)S(1)}, u32[]{:S(2)}, u32[]{:S(2)}) collective-permute-start(bf16[392,128]{1,0:T(8,128)(2,1)S(1)} %collective-permute-done.22.refs_15_), channel_id=1, source_target_pairs={{0,16},{16,0},{1,17},{17,1},{2,18},{18,2},{3,19},{19,3},{4,20},{20... | collective-permute-start | bytes 301064 | tf_op jit(solution)/shard_map/ppermute | solution.py:366
  96.4 10.8 %collective-permute-start.11 = (bf16[392,128]{1,0:T(8,128)(2,1)S(1)}, bf16[392,128]{1,0:T(8,128)(2,1)S(1)}, u32[]{:S(2)}, u32[]{:S(2)}) collective-permute-start(bf16[392,128]{1,0:T(8,128)(2,1)S(1)} %collective-permute-done.10.refs_3_), channel_id=1, source_target_pairs={{0,16},{16,0},{1,17},{17,1},{2,18},{18,2},{3,19},{19,3},{4,20},{20... | collective-permute-start | bytes 301064 | tf_op jit(solution)/shard_map/ppermute | solution.py:366
  98.5 13.8 %collective-permute-start.13 = (bf16[392,128]{1,0:T(8,128)(2,1)S(1)}, bf16[392,128]{1,0:T(8,128)(2,1)S(1)}, u32[]{:S(2)}, u32[]{:S(2)}) collective-permute-start(bf16[392,128]{1,0:T(8,128)(2,1)S(1)} %collective-permute-done.12.refs_5_), channel_id=1, source_target_pairs={{0,16},{16,0},{1,17},{17,1},{2,18},{18,2},{3,19},{19,3},{4,20},{20... | collective-permute-start | bytes 301064 | tf_op jit(solution)/shard_map/ppermute | solution.py:366
  100.7 11.7 %collective-permute-start.15 = (bf16[392,128]{1,0:T(8,128)(2,1)S(1)}, bf16[392,128]{1,0:T(8,128)(2,1)S(1)}, u32[]{:S(2)}, u32[]{:S(2)}) collective-permute-start(bf16[392,128]{1,0:T(8,128)(2,1)S(1)} %collective-permute-done.14.refs_7_), channel_id=1, source_target_pairs={{0,16},{16,0},{1,17},{17,1},{2,18},{18,2},{3,19},{19,3},{4,20},{20... | collective-permute-start | bytes 301064 | tf_op jit(solution)/shard_map/ppermute | solution.py:366
  102.8 10.8 %collective-permute-start.9 = (bf16[392,128]{1,0:T(8,128)(2,1)S(1)}, bf16[392,128]{1,0:T(8,128)(2,1)S(1)}, u32[]{:S(2)}, u32[]{:S(2)}) collective-permute-start(bf16[392,128]{1,0:T(8,128)(2,1)S(1)} %collective-permute-done.8.refs_1_), channel_id=1, source_target_pairs={{0,16},{16,0},{1,17},{17,1},{2,18},{18,2},{3,19},{19,3},{4,20},{20... | collective-permute-start | bytes 301064 | tf_op jit(solution)/shard_map/ppermute | solution.py:366
  105.0 11.7 %collective-permute-start.5 = (bf16[392,128]{1,0:T(8,128)(2,1)S(1)}, bf16[392,128]{1,0:T(8,128)(2,1)S(1)}, u32[]{:S(2)}, u32[]{:S(2)}) collective-permute-start(bf16[392,128]{1,0:T(8,128)(2,1)S(1)} %collective-permute-done.4.refs_21_), channel_id=1, source_target_pairs={{0,16},{16,0},{1,17},{17,1},{2,18},{18,2},{3,19},{19,3},{4,20},{20... | collective-permute-start | bytes 301064 | tf_op jit(solution)/shard_map/ppermute | solution.py:366
  (11 other events, 83.5 us)

commit v3 on v2

v3 whole, which is shorter than its diff:
```python
import functools

import jax
import jax.numpy as jnp
from jax import lax
from jax.experimental import pallas as pl
from jax.experimental.pallas import tpu as pltpu
from jax.sharding import PartitionSpec as P


TB = 128
LANES = 128
UNROLL = 2
SPLIT = 4
STAGES = {(0, 2, 1): 2, (0, 3, 1): 2, (0, 2, 0): 1, (0, 3, 0): 1, (0, 1, 1): 1}
STAGES |= {(k, q, s): 1 for k in (1, 2) for q in range(4) for s in range(2)}
PACK_MIB = 4
ADAM_MIB = 4


beta_first = 0.9
beta_second = 0.95
learning_rate = 0.002
weight_decay = 0.1
adam_epsilon = 1e-08
scale_epsilon = 1e-06
step_count = 10

HBM = pl.BlockSpec(memory_space=pltpu.HBM)
VMEM = pl.BlockSpec(memory_space=pltpu.VMEM)
SMEM = pl.BlockSpec(memory_space=pltpu.SMEM)


def in_hbm(arrays):
    return [pltpu.with_memory_space_constraint(a, pltpu.HBM) for a in arrays]


def in_vmem(arrays):
    return [pltpu.with_memory_space_constraint(a, pltpu.VMEM) for a in arrays]


def extract(raw, wide, part, parts):
    wide[...] = raw[...].astype(jnp.float32)
    return wide[pl.ds(part, TB, stride=parts), :]


def other(index, step, size):
    if size & (size - 1) == 0:
        return index ^ step
    return (index + step) % size


def back(index, step, size):
    if size & (size - 1) == 0:
        return index ^ step
    return (index + size - step) % size


class Plan:
    def __init__(self, parts, owners, owned, tiles):
        self.parts, self.owners, self.owned, self.tiles = parts, owners, owned, tiles
        self.sub_len = owned // parts
        self.room = (self.sub_len + owners - 1) // owners
        self.far = 4 if owners % 4 == 0 and owners > 4 else 1
        self.near = owners // self.far
        self.chunks = [self.far - 1] + list(range(1, self.far - 1)) + [0] if self.far > 1 else [0]
        self.per_chunk = self.near * self.room
        self.pad = (self.room + 7) // 8 * 8
        self.height = self.room * TB + self.pad

    def pattern(self, k, q):
        pairs = []
        for i in range(self.owners):
            far, near = divmod(i, self.near)
            pairs.append((i, other(far, k, self.far) * self.near + other(near, q, self.near)))
        return pairs

    def source(self, me, k, q):
        return back(me // self.near, k, self.far) * self.near + back(me % self.near, q, self.near)


def step_between(here, there, size):
    if size & (size - 1) == 0:
        return here ^ there
    return lax.rem(there + size - here, size)


def fill_order(part, plan, table, order, base, count):
    me = lax.axis_index("shard")
    entries = plan.owners * plan.room

    def clear(j, carry):
        order[base + j] = 0
        return carry

    def zero(j, carry):
        count[j] = 0
        return carry

    def enter(t, carry):
        owner = table[me, part * plan.sub_len + t] // plan.owned
        rank = count[owner]
        count[owner] = rank + 1
        k = step_between(me // plan.near, owner // plan.near, plan.far)
        q = step_between(me % plan.near, owner % plan.near, plan.near)
        order[base + (k * plan.near + q) * plan.room + rank] = t
        return carry

    if entries != plan.sub_len:
        lax.fori_loop(0, entries, clear, 0)
    lax.fori_loop(0, plan.owners, zero, 0, unroll=True)
    lax.fori_loop(0, plan.sub_len, enter, 0, unroll=4)


def find_slots(plan, table, out):
    me = lax.axis_index("shard")
    owned, sub_len = plan.owned, plan.sub_len
    local = table[...] - me * owned
    mine = (local >= 0) & (local < owned)
    before = lax.broadcasted_iota(jnp.int32, (owned, owned), 0)
    after = lax.broadcasted_iota(jnp.int32, (owned, owned), 1)
    same = before // sub_len == after // sub_len
    counts = jnp.where((before < after) & same, 1.0, 0.0).astype(jnp.bfloat16)
    flags = jnp.where(mine, 1.0, 0.0).astype(jnp.bfloat16)
    rank = jnp.dot(flags, counts, preferred_element_type=jnp.float32)
    column = lax.broadcasted_iota(jnp.int32, local.shape, 1) // sub_len
    lane = lax.broadcasted_iota(jnp.int32, out.shape, 1)
    value = jnp.where(mine, local + 1, 0).astype(jnp.float32)
    total = jnp.zeros(out.shape, jnp.float32)
    for part in range(plan.parts):
        for r in range(plan.room):
            chosen = jnp.where((column == part) & (rank == float(r)), value, 0.0)
            found = jnp.sum(chosen, axis=1, keepdims=True)
            total = jnp.where(lane == part * plan.room + r, found, total)
    out[...] = total.astype(jnp.int32) - 1


def pack_kernel(plan, chunk, shift, lead, own, loads, *refs):
    parts, entries, room = plan.parts, plan.per_chunk, plan.room
    here = lax.axis_index("dp")
    part = lax.rem(here + shift, parts)
    refs = list(refs)
    take = lambda n: [refs.pop(0) for _ in range(n)]
    (table,) = take(1) if lead or own else (None,)
    (order,) = take(1) if not lead else (None,)
    (grads,) = take(1) if not lead else (None,)
    sources = take(loads)
    (order,) = take(1) if lead else (order,)
    (out,) = take(1)
    (order_own, slots) = take(2) if own else (None, None)
    targets = take(loads)
    if lead:
        grads = targets[0]
    (wide,) = take(1)
    rows, count = take(2) if lead or own else (None, None)
    (flat,) = take(1) if own else (None,)
    (sems,) = take(1)
    pairs = list(zip(sources, targets))
    pairs += [(table, rows)] * bool(lead or own) + [(table, flat)] * bool(own)
    copies = [pltpu.make_async_copy(a, b, sems.at[n]) for n, (a, b) in enumerate(pairs)]
    for copy in copies:
        copy.start()
    entries_of_part = plan.owners * room
    if lead:
        copies[loads].wait()
        fill_order(part, plan, rows, order, part * entries_of_part, count)
        copies[0].wait()
    base = part * entries_of_part + chunk * entries

    def body(i, carry):
        out[i] = extract(grads.at[order[base + i]], wide, part, parts).astype(out.dtype)
        return carry

    lax.fori_loop(0, entries, body, 0)
    if lead:
        for s in range(1, parts - 1):
            later = lax.rem(part + s, parts)
            fill_order(later, plan, rows, order, later * entries_of_part, count)
    if own:
        if not lead:
            copies[loads].wait()
        copies[loads + 1].wait()
        fill_order(here, plan, rows, order_own, 0, count)
        find_slots(plan, flat, slots)
    for n, copy in enumerate(copies):
        if not (lead and n == 0) and not (lead and n == loads) and not (own and n >= loads):
            copy.wait()


def adam_kernel(plan, chunk, first, *refs):
    parts, entries, room = plan.parts, plan.per_chunk, plan.room
    order, grads, master, moment, second = refs[:5]
    arrived = refs[5 : 4 + parts]
    refs = refs[4 + parts + (0 if first else 3) :]
    master_out, moment_out, second_out = refs[:3]
    blocks = refs[3 : 3 + plan.near]
    wide, peak = refs[3 + plan.near :]
    part = lax.axis_index("dp")
    base = chunk * entries
    first_fix = 1.0 / (1.0 - beta_first**step_count)
    second_fix = 1.0 / (1.0 - beta_second**step_count)
    rows = 32

    def update(i, carry):
        tile = order[base + i]
        wide[...] = grads[tile].astype(jnp.float32)
        top = None
        for b in range(0, TB, rows):
            at = pl.ds(b, rows)
            grad = wide[pl.ds(b * parts + part, rows, stride=parts), :]
            for ref in arrived:
                grad = grad + ref[i, at, :].astype(jnp.float32)
            moment_new = beta_first * moment[tile, at, :] + (1.0 - beta_first) * grad
            second_new = beta_second * second[tile, at, :] + (1.0 - beta_second) * grad * grad
            old = master[tile, at, :]
            step = moment_new * first_fix / (jnp.sqrt(second_new * second_fix) + adam_epsilon)
            master_new = old - learning_rate * (step + weight_decay * old)
            master_out[tile, at, :] = master_new
            moment_out[tile, at, :] = moment_new
            second_out[tile, at, :] = second_new
            size = jnp.abs(master_new)
            for s in range(0, rows, 8):
                top = size[s : s + 8] if top is None else jnp.maximum(top, size[s : s + 8])
        peak[i] = top
        return carry

    lax.fori_loop(0, entries, update, 0, unroll=UNROLL)
    largest = jnp.max(jnp.max(peak[...], axis=2, keepdims=True), axis=1, keepdims=True)
    rounded = (largest + scale_epsilon).astype(jnp.bfloat16).astype(jnp.float32)
    peak[...] = jnp.broadcast_to(rounded, peak.shape)
    row = lax.broadcasted_iota(jnp.int32, (plan.pad, LANES), 0)
    for q, block in enumerate(blocks):
        tail = jnp.zeros((plan.pad, LANES), jnp.float32)
        for r in range(room):
            i = q * room + r
            tile = order[base + i]
            scale = peak[i]
            inverse = 1.0 / scale
            tail = jnp.where(row == r, jnp.concatenate([scale] * (plan.pad // 8), axis=0), tail)
            for b in range(0, TB, 16):
                pair = [master_out[tile, pl.ds(b + s, 8), :] * inverse for s in (0, 8)]
                block[pl.ds(r * TB + b, 16), :] = jnp.concatenate(pair, axis=0).astype(block.dtype)
        block[pl.ds(room * TB, plan.pad), :] = tail.astype(block.dtype)


def tails_kernel(plan, *refs):
    out = refs[-1]
    for n, ref in enumerate(refs[:-1]):
        out[n] = ref[pl.ds(plan.room * TB, plan.pad), :]


def place_kernel(plan, sources, count, tails, first, gathers, *refs):
    room = plan.room
    refs = list(refs)
    take = lambda n: [refs.pop(0) for _ in range(n)]
    (slots,), blocks = take(1), take(count)
    late = take(1) if tails else []
    held = take(3) if first else []
    before = take(2)[1:] if gathers and not first else []
    if not first and not gathers:
        take(1)
    (tiles_out,) = take(1)
    (scales_out,) = take(1) if gathers else (None,)
    saved = take(3) if first else []
    (sems,) = take(1)
    stores = []
    for a, b in zip(held, saved):
        for n in range(0, plan.tiles, plan.tiles // SPLIT):
            piece = pl.ds(n, plan.tiles // SPLIT)
            stores.append(pltpu.make_async_copy(a.at[piece], b.at[piece], refs[0].at[len(stores)]))
    for copy in stores:
        copy.start()
    here, me = lax.axis_index("dp"), lax.axis_index("shard")

    def slot_of(k, q, shift, r):
        part = lax.rem(here + plan.parts - shift, plan.parts)
        return slots[plan.source(me, k, q), part * room + r]

    entries, views = [], []
    for n, (ref, k, q, shift, at) in enumerate(sources):
        views.append(blocks[ref] if at is None else blocks[ref].at[at])
        for r in range(room):
            slot = slot_of(k, q, shift, r)
            copy = pltpu.make_async_copy(views[n].at[pl.ds(r * TB, TB)], tiles_out.at[slot], sems.at[n * room + r])
            entries.append((slot, copy))
            if room * plan.owners == plan.sub_len:
                copy.start()
            else:
                pl.when(slot >= 0)(copy.start)
    if gathers:
        lane = lax.broadcasted_iota(jnp.int32, scales_out.shape, 1)
        total = before[0][...] if before else jnp.zeros(scales_out.shape, jnp.float32)
        ends = [(view[pl.ds(room * TB, plan.pad), :], key[1:4]) for view, key in zip(views, sources)]
        ends += [(late[0][n], key) for n, key in enumerate(tails)]
        for rows, (k, q, shift) in ends:
            for r in range(room):
                wide = jnp.concatenate([rows[r : r + 1].astype(jnp.float32)] * (scales_out.shape[1] // LANES), axis=1)
                total = jnp.where(lane == slot_of(k, q, shift, r), wide, total)
        scales_out[...] = total
    for slot, copy in entries:
        if room * plan.owners == plan.sub_len:
            copy.wait()
        else:
            pl.when(slot >= 0)(copy.wait)
    for copy in stores:
        copy.wait()


def per_device(gradients, tile_table, master, moment, second):
    owners = lax.axis_size("shard")
    parts = lax.axis_size("dp")
    owned = tile_table.shape[1]
    tiles = master.size // (TB * TB)
    plan = Plan(parts, owners, owned, tiles)
    room, entries = plan.room, plan.per_chunk

    grads = gradients.reshape(parts, tiles, TB, TB).transpose(1, 2, 0, 3).reshape(tiles, TB * parts, TB)
    states = [a.reshape(tiles, TB, TB) for a in (master, moment, second)]
    cycles = {s: [(d, (d + s) % parts) for d in range(parts)] for s in range(1, parts)}
    f32_tiles = pltpu.VMEM((tiles, TB, TB), jnp.float32)
    block_shape = pltpu.VMEM((plan.height, TB), jnp.bfloat16)

    order = None
    waiting = list(states)
    states = []
    arrived = {}
    calls = [(k, s) for k in plan.chunks for s in range(1, parts)]
    packed_shape = pltpu.VMEM((entries, TB, TB), jnp.bfloat16)
    slots_shape = jax.ShapeDtypeStruct((owners, (parts * room + LANES - 1) // LANES * LANES), jnp.int32)
    for n, (k, s) in enumerate(calls):
        lead, own = n == 0, n == min(1, len(calls) - 1)
        loading = waiting[: len(waiting) if n == len(calls) - 1 else 1 - lead]
        waiting = waiting[len(loading) :]
        loads = len(loading) + lead
        tabled = lead or own
        operands = in_hbm([tile_table]) * tabled
        operands += in_hbm([grads]) if lead else [order, *in_vmem([grads])]
        operands += in_hbm(loading)
        out_shape = [jax.ShapeDtypeStruct((parts * room * owners,), jnp.int32)] * lead + [packed_shape]
        out_shape += [jax.ShapeDtypeStruct((room * owners,), jnp.int32), slots_shape] * own
        out_shape += [pltpu.VMEM(grads.shape, grads.dtype)] * lead + [f32_tiles] * len(loading)
        result = pl.pallas_call(
            functools.partial(pack_kernel, plan, k, s, lead, own, loads),
            out_shape=out_shape,
            in_specs=[HBM] * tabled + [SMEM, VMEM] * (not lead) + [HBM] * loads,
            out_specs=[SMEM] * lead + [VMEM] + [SMEM, VMEM] * own + [VMEM] * loads,
            scratch_shapes=[pltpu.VMEM((TB * parts, TB), jnp.float32)]
            + [pltpu.SMEM(tile_table.shape, jnp.int32), pltpu.SMEM((owners,), jnp.int32)] * tabled
            + [pltpu.VMEM(tile_table.shape, jnp.int32)] * own
            + [pltpu.SemaphoreType.DMA((max(1, loads + tabled + own),))],
            compiler_params=pltpu.CompilerParams(vmem_limit_bytes=PACK_MIB << 20),
            cost_estimate=pl.CostEstimate(flops=6000000, bytes_accessed=2 << 20, transcendentals=0),
        )(*operands)
        result = list(result)
        if lead:
            order = result.pop(0)
        packed = result.pop(0)
        if own:
            order_own, slots = result.pop(0), result.pop(0)
        if lead:
            grads = result.pop(0)
        states += result
        arrived.setdefault(k, []).append(lax.ppermute(packed, "dp", cycles[s]))

    news = []
    groups = {}
    for k in plan.chunks:
        count = 5 + parts - 1
        results = pl.pallas_call(
            functools.partial(adam_kernel, plan, k, not news),
            out_shape=[f32_tiles] * 3 + [block_shape] * plan.near,
            in_specs=[SMEM] + [VMEM] * (3 + parts) + [VMEM] * len(news),
            out_specs=[VMEM] * (3 + plan.near),
            input_output_aliases={count + j: j for j in range(len(news))},
            scratch_shapes=[pltpu.VMEM((TB * parts, TB), jnp.float32), pltpu.VMEM((entries, 8, LANES), jnp.float32)],
            compiler_params=pltpu.CompilerParams(vmem_limit_bytes=ADAM_MIB << 20),
            cost_estimate=pl.CostEstimate(flops=25000000, bytes_accessed=6 << 20, transcendentals=0),
        )(order_own, *in_vmem([grads, *states]), *arrived[k], *in_vmem(news))
        news, blocks = results[:3], results[3:]
        groups[k] = []
        for q, block in enumerate(blocks):
            if k or q:
                block = lax.ppermute(block, "shard", plan.pattern(k, q))
            groups[k].append(block)

    entries = []
    tails, tail_keys = [], []
    if parts == 2:
        for k in plan.chunks:
            for q, block in enumerate(groups[k]):
                passed = lax.ppermute(block, "dp", cycles[1])
                entries += [((k, q, 0, None), block), ((k, q, 1, None), passed)]
        stage = [STAGES.get(key[:3], 0) for key, _ in entries]
        stage = stage if 2 in stage else [2 * (n == len(entries) - 1) for n in range(len(entries))]
        tail_keys = [key[:3] for (key, _), at in zip(entries, stage) if at == 2]
        ends = pl.pallas_call(
            functools.partial(tails_kernel, plan),
            out_shape=pltpu.VMEM((len(tail_keys), plan.pad, LANES), jnp.bfloat16),
            in_specs=[VMEM] * len(tail_keys),
            out_specs=VMEM,
            compiler_params=pltpu.CompilerParams(vmem_limit_bytes=1 << 20),
            cost_estimate=pl.CostEstimate(flops=1000000, bytes_accessed=1 << 20, transcendentals=0),
            name="tails",
        )(*[groups[k][q] for k, q, _ in tail_keys])
        tails = [lax.ppermute(ends, "dp", cycles[1])]
    else:
        keys = [(k, q) for k in plan.chunks for q in range(plan.near)]
        stacked = jnp.stack([block for k in plan.chunks for block in groups[k]])
        for s in range(parts):
            passed = lax.ppermute(stacked, "dp", cycles[s]) if s else stacked
            entries.append(([(k, q, s, n) for n, (k, q) in enumerate(keys)], passed))
        stage = [0] * len(entries)
    tiles_shape = pltpu.HBM((owned, TB, TB), jnp.bfloat16)
    width = (owned + LANES - 1) // LANES * LANES

    def place(at, previous, ends):
        group = [e for e, level in zip(entries, stage) if level == at]
        first, gathers = not previous, at < 2
        sources = []
        for n, (key, _) in enumerate(group):
            sources += [(n, *each) for each in (key if isinstance(key, list) else [key])]
        operands = [slots, *[a for _, a in group], *ends]
        operands += in_vmem(news) if first else in_hbm(previous[:1])
        operands += previous[1:] if gathers else []
        return pl.pallas_call(
            functools.partial(place_kernel, plan, sources, len(group), tail_keys if ends else [], first, gathers),
            out_shape=[tiles_shape]
            + [jax.ShapeDtypeStruct((1, width), jnp.float32)] * gathers
            + [pltpu.HBM((tiles, TB, TB), jnp.float32)] * (3 * first),
            in_specs=[SMEM]
            + [VMEM] * (len(group) + len(ends))
            + ([VMEM] * 3 if first else [HBM] + [VMEM] * gathers),
            out_specs=[HBM] + [VMEM] * gathers + [HBM] * (3 * first),
            input_output_aliases={} if first else {1 + len(group) + len(ends): 0},
            scratch_shapes=[pltpu.SemaphoreType.DMA((len(sources) * room,))]
            + [pltpu.SemaphoreType.DMA((3 * SPLIT,))] * first,
            compiler_params=pltpu.CompilerParams(vmem_limit_bytes=24 << 20),
            cost_estimate=pl.CostEstimate(flops=5000000, bytes_accessed=2 << 20, transcendentals=0),
        )(*operands)

    staged = max(stage) > 0
    tiles_out, scales, *news = place(0, [], [] if 1 in stage else tails)
    if 1 in stage:
        tiles_out, scales = place(1, [tiles_out, scales], tails)
    scales_out = scales[0, :owned].astype(jnp.bfloat16)
    if staged:
        (tiles_out,) = place(2, [tiles_out], [])
    return (*[a.reshape(master.shape) for a in news], tiles_out, scales_out)


def solution(mesh):
    in_specs = (
        P("dp", "shard", None, None),
        P(),
        P("shard", "dp", None),
        P("shard", "dp", None),
        P("shard", "dp", None),
    )
    out_specs = (
        P("shard", "dp", None),
        P("shard", "dp", None),
        P("shard", "dp", None),
        P("shard", None, None),
        P("shard"),
    )

    return jax.shard_map(per_device, mesh=mesh, in_specs=in_specs, out_specs=out_specs, check_vma=False)
```

time: 119 us -> 122 us (1.025)
  the two profiles are of different devices: /device:TPU:24 before, /device:TPU:0 now
where the time goes in v3:
time: 122 us
  starting transfers between devices  52 us (43%)
  waiting for transfers between devices  42.6 us (35%)
  Pallas kernels  26 us (21%)
    ppermute x15, starting transfers between devices, per_device(): block = lax.ppermute(block, 'shard', plan.pattern(k, q))  33 us
    ppermute x4, waiting for transfers between devices, per_device(): arrived.setdefault(k, []).append(lax.ppermute(packed, 'dp', cycles[s]))  19.3 us
    ppermute x15, waiting for transfers between devices, per_device(): block = lax.ppermute(block, 'shard', plan.pattern(k, q))  12.9 us
    ppermute x16, starting transfers between devices, per_device(): passed = lax.ppermute(block, 'dp', cycles[1])  12.6 us
    pallas_call x4, Pallas kernels, per_device(): pl.pallas_call(functools.partial(pack_kernel, plan, k, s, lead, own, load...  10.8 us
    ppermute x16, waiting for transfers between devices, per_device(): passed = lax.ppermute(block, 'dp', cycles[1])  9.37 us
    pallas_call x3, Pallas kernels, place(): pl.pallas_call(functools.partial(place_kernel, plan, sources, len(group),...  8.83 us
    pallas_call x4, Pallas kernels, per_device(): pl.pallas_call(functools.partial(adam_kernel, plan, k, not news), out_sha...  6.41 us
  transfers between devices with their start and end apart: 36, of which 19 were waited for; matrix products, arithmetic and copies ran while one was open for 0% of the time, Pallas kernels for 17%

profile of v3, /device:TPU:0, one launch (start us, length us, event | category | flops | bytes accessed | tf_op | source)
XLA Modules:
  0.0 121.9 jit_solution(5511326134408994751)
XLA Ops:
  0.6 2.7 %shard_map.92 = (s32[96]{0:T(128)S(1)}, bf16[12,128,128]{2,1,0:T(8,128)(2,1)S(1)}, bf16[48,256,128]{2,1,0:T(8,128)(2,1)S(1)}) custom-call(s32[16,96]{1,0:T(8,128)} %refs_0_.3, bf16[48,256,128]{2,1,0:T(8,128)(2,1)} %bitcast.13), custom_call_target="tpu_custom_call" | custom-call | flops 6000000 | bytes 2097152 | tf_op jit(solution)/shard_map/pallas_call | solution.py:342
  3.4 3.1 %collective-permute-start = (bf16[12,128,128]{2,1,0:T(8,128)(2,1)S(1)}, bf16[12,128,128]{2,1,0:T(8,128)(2,1)S(1)}, u32[]{:S(2)}, u32[]{:S(2)}) collective-permute-start(bf16[12,128,128]{2,1,0:T(8,128)(2,1)S(1)} %get-tuple-element.58), channel_id=1, source_target_pairs={{0,16},{16,0},{1,17},{17,1},{2,18},{18,2},{3,19},{19,3},{4,20},{20... | collective-permute-start | bytes 1179656 | tf_op jit(solution)/shard_map/ppermute | solution.py:363
  6.4 3.2 %shard_map.93 = (bf16[12,128,128]{2,1,0:T(8,128)(2,1)S(1)}, s32[48]{0:T(128)S(1)}, s32[16,128]{1,0:T(8,128)S(1)}, f32[48,128,128]{2,1,0:T(8,128)S(1)}) custom-call(s32[16,96]{1,0:T(8,128)} %refs_0_.3, s32[96]{0:T(128)S(1)} %get-tuple-element.51.refs_1_.refs_0_, bf16[48,256,128]{2,1,0:T(8,128)(2,1)S(1)} %get-tuple-element.52.refs_2_.refs_1_, ...), custom_call_target="tpu_custom_call" | custom-call | flops 6000000 | bytes 2097152 | tf_op jit(solution)/shard_map/pallas_call | solution.py:342
  9.7 2.4 %shard_map.94 = (bf16[12,128,128]{2,1,0:T(8,128)(2,1)S(1)}, f32[48,128,128]{2,1,0:T(8,128)S(1)}) custom-call(s32[96]{0:T(128)S(1)} %get-tuple-element.51.refs_1_.refs_0_, bf16[48,256,128]{2,1,0:T(8,128)(2,1)S(1)} %get-tuple-element.52.refs_2_.refs_1_, f32[48,128,128]{2,1,0:T(8,128)} %bitcast.15), custom_call_target="tpu_custom_call" | custom-call | flops 6000000 | bytes 2097152 | tf_op jit(solution)/shard_map/pallas_call | solution.py:342
  12.1 2.1 %collective-permute-start.10 = (bf16[12,128,128]{2,1,0:T(8,128)(2,1)S(1)}, bf16[12,128,128]{2,1,0:T(8,128)(2,1)S(1)}, u32[]{:S(2)}, u32[]{:S(2)}) collective-permute-start(bf16[12,128,128]{2,1,0:T(8,128)(2,1)S(1)} %get-tuple-element.64), channel_id=1, source_target_pairs={{0,16},{16,0},{1,17},{17,1},{2,18},{18,2},{3,19},{19,3},{4,20},{20... | collective-permute-start | bytes 1179656 | tf_op jit(solution)/shard_map/ppermute | solution.py:363
  14.2 2.4 %shard_map.95 = (bf16[12,128,128]{2,1,0:T(8,128)(2,1)S(1)}, f32[48,128,128]{2,1,0:T(8,128)S(1)}) custom-call(s32[96]{0:T(128)S(1)} %get-tuple-element.51.refs_1_.refs_0_, bf16[48,256,128]{2,1,0:T(8,128)(2,1)S(1)} %get-tuple-element.52.refs_2_.refs_1_, f32[48,128,128]{2,1,0:T(8,128)} %bitcast.16), custom_call_target="tpu_custom_call" | custom-call | flops 6000000 | bytes 2097152 | tf_op jit(solution)/shard_map/pallas_call | solution.py:342
  16.7 1.6 %shard_map.96 = (f32[48,128,128]{2,1,0:T(8,128)S(1)}, f32[48,128,128]{2,1,0:T(8,128)S(1)}, f32[48,128,128]{2,1,0:T(8,128)S(1)}, bf16[392,128]{1,0:T(8,128)(2,1)S...) custom-call(s32[48]{0:T(128)S(1)} %get-tuple-element.54.refs_0_, ...), custom_call_target="tpu_custom_call" | custom-call | flops 25000000 | bytes 6291456 | tf_op jit(solution)/shard_map/pallas_call | solution.py:369
  18.3 6.5 %collective-permute-done.11.refs_5_ = bf16[12,128,128]{2,1,0:T(8,128)(2,1)S(1)} collective-permute-done((bf16[12,128,128]{2,1,0:T(8,128)(2,1)S(1)}, bf16[12,128,128]{2,1,0:T(8,128)(2,1)S(1)}, u32[]{:S(2)}, u32[]{:S(2)}) %collective-permute-start.11) | collective-permute-done | bytes 393248 | tf_op jit(solution)/shard_map/ppermute | solution.py:363
  24.8 1.6 %shard_map.97 = (f32[48,128,128]{2,1,0:T(8,128)S(1)}, f32[48,128,128]{2,1,0:T(8,128)S(1)}, f32[48,128,128]{2,1,0:T(8,128)S(1)}, bf16[392,128]{1,0:T(8,128)(2,1)S...) custom-call(s32[48]{0:T(128)S(1)} %get-tuple-element.54.refs_0_, ...), custom_call_target="tpu_custom_call", output_to_operand_aliasing={{0}: (6, {}), {1}: (7, {}), {2}: (8, {})} | custom-call | flops 25000000 | bytes 6291456 | tf_op jit(solution)/shard_map/pallas_call | solution.py:369
  26.4 6.8 %collective-permute-done.10.refs_5_ = bf16[12,128,128]{2,1,0:T(8,128)(2,1)S(1)} collective-permute-done((bf16[12,128,128]{2,1,0:T(8,128)(2,1)S(1)}, bf16[12,128,128]{2,1,0:T(8,128)(2,1)S(1)}, u32[]{:S(2)}, u32[]{:S(2)}) %collective-permute-start.10) | collective-permute-done | bytes 393248 | tf_op jit(solution)/shard_map/ppermute | solution.py:363
  34.9 6.0 %collective-permute-done.9.refs_5_ = bf16[12,128,128]{2,1,0:T(8,128)(2,1)S(1)} collective-permute-done((bf16[12,128,128]{2,1,0:T(8,128)(2,1)S(1)}, bf16[12,128,128]{2,1,0:T(8,128)(2,1)S(1)}, u32[]{:S(2)}, u32[]{:S(2)}) %collective-permute-start.9) | collective-permute-done | bytes 393248 | tf_op jit(solution)/shard_map/ppermute | solution.py:363
  42.4 1.8 %collective-permute-start.14 = (bf16[392,128]{1,0:T(8,128)(2,1)S(1)}, bf16[392,128]{1,0:T(8,128)(2,1)S(1)}, u32[]{:S(2)}, u32[]{:S(2)}) collective-permute-start(bf16[392,128]{1,0:T(8,128)(2,1)S(1)} %get-tuple-element.83), channel_id=1, source_target_pairs={{0,2},{1,3},{2,0},{3,1},{4,6},{5,7},{6,4},{7,5},{8,10},{9,11},{10,... | collective-permute-start | bytes 301064 | tf_op jit(solution)/shard_map/ppermute | solution.py:383
  46.1 3.6 %collective-permute-start.1 = (bf16[392,128]{1,0:T(8,128)(2,1)S(1)}, bf16[392,128]{1,0:T(8,128)(2,1)S(1)}, u32[]{:S(2)}, u32[]{:S(2)}) collective-permute-start(bf16[392,128]{1,0:T(8,128)(2,1)S(1)} %get-tuple-element.59), channel_id=1, source_target_pairs={{0,12},{1,13},{2,14},{3,15},{4,8},{5,9},{6,10},{7,11},{8,4},{9,5},... | collective-permute-start | bytes 301064 | tf_op jit(solution)/shard_map/ppermute | solution.py:383
  49.7 4.1 %collective-permute-start.5 = (bf16[392,128]{1,0:T(8,128)(2,1)S(1)}, bf16[392,128]{1,0:T(8,128)(2,1)S(1)}, u32[]{:S(2)}, u32[]{:S(2)}) collective-permute-start(bf16[392,128]{1,0:T(8,128)(2,1)S(1)} %get-tuple-element.61), channel_id=1, source_target_pairs={{0,14},{1,15},{2,12},{3,13},{4,10},{5,11},{6,8},{7,9},{8,6},{9,7},... | collective-permute-start | bytes 301064 | tf_op jit(solution)/shard_map/ppermute | solution.py:383
  56.9 11.3 %collective-permute-start.30 = (bf16[392,128]{1,0:T(8,128)(2,1)S(1)}, bf16[392,128]{1,0:T(8,128)(2,1)S(1)}, u32[]{:S(2)}, u32[]{:S(2)}) collective-permute-start(bf16[392,128]{1,0:T(8,128)(2,1)S(1)} %get-tuple-element.91), channel_id=1, source_target_pairs={{0,10},{1,11},{2,8},{3,9},{4,14},{5,15},{6,12},{7,13},{8,2},{9,3},... | collective-permute-start | bytes 301064 | tf_op jit(solution)/shard_map/ppermute | solution.py:383
  68.2 1.6 %collective-permute-start.32 = (bf16[392,128]{1,0:T(8,128)(2,1)S(1)}, bf16[392,128]{1,0:T(8,128)(2,1)S(1)}, u32[]{:S(2)}, u32[]{:S(2)}) collective-permute-start(bf16[392,128]{1,0:T(8,128)(2,1)S(1)} %get-tuple-element.92), channel_id=1, source_target_pairs={{0,11},{1,10},{2,9},{3,8},{4,15},{5,14},{6,13},{7,12},{8,3},{9,2},... | collective-permute-start | bytes 301064 | tf_op jit(solution)/shard_map/ppermute | solution.py:383
  69.8 5.8 %collective-permute-start.18 = (bf16[392,128]{1,0:T(8,128)(2,1)S(1)}, bf16[392,128]{1,0:T(8,128)(2,1)S(1)}, u32[]{:S(2)}, u32[]{:S(2)}) collective-permute-start(bf16[392,128]{1,0:T(8,128)(2,1)S(1)} %get-tuple-element.85), channel_id=1, source_target_pairs={{0,4},{1,5},{2,6},{3,7},{4,0},{5,1},{6,2},{7,3},{8,12},{9,13},{10,... | collective-permute-start | bytes 301064 | tf_op jit(solution)/shard_map/ppermute | solution.py:383
  75.7 3.1 %collective-permute-done.26.refs_9_ = bf16[392,128]{1,0:T(8,128)(2,1)S(1)} collective-permute-done((bf16[392,128]{1,0:T(8,128)(2,1)S(1)}, bf16[392,128]{1,0:T(8,128)(2,1)S(1)}, u32[]{:S(2)}, u32[]{:S(2)}) %collective-permute-start.26) | collective-permute-done | bytes 100384 | tf_op jit(solution)/shard_map/ppermute | solution.py:383
  80.6 3.4 %collective-permute-done.30.refs_13_ = bf16[392,128]{1,0:T(8,128)(2,1)S(1)} collective-permute-done((bf16[392,128]{1,0:T(8,128)(2,1)S(1)}, bf16[392,128]{1,0:T(8,128)(2,1)S(1)}, u32[]{:S(2)}, u32[]{:S(2)}) %collective-permute-start.30) | collective-permute-done | bytes 100384 | tf_op jit(solution)/shard_map/ppermute | solution.py:383
  86.4 2.2 %collective-permute-done.20.refs_3_ = bf16[392,128]{1,0:T(8,128)(2,1)S(1)} collective-permute-done((bf16[392,128]{1,0:T(8,128)(2,1)S(1)}, bf16[392,128]{1,0:T(8,128)(2,1)S(1)}, u32[]{:S(2)}, u32[]{:S(2)}) %collective-permute-start.20) | collective-permute-done | bytes 100384 | tf_op jit(solution)/shard_map/ppermute | solution.py:383
  90.6 1.6 %collective-permute-done.24.refs_7_ = bf16[392,128]{1,0:T(8,128)(2,1)S(1)} collective-permute-done((bf16[392,128]{1,0:T(8,128)(2,1)S(1)}, bf16[392,128]{1,0:T(8,128)(2,1)S(1)}, u32[]{:S(2)}, u32[]{:S(2)}) %collective-permute-start.24) | collective-permute-done | bytes 100384 | tf_op jit(solution)/shard_map/ppermute | solution.py:383
  106.9 5.0 %shard_map.100 = (bf16[96,128,128]{2,1,0:T(8,128)(2,1)}, f32[1,128]{1,0:T(1,128)S(1)}, f32[48,128,128]{2,1,0:T(8,128)}, f32[48,128,128]{2,1,0:T(8,128)}, f32[48,128,128]{2,1,0:T(8,128)}) custom-call(s32[16,128]{1,0:T(8,128)S(1)} %get-tuple-element.53.refs_0_, bf16[392,128]{1,0:T(8,128)(2,1)S(1)} %collective-permute-done.1.refs_1_, ...), custom_call_target="tpu_custom_call" | custom-call | flops 5000000 | bytes 2097152 | tf_op jit(solution)/shard_map/pallas_call | solution.py:425
  114.9 2.1 %collective-permute-done.25.refs_8_ = bf16[392,128]{1,0:T(8,128)(2,1)S(1)} collective-permute-done((bf16[392,128]{1,0:T(8,128)(2,1)S(1)}, bf16[392,128]{1,0:T(8,128)(2,1)S(1)}, u32[]{:S(2)}, u32[]{:S(2)}) %collective-permute-start.25) | collective-permute-done | bytes 100384 | tf_op jit(solution)/shard_map/ppermute | solution.py:391
  117.1 2.4 %shard_map.101 = (bf16[96,128,128]{2,1,0:T(8,128)(2,1)}, f32[1,128]{1,0:T(1,128)S(1)}) custom-call(s32[16,128]{1,0:T(8,128)S(1)} %get-tuple-element.53.refs_0_, bf16[392,128]{1,0:T(8,128)(2,1)S(1)} %collective-permute-done.18.refs_1_, bf16[392,128]{1,0:T(8,128)(2,1)S(1)} %collective-permute-done.19.refs_2_, ...), custom_call_target="tpu_custom_call", output_to_operand_aliasing={{0}: (21, {})} | custom-call | flops 5000000 | bytes 2097152 | tf_op jit(solution)/shard_map/pallas_call | solution.py:425
  (62 shorter events, 34.7 us)
Async XLA Ops:
  3.4 13.4 %collective-permute-start = (bf16[12,128,128]{2,1,0:T(8,128)(2,1)S(1)}, bf16[12,128,128]{2,1,0:T(8,128)(2,1)S(1)}, u32[]{:S(2)}, u32[]{:S(2)}) collective-permute-start(bf16[12,128,128]{2,1,0:T(8,128)(2,1)S(1)} %get-tuple-element.58), channel_id=1, source_target_pairs={{0,16},{16,0},{1,17},{17,1},{2,18},{18,2},{3,19},{19,3},{4,20},{20... | collective-permute-start | bytes 1179656 | tf_op jit(solution)/shard_map/ppermute | solution.py:363
  9.6 15.2 %collective-permute-start.11 = (bf16[12,128,128]{2,1,0:T(8,128)(2,1)S(1)}, bf16[12,128,128]{2,1,0:T(8,128)(2,1)S(1)}, u32[]{:S(2)}, u32[]{:S(2)}) collective-permute-start(bf16[12,128,128]{2,1,0:T(8,128)(2,1)S(1)} %get-tuple-element.65), channel_id=1, source_target_pairs={{0,16},{16,0},{1,17},{17,1},{2,18},{18,2},{3,19},{19,3},{4,20},{20... | collective-permute-start | bytes 1179656 | tf_op jit(solution)/shard_map/ppermute | solution.py:363
  12.1 21.1 %collective-permute-start.10 = (bf16[12,128,128]{2,1,0:T(8,128)(2,1)S(1)}, bf16[12,128,128]{2,1,0:T(8,128)(2,1)S(1)}, u32[]{:S(2)}, u32[]{:S(2)}) collective-permute-start(bf16[12,128,128]{2,1,0:T(8,128)(2,1)S(1)} %get-tuple-element.64), channel_id=1, source_target_pairs={{0,16},{16,0},{1,17},{17,1},{2,18},{18,2},{3,19},{19,3},{4,20},{20... | collective-permute-start | bytes 1179656 | tf_op jit(solution)/shard_map/ppermute | solution.py:363
  16.6 24.2 %collective-permute-start.9 = (bf16[12,128,128]{2,1,0:T(8,128)(2,1)S(1)}, bf16[12,128,128]{2,1,0:T(8,128)(2,1)S(1)}, u32[]{:S(2)}, u32[]{:S(2)}) collective-permute-start(bf16[12,128,128]{2,1,0:T(8,128)(2,1)S(1)} %get-tuple-element.63), channel_id=1, source_target_pairs={{0,16},{16,0},{1,17},{17,1},{2,18},{18,2},{3,19},{19,3},{4,20},{20... | collective-permute-start | bytes 1179656 | tf_op jit(solution)/shard_map/ppermute | solution.py:363
  44.2 9.6 %collective-permute-start.12 = (bf16[392,128]{1,0:T(8,128)(2,1)S(1)}, bf16[392,128]{1,0:T(8,128)(2,1)S(1)}, u32[]{:S(2)}, u32[]{:S(2)}) collective-permute-start(bf16[392,128]{1,0:T(8,128)(2,1)S(1)} %get-tuple-element.75.refs_9_), channel_id=1, source_target_pairs={{0,16},{16,0},{1,17},{17,1},{2,18},{18,2},{3,19},{19,3},{4,20},{20... | collective-permute-start | bytes 301064 | tf_op jit(solution)/shard_map/ppermute | solution.py:391
  45.7 9.6 %collective-permute-start.13 = (bf16[392,128]{1,0:T(8,128)(2,1)S(1)}, bf16[392,128]{1,0:T(8,128)(2,1)S(1)}, u32[]{:S(2)}, u32[]{:S(2)}) collective-permute-start(bf16[392,128]{1,0:T(8,128)(2,1)S(1)} %get-tuple-element.76), channel_id=1, source_target_pairs={{0,1},{1,0},{2,3},{3,2},{4,5},{5,4},{6,7},{7,6},{8,9},{9,8},{10,11... | collective-permute-start | bytes 301064 | tf_op jit(solution)/shard_map/ppermute | solution.py:383
  46.1 9.2 %collective-permute-start.1 = (bf16[392,128]{1,0:T(8,128)(2,1)S(1)}, bf16[392,128]{1,0:T(8,128)(2,1)S(1)}, u32[]{:S(2)}, u32[]{:S(2)}) collective-permute-start(bf16[392,128]{1,0:T(8,128)(2,1)S(1)} %get-tuple-element.59), channel_id=1, source_target_pairs={{0,12},{1,13},{2,14},{3,15},{4,8},{5,9},{6,10},{7,11},{8,4},{9,5},... | collective-permute-start | bytes 301064 | tf_op jit(solution)/shard_map/ppermute | solution.py:383
  49.7 18.5 %collective-permute-start.5 = (bf16[392,128]{1,0:T(8,128)(2,1)S(1)}, bf16[392,128]{1,0:T(8,128)(2,1)S(1)}, u32[]{:S(2)}, u32[]{:S(2)}) collective-permute-start(bf16[392,128]{1,0:T(8,128)(2,1)S(1)} %get-tuple-element.61), channel_id=1, source_target_pairs={{0,14},{1,15},{2,12},{3,13},{4,10},{5,11},{6,8},{7,9},{8,6},{9,7},... | collective-permute-start | bytes 301064 | tf_op jit(solution)/shard_map/ppermute | solution.py:383
  53.8 16.0 %collective-permute-start.7 = (bf16[392,128]{1,0:T(8,128)(2,1)S(1)}, bf16[392,128]{1,0:T(8,128)(2,1)S(1)}, u32[]{:S(2)}, u32[]{:S(2)}) collective-permute-start(bf16[392,128]{1,0:T(8,128)(2,1)S(1)} %get-tuple-element.62), channel_id=1, source_target_pairs={{0,15},{1,14},{2,13},{3,12},{4,11},{5,10},{6,9},{7,8},{8,7},{9,6},... | collective-permute-start | bytes 301064 | tf_op jit(solution)/shard_map/ppermute | solution.py:383
  55.3 23.4 %collective-permute-start.26 = (bf16[392,128]{1,0:T(8,128)(2,1)S(1)}, bf16[392,128]{1,0:T(8,128)(2,1)S(1)}, u32[]{:S(2)}, u32[]{:S(2)}) collective-permute-start(bf16[392,128]{1,0:T(8,128)(2,1)S(1)} %get-tuple-element.89), channel_id=1, source_target_pairs={{0,8},{1,9},{2,10},{3,11},{4,12},{5,13},{6,14},{7,15},{8,0},{9,1},... | collective-permute-start | bytes 301064 | tf_op jit(solution)/shard_map/ppermute | solution.py:383
  55.3 23.9 %collective-permute-start.28 = (bf16[392,128]{1,0:T(8,128)(2,1)S(1)}, bf16[392,128]{1,0:T(8,128)(2,1)S(1)}, u32[]{:S(2)}, u32[]{:S(2)}) collective-permute-start(bf16[392,128]{1,0:T(8,128)(2,1)S(1)} %get-tuple-element.90), channel_id=1, source_target_pairs={{0,9},{1,8},{2,11},{3,10},{4,13},{5,12},{6,15},{7,14},{8,1},{9,0},... | collective-permute-start | bytes 301064 | tf_op jit(solution)/shard_map/ppermute | solution.py:383
  56.9 27.1 %collective-permute-start.30 = (bf16[392,128]{1,0:T(8,128)(2,1)S(1)}, bf16[392,128]{1,0:T(8,128)(2,1)S(1)}, u32[]{:S(2)}, u32[]{:S(2)}) collective-permute-start(bf16[392,128]{1,0:T(8,128)(2,1)S(1)} %get-tuple-element.91), channel_id=1, source_target_pairs={{0,10},{1,11},{2,8},{3,9},{4,14},{5,15},{6,12},{7,13},{8,2},{9,3},... | collective-permute-start | bytes 301064 | tf_op jit(solution)/shard_map/ppermute | solution.py:383
  68.2 16.0 %collective-permute-start.32 = (bf16[392,128]{1,0:T(8,128)(2,1)S(1)}, bf16[392,128]{1,0:T(8,128)(2,1)S(1)}, u32[]{:S(2)}, u32[]{:S(2)}) collective-permute-start(bf16[392,128]{1,0:T(8,128)(2,1)S(1)} %get-tuple-element.92), channel_id=1, source_target_pairs={{0,11},{1,10},{2,9},{3,8},{4,15},{5,14},{6,13},{7,12},{8,3},{9,2},... | collective-permute-start | bytes 301064 | tf_op jit(solution)/shard_map/ppermute | solution.py:383
  69.8 16.5 %collective-permute-start.18 = (bf16[392,128]{1,0:T(8,128)(2,1)S(1)}, bf16[392,128]{1,0:T(8,128)(2,1)S(1)}, u32[]{:S(2)}, u32[]{:S(2)}) collective-permute-start(bf16[392,128]{1,0:T(8,128)(2,1)S(1)} %get-tuple-element.85), channel_id=1, source_target_pairs={{0,4},{1,5},{2,6},{3,7},{4,0},{5,1},{6,2},{7,3},{8,12},{9,13},{10,... | collective-permute-start | bytes 301064 | tf_op jit(solution)/shard_map/ppermute | solution.py:383
  78.7 9.9 %collective-permute-start.20 = (bf16[392,128]{1,0:T(8,128)(2,1)S(1)}, bf16[392,128]{1,0:T(8,128)(2,1)S(1)}, u32[]{:S(2)}, u32[]{:S(2)}) collective-permute-start(bf16[392,128]{1,0:T(8,128)(2,1)S(1)} %get-tuple-element.86), channel_id=1, source_target_pairs={{0,5},{1,4},{2,7},{3,6},{4,1},{5,0},{6,3},{7,2},{8,13},{9,12},{10,... | collective-permute-start | bytes 301064 | tf_op jit(solution)/shard_map/ppermute | solution.py:383
  79.2 10.3 %collective-permute-start.22 = (bf16[392,128]{1,0:T(8,128)(2,1)S(1)}, bf16[392,128]{1,0:T(8,128)(2,1)S(1)}, u32[]{:S(2)}, u32[]{:S(2)}) collective-permute-start(bf16[392,128]{1,0:T(8,128)(2,1)S(1)} %get-tuple-element.87), channel_id=1, source_target_pairs={{0,6},{1,7},{2,4},{3,5},{4,2},{5,3},{6,0},{7,1},{8,14},{9,15},{10,... | collective-permute-start | bytes 301064 | tf_op jit(solution)/shard_map/ppermute | solution.py:383
  84.2 10.4 %collective-permute-start.2 = (bf16[392,128]{1,0:T(8,128)(2,1)S(1)}, bf16[392,128]{1,0:T(8,128)(2,1)S(1)}, u32[]{:S(2)}, u32[]{:S(2)}) collective-permute-start(bf16[392,128]{1,0:T(8,128)(2,1)S(1)} %collective-permute-done.1.refs_1_), channel_id=1, source_target_pairs={{0,16},{16,0},{1,17},{17,1},{2,18},{18,2},{3,19},{19,3},{4,20},{20... | collective-permute-start | bytes 301064 | tf_op jit(solution)/shard_map/ppermute | solution.py:391
  86.4 9.8 %collective-permute-start.4 = (bf16[392,128]{1,0:T(8,128)(2,1)S(1)}, bf16[392,128]{1,0:T(8,128)(2,1)S(1)}, u32[]{:S(2)}, u32[]{:S(2)}) collective-permute-start(bf16[392,128]{1,0:T(8,128)(2,1)S(1)} %collective-permute-done.3.refs_3_), channel_id=1, source_target_pairs={{0,16},{16,0},{1,17},{17,1},{2,18},{18,2},{3,19},{19,3},{4,20},{20... | collective-permute-start | bytes 301064 | tf_op jit(solution)/shard_map/ppermute | solution.py:391
  96.6 9.7 %collective-permute-start.31 = (bf16[392,128]{1,0:T(8,128)(2,1)S(1)}, bf16[392,128]{1,0:T(8,128)(2,1)S(1)}, u32[]{:S(2)}, u32[]{:S(2)}) collective-permute-start(bf16[392,128]{1,0:T(8,128)(2,1)S(1)} %collective-permute-done.30.refs_13_), channel_id=1, source_target_pairs={{0,16},{16,0},{1,17},{17,1},{2,18},{18,2},{3,19},{19,3},{4,20},{20... | collective-permute-start | bytes 301064 | tf_op jit(solution)/shard_map/ppermute | solution.py:391
  98.2 13.7 %collective-permute-start.33 = (bf16[392,128]{1,0:T(8,128)(2,1)S(1)}, bf16[392,128]{1,0:T(8,128)(2,1)S(1)}, u32[]{:S(2)}, u32[]{:S(2)}) collective-permute-start(bf16[392,128]{1,0:T(8,128)(2,1)S(1)} %collective-permute-done.32.refs_15_), channel_id=1, source_target_pairs={{0,16},{16,0},{1,17},{17,1},{2,18},{18,2},{3,19},{19,3},{4,20},{20... | collective-permute-start | bytes 301064 | tf_op jit(solution)/shard_map/ppermute | solution.py:391
  99.9 13.6 %collective-permute-start.19 = (bf16[392,128]{1,0:T(8,128)(2,1)S(1)}, bf16[392,128]{1,0:T(8,128)(2,1)S(1)}, u32[]{:S(2)}, u32[]{:S(2)}) collective-permute-start(bf16[392,128]{1,0:T(8,128)(2,1)S(1)} %collective-permute-done.18.refs_1_), channel_id=1, source_target_pairs={{0,16},{16,0},{1,17},{17,1},{2,18},{18,2},{3,19},{19,3},{4,20},{20... | collective-permute-start | bytes 301064 | tf_op jit(solution)/shard_map/ppermute | solution.py:391
  102.0 12.0 %collective-permute-start.21 = (bf16[392,128]{1,0:T(8,128)(2,1)S(1)}, bf16[392,128]{1,0:T(8,128)(2,1)S(1)}, u32[]{:S(2)}, u32[]{:S(2)}) collective-permute-start(bf16[392,128]{1,0:T(8,128)(2,1)S(1)} %collective-permute-done.20.refs_3_), channel_id=1, source_target_pairs={{0,16},{16,0},{1,17},{17,1},{2,18},{18,2},{3,19},{19,3},{4,20},{20... | collective-permute-start | bytes 301064 | tf_op jit(solution)/shard_map/ppermute | solution.py:391
  104.2 10.8 %collective-permute-start.23 = (bf16[392,128]{1,0:T(8,128)(2,1)S(1)}, bf16[392,128]{1,0:T(8,128)(2,1)S(1)}, u32[]{:S(2)}, u32[]{:S(2)}) collective-permute-start(bf16[392,128]{1,0:T(8,128)(2,1)S(1)} %collective-permute-done.22.refs_5_), channel_id=1, source_target_pairs={{0,16},{16,0},{1,17},{17,1},{2,18},{18,2},{3,19},{19,3},{4,20},{20... | collective-permute-start | bytes 301064 | tf_op jit(solution)/shard_map/ppermute | solution.py:391
  106.3 10.8 %collective-permute-start.25 = (bf16[392,128]{1,0:T(8,128)(2,1)S(1)}, bf16[392,128]{1,0:T(8,128)(2,1)S(1)}, u32[]{:S(2)}, u32[]{:S(2)}) collective-permute-start(bf16[392,128]{1,0:T(8,128)(2,1)S(1)} %collective-permute-done.24.refs_7_), channel_id=1, source_target_pairs={{0,16},{16,0},{1,17},{17,1},{2,18},{18,2},{3,19},{19,3},{4,20},{20... | collective-permute-start | bytes 301064 | tf_op jit(solution)/shard_map/ppermute | solution.py:391
  (12 other events, 83.1 us)

commit v4 on v3

--- a/solution.py
+++ b/solution.py
@@ -12,8 +12,14 @@
 LANES = 128
 UNROLL = 2
 SPLIT = 4
-STAGES = {(0, 2, 1): 2, (0, 3, 1): 2, (0, 2, 0): 1, (0, 3, 0): 1, (0, 1, 1): 1}
-STAGES |= {(k, q, s): 1 for k in (1, 2) for q in range(4) for s in range(2)}
+MERGES = (
+    ((3, 0), (3, 1), (3, 2), (3, 3)),
+    ((1, 0), (1, 1), (1, 2), (1, 3)),
+    ((2, 0),),
+    ((2, 1), (0, 1)),
+    ((2, 2), (2, 3)),
+    ((0, 2), (0, 3)),
+)
 PACK_MIB = 4
 ADAM_MIB = 4
 
@@ -109,7 +115,7 @@
     if entries != plan.sub_len:
         lax.fori_loop(0, entries, clear, 0)
     lax.fori_loop(0, plan.owners, zero, 0, unroll=True)
-    lax.fori_loop(0, plan.sub_len, enter, 0, unroll=4)
+    lax.fori_loop(0, plan.sub_len, enter, 0, unroll=12)
 
 
 def find_slots(plan, table, out):
@@ -155,7 +161,11 @@
     rows, count = take(2) if lead or own else (None, None)
     (flat,) = take(1) if own else (None,)
     (sems,) = take(1)
-    pairs = list(zip(sources, targets))
+    pairs = []
+    for a, b in zip(sources, targets):
+        size = a.shape[0] // SPLIT
+        pairs += [(a.at[pl.ds(n * size, size)], b.at[pl.ds(n * size, size)]) for n in range(SPLIT)]
+    loads *= SPLIT
     pairs += [(table, rows)] * bool(lead or own) + [(table, flat)] * bool(own)
     copies = [pltpu.make_async_copy(a, b, sems.at[n]) for n, (a, b) in enumerate(pairs)]
     for copy in copies:
@@ -164,14 +174,15 @@
     if lead:
         copies[loads].wait()
         fill_order(part, plan, rows, order, part * entries_of_part, count)
-        copies[0].wait()
+        for copy in copies[:loads]:
+            copy.wait()
     base = part * entries_of_part + chunk * entries
 
     def body(i, carry):
         out[i] = extract(grads.at[order[base + i]], wide, part, parts).astype(out.dtype)
         return carry
 
-    lax.fori_loop(0, entries, body, 0)
+    lax.fori_loop(0, entries, body, 0, unroll=3)
     if lead:
         for s in range(1, parts - 1):
             later = lax.rem(part + s, parts)
@@ -183,7 +194,7 @@
         fill_order(here, plan, rows, order_own, 0, count)
         find_slots(plan, flat, slots)
     for n, copy in enumerate(copies):
-        if not (lead and n == 0) and not (lead and n == loads) and not (own and n >= loads):
+        if n < loads and not lead:
             copy.wait()
 
 
@@ -194,7 +205,8 @@
     refs = refs[4 + parts + (0 if first else 3) :]
     master_out, moment_out, second_out = refs[:3]
     blocks = refs[3 : 3 + plan.near]
-    wide, peak = refs[3 + plan.near :]
+    apart = refs[3 + plan.near : -2]
+    wide, peak = refs[-2:]
     part = lax.axis_index("dp")
     base = chunk * entries
     first_fix = 1.0 / (1.0 - beta_first**step_count)
@@ -240,36 +252,50 @@
             for b in range(0, TB, 16):
                 pair = [master_out[tile, pl.ds(b + s, 8), :] * inverse for s in (0, 8)]
                 block[pl.ds(r * TB + b, 16), :] = jnp.concatenate(pair, axis=0).astype(block.dtype)
-        block[pl.ds(room * TB, plan.pad), :] = tail.astype(block.dtype)
-
-
-def tails_kernel(plan, *refs):
-    out = refs[-1]
-    for n, ref in enumerate(refs[:-1]):
-        out[n] = ref[pl.ds(plan.room * TB, plan.pad), :]
-
-
-def place_kernel(plan, sources, count, tails, first, gathers, *refs):
+        if q == 0 and apart:
+            apart[0][...] = tail.astype(block.dtype)
+        else:
+            block[pl.ds(room * TB, plan.pad), :] = tail.astype(block.dtype)
+
+
+def store_kernel(held, saved, sems):
+    size = held.shape[0] // SPLIT
+    copies = []
+    for n in range(SPLIT):
+        piece = pl.ds(n * size, size)
+        copies.append(pltpu.make_async_copy(held.at[piece], saved.at[piece], sems.at[n]))
+    for copy in copies:
+        copy.start()
+    for copy in copies:
+        copy.wait()
+
+
+def merge_kernel(plan, count, ends, *refs):
+    blocks, tails = refs[:count], refs[count : count + ends]
+    rows = plan.room * TB
+    for n, block in enumerate(blocks):
+        refs[count + ends][pl.ds(n * rows, rows), :] = block[pl.ds(0, rows), :]
+    if ends:
+        out = refs[-1]
+        group = lax.broadcasted_iota(jnp.int32, out.shape, 1) // (LANES // ends)
+        total = jnp.zeros(out.shape, jnp.float32)
+        for n, ref in enumerate(tails):
+            tail = ref[pl.ds(ref.shape[0] - plan.pad, plan.pad), :].astype(jnp.float32)
+            total = jnp.where(group == n, tail, total)
+        out[...] = total.astype(out.dtype)
+
+
+def place_kernel(plan, sources, count, keys, first, gathers, *refs):
     room = plan.room
     refs = list(refs)
     take = lambda n: [refs.pop(0) for _ in range(n)]
     (slots,), blocks = take(1), take(count)
-    late = take(1) if tails else []
-    held = take(3) if first else []
-    before = take(2)[1:] if gathers and not first else []
-    if not first and not gathers:
+    late = take(plan.parts) if gathers and keys else []
+    if not first:
         take(1)
     (tiles_out,) = take(1)
     (scales_out,) = take(1) if gathers else (None,)
-    saved = take(3) if first else []
     (sems,) = take(1)
-    stores = []
-    for a, b in zip(held, saved):
-        for n in range(0, plan.tiles, plan.tiles // SPLIT):
-            piece = pl.ds(n, plan.tiles // SPLIT)
-            stores.append(pltpu.make_async_copy(a.at[piece], b.at[piece], refs[0].at[len(stores)]))
-    for copy in stores:
-        copy.start()
     here, me = lax.axis_index("dp"), lax.axis_index("shard")
 
     def slot_of(k, q, shift, r):
@@ -278,10 +304,12 @@
 
     entries, views = [], []
     for n, (ref, k, q, shift, at) in enumerate(sources):
-        views.append(blocks[ref] if at is None else blocks[ref].at[at])
+        stacked = len(blocks[ref].shape) == 3
+        views.append(blocks[ref].at[at] if stacked else blocks[ref])
+        start = 0 if stacked or at is None else at * room * TB
         for r in range(room):
             slot = slot_of(k, q, shift, r)
-            copy = pltpu.make_async_copy(views[n].at[pl.ds(r * TB, TB)], tiles_out.at[slot], sems.at[n * room + r])
+            copy = pltpu.make_async_copy(views[n].at[pl.ds(start + r * TB, TB)], tiles_out.at[slot], sems.at[n * room + r])
             entries.append((slot, copy))
             if room * plan.owners == plan.sub_len:
                 copy.start()
@@ -289,9 +317,16 @@
                 pl.when(slot >= 0)(copy.start)
     if gathers:
         lane = lax.broadcasted_iota(jnp.int32, scales_out.shape, 1)
-        total = before[0][...] if before else jnp.zeros(scales_out.shape, jnp.float32)
-        ends = [(view[pl.ds(room * TB, plan.pad), :], key[1:4]) for view, key in zip(views, sources)]
-        ends += [(late[0][n], key) for n, key in enumerate(tails)]
+        total = jnp.zeros(scales_out.shape, jnp.float32)
+        ends = []
+        if keys:
+            for shift, ref in enumerate(late):
+                packed = ref[...].astype(jnp.float32)
+                for n, (k, q) in enumerate(keys):
+                    at = n * (LANES // len(keys))
+                    ends.append((jnp.broadcast_to(packed[:, at : at + 1], packed.shape), (k, q, shift)))
+        else:
+            ends = [(view[pl.ds(room * TB, plan.pad), :], key[1:4]) for view, key in zip(views, sources)]
         for rows, (k, q, shift) in ends:
             for r in range(room):
                 wide = jnp.concatenate([rows[r : r + 1].astype(jnp.float32)] * (scales_out.shape[1] // LANES), axis=1)
@@ -302,8 +337,6 @@
             copy.wait()
         else:
             pl.when(slot >= 0)(copy.wait)
-    for copy in stores:
-        copy.wait()
 
 
 def per_device(gradients, tile_table, master, moment, second):
@@ -347,7 +380,7 @@
             scratch_shapes=[pltpu.VMEM((TB * parts, TB), jnp.float32)]
             + [pltpu.SMEM(tile_table.shape, jnp.int32), pltpu.SMEM((owners,), jnp.int32)] * tabled
             + [pltpu.VMEM(tile_table.shape, jnp.int32)] * own
-            + [pltpu.SemaphoreType.DMA((max(1, loads + tabled + own),))],
+            + [pltpu.SemaphoreType.DMA((max(1, loads * SPLIT + tabled + own),))],
             compiler_params=pltpu.CompilerParams(vmem_limit_bytes=PACK_MIB << 20),
             cost_estimate=pl.CostEstimate(flops=6000000, bytes_accessed=2 << 20, transcendentals=0),
         )(*operands)
@@ -366,43 +399,59 @@
     groups = {}
     for k in plan.chunks:
         count = 5 + parts - 1
+        apart = parts == 2 and k == 0
+        shapes = [block_shape] * plan.near
+        if apart:
+            shapes[0] = pltpu.VMEM((room * TB, TB), jnp.bfloat16)
+            shapes.append(pltpu.VMEM((plan.pad, LANES), jnp.bfloat16))
         results = pl.pallas_call(
             functools.partial(adam_kernel, plan, k, not news),
-            out_shape=[f32_tiles] * 3 + [block_shape] * plan.near,
+            out_shape=[f32_tiles] * 3 + shapes,
             in_specs=[SMEM] + [VMEM] * (3 + parts) + [VMEM] * len(news),
-            out_specs=[VMEM] * (3 + plan.near),
+            out_specs=[VMEM] * (3 + len(shapes)),
             input_output_aliases={count + j: j for j in range(len(news))},
             scratch_shapes=[pltpu.VMEM((TB * parts, TB), jnp.float32), pltpu.VMEM((entries, 8, LANES), jnp.float32)],
             compiler_params=pltpu.CompilerParams(vmem_limit_bytes=ADAM_MIB << 20),
             cost_estimate=pl.CostEstimate(flops=25000000, bytes_accessed=6 << 20, transcendentals=0),
         )(order_own, *in_vmem([grads, *states]), *arrived[k], *in_vmem(news))
-        news, blocks = results[:3], results[3:]
+        news, blocks = results[:3], results[3 : 3 + plan.near]
+        if apart:
+            tail_apart = results[-1]
         groups[k] = []
         for q, block in enumerate(blocks):
             if k or q:
                 block = lax.ppermute(block, "shard", plan.pattern(k, q))
             groups[k].append(block)
 
-    entries = []
+    entries, stage = [], []
     tails, tail_keys = [], []
     if parts == 2:
-        for k in plan.chunks:
-            for q, block in enumerate(groups[k]):
-                passed = lax.ppermute(block, "dp", cycles[1])
-                entries += [((k, q, 0, None), block), ((k, q, 1, None), passed)]
-        stage = [STAGES.get(key[:3], 0) for key, _ in entries]
-        stage = stage if 2 in stage else [2 * (n == len(entries) - 1) for n in range(len(entries))]
-        tail_keys = [key[:3] for (key, _), at in zip(entries, stage) if at == 2]
-        ends = pl.pallas_call(
-            functools.partial(tails_kernel, plan),
-            out_shape=pltpu.VMEM((len(tail_keys), plan.pad, LANES), jnp.bfloat16),
-            in_specs=[VMEM] * len(tail_keys),
-            out_specs=VMEM,
-            compiler_params=pltpu.CompilerParams(vmem_limit_bytes=1 << 20),
-            cost_estimate=pl.CostEstimate(flops=1000000, bytes_accessed=1 << 20, transcendentals=0),
-            name="tails",
-        )(*[groups[k][q] for k, q, _ in tail_keys])
-        tails = [lax.ppermute(ends, "dp", cycles[1])]
+        tail_keys = [(k, q) for k in plan.chunks for q in range(plan.near)]
+        merges = [keys for keys in MERGES if all(key in tail_keys for key in keys)]
+        rest = [key for key in tail_keys if key != (0, 0) and not any(key in keys for keys in merges)]
+        merges = [[key] for key in rest] + merges
+        for (k, q), block in ((key, groups[key[0]][key[1]]) for key in tail_keys):
+            entries.append(((k, q, 0, None), block))
+            stage.append(int((k, q) in merges[-1] and len(merges) > 1))
+        entries.append(((0, 0, 1, None), lax.ppermute(groups[0][0], "dp", cycles[1])))
+        stage.append(0)
+        for n, keys in enumerate(merges):
+            ends = [tail_apart if key == (0, 0) else groups[key[0]][key[1]] for key in tail_keys]
+            ends = ends if n == len(merges) - 1 else []
+            merged = pl.pallas_call(
+                functools.partial(merge_kernel, plan, len(keys), len(ends)),
+                out_shape=[pltpu.VMEM((len(keys) * room * TB, TB), jnp.bfloat16)]
+                + [pltpu.VMEM((plan.pad, LANES), jnp.bfloat16)] * bool(ends),
+                in_specs=[VMEM] * (len(keys) + len(ends)),
+                out_specs=[VMEM] * (1 + bool(ends)),
+                compiler_params=pltpu.CompilerParams(vmem_limit_bytes=1 << 20),
+                cost_estimate=pl.CostEstimate(flops=1000000, bytes_accessed=1 << 20, transcendentals=0),
+            )(*[groups[k][q] for k, q in keys], *ends)
+            if ends:
+                tails = [merged[1], lax.ppermute(merged[1], "dp", cycles[1])]
+            passed = lax.ppermute(merged[0], "dp", cycles[1])
+            entries.append(([(k, q, 1, j) for j, (k, q) in enumerate(keys)], passed))
+            stage.append(2 if n == len(merges) - 1 else int(n > 0 and len(merges) > 1))
     else:
         keys = [(k, q) for k in plan.chunks for q in range(plan.near)]
         stacked = jnp.stack([block for k in plan.chunks for block in groups[k]])
@@ -410,42 +459,54 @@
             passed = lax.ppermute(stacked, "dp", cycles[s]) if s else stacked
             entries.append(([(k, q, s, n) for n, (k, q) in enumerate(keys)], passed))
         stage = [0] * len(entries)
+    saved = []
+    for new in news:
+        saved.append(
+            pl.pallas_call(
+                store_kernel,
+                out_shape=pltpu.HBM((tiles, TB, TB), jnp.float32),
+                in_specs=[VMEM],
+                out_specs=HBM,
+                scratch_shapes=[pltpu.SemaphoreType.DMA((SPLIT,))],
+                compiler_params=pltpu.CompilerParams(vmem_limit_bytes=1 << 20),
+                cost_estimate=pl.CostEstimate(flops=2000000, bytes_accessed=2 << 20, transcendentals=0),
+            )(*in_vmem([new]))
+        )
+
     tiles_shape = pltpu.HBM((owned, TB, TB), jnp.bfloat16)
     width = (owned + LANES - 1) // LANES * LANES
 
-    def place(at, previous, ends):
+    def place(at, previous, ends, gathers):
         group = [e for e, level in zip(entries, stage) if level == at]
-        first, gathers = not previous, at < 2
+        first = not previous
         sources = []
         for n, (key, _) in enumerate(group):
             sources += [(n, *each) for each in (key if isinstance(key, list) else [key])]
         operands = [slots, *[a for _, a in group], *ends]
-        operands += in_vmem(news) if first else in_hbm(previous[:1])
-        operands += previous[1:] if gathers else []
+        operands += in_hbm(previous)
         return pl.pallas_call(
-            functools.partial(place_kernel, plan, sources, len(group), tail_keys if ends else [], first, gathers),
+            functools.partial(place_kernel, plan, sources, len(group), tail_keys, first, gathers),
             out_shape=[tiles_shape]
-            + [jax.ShapeDtypeStruct((1, width), jnp.float32)] * gathers
-            + [pltpu.HBM((tiles, TB, TB), jnp.float32)] * (3 * first),
+            + [jax.ShapeDtypeStruct((1, width), jnp.float32)] * gathers,
             in_specs=[SMEM]
             + [VMEM] * (len(group) + len(ends))
-            + ([VMEM] * 3 if first else [HBM] + [VMEM] * gathers),
-            out_specs=[HBM] + [VMEM] * gathers + [HBM] * (3 * first),
+            + [HBM] * len(previous),
+            out_specs=[HBM] + [VMEM] * gathers,
             input_output_aliases={} if first else {1 + len(group) + len(ends): 0},
-            scratch_shapes=[pltpu.SemaphoreType.DMA((len(sources) * room,))]
-            + [pltpu.SemaphoreType.DMA((3 * SPLIT,))] * first,
+            scratch_shapes=[pltpu.SemaphoreType.DMA((len(sources) * room,))],
             compiler_params=pltpu.CompilerParams(vmem_limit_bytes=24 << 20),
             cost_estimate=pl.CostEstimate(flops=5000000, bytes_accessed=2 << 20, transcendentals=0),
         )(*operands)
 
-    staged = max(stage) > 0
-    tiles_out, scales, *news = place(0, [], [] if 1 in stage else tails)
     if 1 in stage:
-        tiles_out, scales = place(1, [tiles_out, scales], tails)
+        (tiles_out,) = place(0, [], [], False)
+        tiles_out, scales = place(1, [tiles_out], tails, True)
+    else:
+        tiles_out, scales = place(0, [], tails, True)
     scales_out = scales[0, :owned].astype(jnp.bfloat16)
-    if staged:
-        (tiles_out,) = place(2, [tiles_out], [])
-    return (*[a.reshape(master.shape) for a in news], tiles_out, scales_out)
+    if 2 in stage:
+        (tiles_out,) = place(2, [tiles_out], [], False)
+    return (*[a.reshape(master.shape) for a in saved], tiles_out, scales_out)
 
 
 def solution(mesh):

time: 122 us -> 98 us (0.80)
  waiting for transfers between devices: 42.6 us -> 27.3 us
  starting transfers between devices: 52 us -> 41 us
  Pallas kernels: 26 us -> 28.1 us
    ppermute x15, starting transfers between devices: 33 us -> 25.2 us  [per_device(): block = lax.ppermute(block, 'shard', plan.pattern(k, q))]
    ppermute x17 -> x8, waiting for transfers between devices: 10.4 us -> 3.8 us  [the longest x1 2.24 us: per_device(): tails = [merged[1], lax.ppermute(merged[1], 'dp', cycles[1])]]
    ppermute x4, waiting for transfers between devices: 19.3 us -> 13.3 us  [per_device(): arrived.setdefault(k, []).append(lax.ppermute(packed, 'dp', cycles[s]))]
    pallas_call x1 -> x9, Pallas kernels: 0.01 us -> 5.19 us  [the longest x3 5.07 us: per_device(): pl.pallas_call(store_kernel, out_shape=pltpu.HBM((tiles, TB, TB), jnp.flo...]
    ppermute x17 -> x8, starting transfers between devices: 13.7 us -> 10.5 us  [the longest x6 7.35 us: per_device(): passed = lax.ppermute(merged[0], 'dp', cycles[1])]
    pallas_call x3, Pallas kernels: 8.83 us -> 5.88 us  [place(): pl.pallas_call(functools.partial(place_kernel, plan, sources, len(group),...]
    ppermute x15, waiting for transfers between devices: 12.9 us -> 10.2 us  [per_device(): block = lax.ppermute(block, 'shard', plan.pattern(k, q))]
  transfers between devices with their start and end apart: 36 -> 27, of which waited for: 19 -> 8; matrix products, arithmetic and copies ran while one was open for 0% -> 1% of each run, Pallas kernels for 17% -> 25%
where the time goes in v4:
time: 98 us; the launch traced here: 97.7 us
  starting transfers between devices  41 us (42%)
  Pallas kernels  28.1 us (29%)
  waiting for transfers between devices  27.3 us (28%)
    ppermute x15, starting transfers between devices, per_device(): block = lax.ppermute(block, 'shard', plan.pattern(k, q))  25.2 us
    ppermute x4, waiting for transfers between devices, per_device(): arrived.setdefault(k, []).append(lax.ppermute(packed, 'dp', cycles[s]))  13.3 us
    pallas_call x4, Pallas kernels, per_device(): pl.pallas_call(functools.partial(pack_kernel, plan, k, s, lead, own, load...  10.6 us
    ppermute x15, waiting for transfers between devices, per_device(): block = lax.ppermute(block, 'shard', plan.pattern(k, q))  10.2 us
    ppermute x6, starting transfers between devices, per_device(): passed = lax.ppermute(merged[0], 'dp', cycles[1])  7.35 us
    pallas_call x4, Pallas kernels, per_device(): pl.pallas_call(functools.partial(adam_kernel, plan, k, not news), out_sha...  6.42 us
    pallas_call x3, Pallas kernels, place(): pl.pallas_call(functools.partial(place_kernel, plan, sources, len(group),...  5.88 us
    ppermute x4, starting transfers between devices, per_device(): arrived.setdefault(k, []).append(lax.ppermute(packed, 'dp', cycles[s]))  5.3 us
  transfers between devices with their start and end apart: 27, of which 8 were waited for; matrix products, arithmetic and copies ran while one was open for 1% of the time, Pallas kernels for 25%

profile of v4, /device:TPU:0, one launch (start us, length us, event | category | flops | bytes accessed | tf_op | source)
XLA Modules:
  0.0 97.7 jit_solution(14966742442731847581)
XLA Ops:
  0.6 2.7 %shard_map.92 = (s32[96]{0:T(128)S(1)}, bf16[12,128,128]{2,1,0:T(8,128)(2,1)S(1)}, bf16[48,256,128]{2,1,0:T(8,128)(2,1)S(1)}) custom-call(s32[16,96]{1,0:T(8,128)} %refs_0_.3, bf16[48,256,128]{2,1,0:T(8,128)(2,1)} %bitcast.13), custom_call_target="tpu_custom_call" | custom-call | flops 6000000 | bytes 2097152 | tf_op jit(solution)/shard_map/pallas_call | solution.py:375
  3.3 3.1 %collective-permute-start.3 = (bf16[12,128,128]{2,1,0:T(8,128)(2,1)S(1)}, bf16[12,128,128]{2,1,0:T(8,128)(2,1)S(1)}, u32[]{:S(2)}, u32[]{:S(2)}) collective-permute-start(bf16[12,128,128]{2,1,0:T(8,128)(2,1)S(1)} %get-tuple-element.58), channel_id=1, source_target_pairs={{0,16},{16,0},{1,17},{17,1},{2,18},{18,2},{3,19},{19,3},{4,20},{20... | collective-permute-start | bytes 1179656 | tf_op jit(solution)/shard_map/ppermute | solution.py:396
  6.4 3.1 %shard_map.93 = (bf16[12,128,128]{2,1,0:T(8,128)(2,1)S(1)}, s32[48]{0:T(128)S(1)}, s32[16,128]{1,0:T(8,128)S(1)}, f32[48,128,128]{2,1,0:T(8,128)S(1)}) custom-call(s32[16,96]{1,0:T(8,128)} %refs_0_.3, s32[96]{0:T(128)S(1)} %get-tuple-element.49.refs_1_.refs_0_, bf16[48,256,128]{2,1,0:T(8,128)(2,1)S(1)} %get-tuple-element.50.refs_2_.refs_1_, ...), custom_call_target="tpu_custom_call" | custom-call | flops 6000000 | bytes 2097152 | tf_op jit(solution)/shard_map/pallas_call | solution.py:375
  9.6 2.4 %shard_map.95 = (bf16[12,128,128]{2,1,0:T(8,128)(2,1)S(1)}, f32[48,128,128]{2,1,0:T(8,128)S(1)}) custom-call(s32[96]{0:T(128)S(1)} %get-tuple-element.49.refs_1_.refs_0_, bf16[48,256,128]{2,1,0:T(8,128)(2,1)S(1)} %get-tuple-element.50.refs_2_.refs_1_, f32[48,128,128]{2,1,0:T(8,128)} %bitcast.15), custom_call_target="tpu_custom_call" | custom-call | flops 6000000 | bytes 2097152 | tf_op jit(solution)/shard_map/pallas_call | solution.py:375
  12.0 2.1 %collective-permute-start = (bf16[12,128,128]{2,1,0:T(8,128)(2,1)S(1)}, bf16[12,128,128]{2,1,0:T(8,128)(2,1)S(1)}, u32[]{:S(2)}, u32[]{:S(2)}) collective-permute-start(bf16[12,128,128]{2,1,0:T(8,128)(2,1)S(1)} %get-tuple-element.55), channel_id=1, source_target_pairs={{0,16},{16,0},{1,17},{17,1},{2,18},{18,2},{3,19},{19,3},{4,20},{20... | collective-permute-start | bytes 1179656 | tf_op jit(solution)/shard_map/ppermute | solution.py:396
  14.1 2.4 %shard_map.94 = (bf16[12,128,128]{2,1,0:T(8,128)(2,1)S(1)}, f32[48,128,128]{2,1,0:T(8,128)S(1)}) custom-call(s32[96]{0:T(128)S(1)} %get-tuple-element.49.refs_1_.refs_0_, bf16[48,256,128]{2,1,0:T(8,128)(2,1)S(1)} %get-tuple-element.50.refs_2_.refs_1_, f32[48,128,128]{2,1,0:T(8,128)} %bitcast.16), custom_call_target="tpu_custom_call" | custom-call | flops 6000000 | bytes 2097152 | tf_op jit(solution)/shard_map/pallas_call | solution.py:375
  18.2 6.6 %collective-permute-done.2.refs_5_ = bf16[12,128,128]{2,1,0:T(8,128)(2,1)S(1)} collective-permute-done((bf16[12,128,128]{2,1,0:T(8,128)(2,1)S(1)}, bf16[12,128,128]{2,1,0:T(8,128)(2,1)S(1)}, u32[]{:S(2)}, u32[]{:S(2)}) %collective-permute-start.2) | collective-permute-done | bytes 393248 | tf_op jit(solution)/shard_map/ppermute | solution.py:396
  26.4 2.1 %collective-permute-start.10 = (bf16[392,128]{1,0:T(8,128)(2,1)S(1)}, bf16[392,128]{1,0:T(8,128)(2,1)S(1)}, u32[]{:S(2)}, u32[]{:S(2)}) collective-permute-start(bf16[392,128]{1,0:T(8,128)(2,1)S(1)} %get-tuple-element.78), channel_id=1, source_target_pairs={{0,4},{1,5},{2,6},{3,7},{4,0},{5,1},{6,2},{7,3},{8,12},{9,13},{10,... | collective-permute-start | bytes 301064 | tf_op jit(solution)/shard_map/ppermute | solution.py:423
  29.9 3.3 %collective-permute-done.refs_5_ = bf16[12,128,128]{2,1,0:T(8,128)(2,1)S(1)} collective-permute-done((bf16[12,128,128]{2,1,0:T(8,128)(2,1)S(1)}, bf16[12,128,128]{2,1,0:T(8,128)(2,1)S(1)}, u32[]{:S(2)}, u32[]{:S(2)}) %collective-permute-start) | collective-permute-done | bytes 393248 | tf_op jit(solution)/shard_map/ppermute | solution.py:396
  33.2 4.1 %collective-permute-start.6 = (bf16[392,128]{1,0:T(8,128)(2,1)S(1)}, bf16[392,128]{1,0:T(8,128)(2,1)S(1)}, u32[]{:S(2)}, u32[]{:S(2)}) collective-permute-start(bf16[392,128]{1,0:T(8,128)(2,1)S(1)} %get-tuple-element.74), channel_id=1, source_target_pairs={{0,12},{1,13},{2,14},{3,15},{4,8},{5,9},{6,10},{7,11},{8,4},{9,5},... | collective-permute-start | bytes 301064 | tf_op jit(solution)/shard_map/ppermute | solution.py:423
  37.3 3.5 %collective-permute-done.1.refs_5_ = bf16[12,128,128]{2,1,0:T(8,128)(2,1)S(1)} collective-permute-done((bf16[12,128,128]{2,1,0:T(8,128)(2,1)S(1)}, bf16[12,128,128]{2,1,0:T(8,128)(2,1)S(1)}, u32[]{:S(2)}, u32[]{:S(2)}) %collective-permute-start.1) | collective-permute-done | bytes 393248 | tf_op jit(solution)/shard_map/ppermute | solution.py:396
  40.8 2.4 %collective-permute-start.7 = (bf16[392,128]{1,0:T(8,128)(2,1)S(1)}, bf16[392,128]{1,0:T(8,128)(2,1)S(1)}, u32[]{:S(2)}, u32[]{:S(2)}) collective-permute-start(bf16[392,128]{1,0:T(8,128)(2,1)S(1)} %get-tuple-element.75), channel_id=1, source_target_pairs={{0,13},{1,12},{2,15},{3,14},{4,9},{5,8},{6,11},{7,10},{8,5},{9,4},... | collective-permute-start | bytes 301064 | tf_op jit(solution)/shard_map/ppermute | solution.py:423
  43.2 2.3 %collective-permute-start.8 = (bf16[392,128]{1,0:T(8,128)(2,1)S(1)}, bf16[392,128]{1,0:T(8,128)(2,1)S(1)}, u32[]{:S(2)}, u32[]{:S(2)}) collective-permute-start(bf16[392,128]{1,0:T(8,128)(2,1)S(1)} %get-tuple-element.76), channel_id=1, source_target_pairs={{0,14},{1,15},{2,12},{3,13},{4,10},{5,11},{6,8},{7,9},{8,6},{9,7},... | collective-permute-start | bytes 301064 | tf_op jit(solution)/shard_map/ppermute | solution.py:423
  45.5 3.2 %collective-permute-start.9 = (bf16[392,128]{1,0:T(8,128)(2,1)S(1)}, bf16[392,128]{1,0:T(8,128)(2,1)S(1)}, u32[]{:S(2)}, u32[]{:S(2)}) collective-permute-start(bf16[392,128]{1,0:T(8,128)(2,1)S(1)} %get-tuple-element.77), channel_id=1, source_target_pairs={{0,15},{1,14},{2,13},{3,12},{4,11},{5,10},{6,9},{7,8},{8,7},{9,6},... | collective-permute-start | bytes 301064 | tf_op jit(solution)/shard_map/ppermute | solution.py:423
  53.6 4.8 %collective-permute-start.15 = (bf16[392,128]{1,0:T(8,128)(2,1)S(1)}, bf16[392,128]{1,0:T(8,128)(2,1)S(1)}, u32[]{:S(2)}, u32[]{:S(2)}) collective-permute-start(bf16[392,128]{1,0:T(8,128)(2,1)S(1)} %get-tuple-element.83), channel_id=1, source_target_pairs={{0,9},{1,8},{2,11},{3,10},{4,13},{5,12},{6,15},{7,14},{8,1},{9,0},... | collective-permute-start | bytes 301064 | tf_op jit(solution)/shard_map/ppermute | solution.py:423
  58.4 2.5 %collective-permute-start.16 = (bf16[392,128]{1,0:T(8,128)(2,1)S(1)}, bf16[392,128]{1,0:T(8,128)(2,1)S(1)}, u32[]{:S(2)}, u32[]{:S(2)}) collective-permute-start(bf16[392,128]{1,0:T(8,128)(2,1)S(1)} %get-tuple-element.84), channel_id=1, source_target_pairs={{0,10},{1,11},{2,8},{3,9},{4,14},{5,15},{6,12},{7,13},{8,2},{9,3},... | collective-permute-start | bytes 301064 | tf_op jit(solution)/shard_map/ppermute | solution.py:423
  64.6 6.1 %collective-permute-done.16.refs_12_.refs_0_.refs_11_ = bf16[392,128]{1,0:T(8,128)(2,1)S(1)} collective-permute-done((bf16[392,128]{1,0:T(8,128)(2,1)S(1)}, bf16[392,128]{1,0:T(8,128)(2,1)S(1)}, u32[]{:S(2)}, u32[]{:S(2)}) %collective-permute-start.16) | collective-permute-done | bytes 100384 | tf_op jit(solution)/shard_map/ppermute | solution.py:423
  70.7 1.9 %collective-permute-done.17.refs_13_.refs_1_.refs_12_ = bf16[392,128]{1,0:T(8,128)(2,1)S(1)} collective-permute-done((bf16[392,128]{1,0:T(8,128)(2,1)S(1)}, bf16[392,128]{1,0:T(8,128)(2,1)S(1)}, u32[]{:S(2)}, u32[]{:S(2)}) %collective-permute-start.17) | collective-permute-done | bytes 100384 | tf_op jit(solution)/shard_map/ppermute | solution.py:423
  75.1 2.1 %collective-permute-done.14.refs_10_.refs_0_.refs_9_ = bf16[392,128]{1,0:T(8,128)(2,1)S(1)} collective-permute-done((bf16[392,128]{1,0:T(8,128)(2,1)S(1)}, bf16[392,128]{1,0:T(8,128)(2,1)S(1)}, u32[]{:S(2)}, u32[]{:S(2)}) %collective-permute-start.14) | collective-permute-done | bytes 100384 | tf_op jit(solution)/shard_map/ppermute | solution.py:423
  82.6 1.7 %shard_map.101 = f32[48,128,128]{2,1,0:T(8,128)} custom-call(f32[48,128,128]{2,1,0:T(8,128)S(1)} %get-tuple-element.69.held), custom_call_target="tpu_custom_call" | custom-call | flops 2000000 | bytes 2097152 | tf_op jit(solution)/shard_map/pallas_call | solution.py:465
  84.3 1.7 %shard_map.102 = f32[48,128,128]{2,1,0:T(8,128)} custom-call(f32[48,128,128]{2,1,0:T(8,128)S(1)} %get-tuple-element.70.held), custom_call_target="tpu_custom_call" | custom-call | flops 2000000 | bytes 2097152 | tf_op jit(solution)/shard_map/pallas_call | solution.py:465
  86.0 2.4 %shard_map.109.refs_9_ = bf16[96,128,128]{2,1,0:T(8,128)(2,1)} custom-call(s32[16,128]{1,0:T(8,128)S(1)} %get-tuple-element.71.refs_0_, bf16[392,128]{1,0:T(8,128)(2,1)S(1)} %collective-permute-done.6.refs_2_.refs_0_.refs_1_, bf16[392,128]{1,0:T(8,128)(2,1)S(1)} %collective-permute-done.7.refs_3_.refs_1_.refs_2_, ...), custom_call_target="tpu_custom_call" | custom-call | flops 5000000 | bytes 2097152 | tf_op jit(solution)/shard_map/pallas_call | solution.py:487
  88.4 2.2 %collective-permute-done.24.refs_8_ = bf16[8,128]{1,0:T(8,128)(2,1)S(1)} collective-permute-done((bf16[8,128]{1,0:T(8,128)(2,1)S(1)}, bf16[8,128]{1,0:T(8,128)(2,1)S(1)}, u32[]{:S(2)}, u32[]{:S(2)}) %collective-permute-start.24) | collective-permute-done | bytes 2080 | tf_op jit(solution)/shard_map/ppermute | solution.py:451
  92.2 2.0 %shard_map.110 = (bf16[96,128,128]{2,1,0:T(8,128)(2,1)}, f32[1,128]{1,0:T(1,128)S(1)}) custom-call(s32[16,128]{1,0:T(8,128)S(1)} %get-tuple-element.71.refs_0_, bf16[392,128]{1,0:T(8,128)(2,1)S(1)} %collective-permute-done.4.refs_0_.refs_16_.refs_1_, ...), custom_call_target="tpu_custom_call", output_to_operand_aliasing={{0}: (9, {})} | custom-call | flops 5000000 | bytes 2097152 | tf_op jit(solution)/shard_map/pallas_call | solution.py:487
  (52 shorter events, 26.1 us)
Async XLA Ops:
  3.3 13.3 %collective-permute-start.3 = (bf16[12,128,128]{2,1,0:T(8,128)(2,1)S(1)}, bf16[12,128,128]{2,1,0:T(8,128)(2,1)S(1)}, u32[]{:S(2)}, u32[]{:S(2)}) collective-permute-start(bf16[12,128,128]{2,1,0:T(8,128)(2,1)S(1)} %get-tuple-element.58), channel_id=1, source_target_pairs={{0,16},{16,0},{1,17},{17,1},{2,18},{18,2},{3,19},{19,3},{4,20},{20... | collective-permute-start | bytes 1179656 | tf_op jit(solution)/shard_map/ppermute | solution.py:396
  9.5 15.3 %collective-permute-start.2 = (bf16[12,128,128]{2,1,0:T(8,128)(2,1)S(1)}, bf16[12,128,128]{2,1,0:T(8,128)(2,1)S(1)}, u32[]{:S(2)}, u32[]{:S(2)}) collective-permute-start(bf16[12,128,128]{2,1,0:T(8,128)(2,1)S(1)} %get-tuple-element.57), channel_id=1, source_target_pairs={{0,16},{16,0},{1,17},{17,1},{2,18},{18,2},{3,19},{19,3},{4,20},{20... | collective-permute-start | bytes 1179656 | tf_op jit(solution)/shard_map/ppermute | solution.py:396
  12.0 21.2 %collective-permute-start = (bf16[12,128,128]{2,1,0:T(8,128)(2,1)S(1)}, bf16[12,128,128]{2,1,0:T(8,128)(2,1)S(1)}, u32[]{:S(2)}, u32[]{:S(2)}) collective-permute-start(bf16[12,128,128]{2,1,0:T(8,128)(2,1)S(1)} %get-tuple-element.55), channel_id=1, source_target_pairs={{0,16},{16,0},{1,17},{17,1},{2,18},{18,2},{3,19},{19,3},{4,20},{20... | collective-permute-start | bytes 1179656 | tf_op jit(solution)/shard_map/ppermute | solution.py:396
  16.5 24.3 %collective-permute-start.1 = (bf16[12,128,128]{2,1,0:T(8,128)(2,1)S(1)}, bf16[12,128,128]{2,1,0:T(8,128)(2,1)S(1)}, u32[]{:S(2)}, u32[]{:S(2)}) collective-permute-start(bf16[12,128,128]{2,1,0:T(8,128)(2,1)S(1)} %get-tuple-element.56), channel_id=1, source_target_pairs={{0,16},{16,0},{1,17},{17,1},{2,18},{18,2},{3,19},{19,3},{4,20},{20... | collective-permute-start | bytes 1179656 | tf_op jit(solution)/shard_map/ppermute | solution.py:396
  26.4 16.8 %collective-permute-start.10 = (bf16[392,128]{1,0:T(8,128)(2,1)S(1)}, bf16[392,128]{1,0:T(8,128)(2,1)S(1)}, u32[]{:S(2)}, u32[]{:S(2)}) collective-permute-start(bf16[392,128]{1,0:T(8,128)(2,1)S(1)} %get-tuple-element.78), channel_id=1, source_target_pairs={{0,4},{1,5},{2,6},{3,7},{4,0},{5,1},{6,2},{7,3},{8,12},{9,13},{10,... | collective-permute-start | bytes 301064 | tf_op jit(solution)/shard_map/ppermute | solution.py:423
  28.5 17.0 %collective-permute-start.11 = (bf16[392,128]{1,0:T(8,128)(2,1)S(1)}, bf16[392,128]{1,0:T(8,128)(2,1)S(1)}, u32[]{:S(2)}, u32[]{:S(2)}) collective-permute-start(bf16[392,128]{1,0:T(8,128)(2,1)S(1)} %get-tuple-element.79), channel_id=1, source_target_pairs={{0,5},{1,4},{2,7},{3,6},{4,1},{5,0},{6,3},{7,2},{8,13},{9,12},{10,... | collective-permute-start | bytes 301064 | tf_op jit(solution)/shard_map/ppermute | solution.py:423
  28.5 20.2 %collective-permute-start.12 = (bf16[392,128]{1,0:T(8,128)(2,1)S(1)}, bf16[392,128]{1,0:T(8,128)(2,1)S(1)}, u32[]{:S(2)}, u32[]{:S(2)}) collective-permute-start(bf16[392,128]{1,0:T(8,128)(2,1)S(1)} %get-tuple-element.80), channel_id=1, source_target_pairs={{0,6},{1,7},{2,4},{3,5},{4,2},{5,3},{6,0},{7,1},{8,14},{9,15},{10,... | collective-permute-start | bytes 301064 | tf_op jit(solution)/shard_map/ppermute | solution.py:423
  33.2 18.8 %collective-permute-start.6 = (bf16[392,128]{1,0:T(8,128)(2,1)S(1)}, bf16[392,128]{1,0:T(8,128)(2,1)S(1)}, u32[]{:S(2)}, u32[]{:S(2)}) collective-permute-start(bf16[392,128]{1,0:T(8,128)(2,1)S(1)} %get-tuple-element.74), channel_id=1, source_target_pairs={{0,12},{1,13},{2,14},{3,15},{4,8},{5,9},{6,10},{7,11},{8,4},{9,5},... | collective-permute-start | bytes 301064 | tf_op jit(solution)/shard_map/ppermute | solution.py:423
  40.8 12.8 %collective-permute-start.7 = (bf16[392,128]{1,0:T(8,128)(2,1)S(1)}, bf16[392,128]{1,0:T(8,128)(2,1)S(1)}, u32[]{:S(2)}, u32[]{:S(2)}) collective-permute-start(bf16[392,128]{1,0:T(8,128)(2,1)S(1)} %get-tuple-element.75), channel_id=1, source_target_pairs={{0,13},{1,12},{2,15},{3,14},{4,9},{5,8},{6,11},{7,10},{8,5},{9,4},... | collective-permute-start | bytes 301064 | tf_op jit(solution)/shard_map/ppermute | solution.py:423
  43.2 10.4 %collective-permute-start.8 = (bf16[392,128]{1,0:T(8,128)(2,1)S(1)}, bf16[392,128]{1,0:T(8,128)(2,1)S(1)}, u32[]{:S(2)}, u32[]{:S(2)}) collective-permute-start(bf16[392,128]{1,0:T(8,128)(2,1)S(1)} %get-tuple-element.76), channel_id=1, source_target_pairs={{0,14},{1,15},{2,12},{3,13},{4,10},{5,11},{6,8},{7,9},{8,6},{9,7},... | collective-permute-start | bytes 301064 | tf_op jit(solution)/shard_map/ppermute | solution.py:423
  45.5 12.8 %collective-permute-start.9 = (bf16[392,128]{1,0:T(8,128)(2,1)S(1)}, bf16[392,128]{1,0:T(8,128)(2,1)S(1)}, u32[]{:S(2)}, u32[]{:S(2)}) collective-permute-start(bf16[392,128]{1,0:T(8,128)(2,1)S(1)} %get-tuple-element.77), channel_id=1, source_target_pairs={{0,15},{1,14},{2,13},{3,12},{4,11},{5,10},{6,9},{7,8},{8,7},{9,6},... | collective-permute-start | bytes 301064 | tf_op jit(solution)/shard_map/ppermute | solution.py:423
  48.8 12.2 %collective-permute-start.13 = (bf16[392,128]{1,0:T(8,128)(2,1)S(1)}, bf16[392,128]{1,0:T(8,128)(2,1)S(1)}, u32[]{:S(2)}, u32[]{:S(2)}) collective-permute-start(bf16[392,128]{1,0:T(8,128)(2,1)S(1)} %get-tuple-element.81), channel_id=1, source_target_pairs={{0,7},{1,6},{2,5},{3,4},{4,3},{5,2},{6,1},{7,0},{8,15},{9,14},{10,... | collective-permute-start | bytes 301064 | tf_op jit(solution)/shard_map/ppermute | solution.py:423
  52.0 10.6 %collective-permute-start.25 = (bf16[384,128]{1,0:T(8,128)(2,1)S(1)}, bf16[384,128]{1,0:T(8,128)(2,1)S(1)}, u32[]{:S(2)}, u32[]{:S(2)}) collective-permute-start(bf16[384,128]{1,0:T(8,128)(2,1)S(1)} %get-tuple-element.90.refs_13_), channel_id=1, source_target_pairs={{0,16},{16,0},{1,17},{17,1},{2,18},{18,2},{3,19},{19,3},{4,20},{20... | collective-permute-start | bytes 294920 | tf_op jit(solution)/shard_map/ppermute | solution.py:436
  53.6 9.5 %collective-permute-start.18 = (bf16[392,128]{1,0:T(8,128)(2,1)S(1)}, bf16[392,128]{1,0:T(8,128)(2,1)S(1)}, u32[]{:S(2)}, u32[]{:S(2)}) collective-permute-start(bf16[392,128]{1,0:T(8,128)(2,1)S(1)} %get-tuple-element.87), channel_id=1, source_target_pairs={{0,1},{1,0},{2,3},{3,2},{4,5},{5,4},{6,7},{7,6},{8,9},{9,8},{10,11... | collective-permute-start | bytes 301064 | tf_op jit(solution)/shard_map/ppermute | solution.py:423
  53.6 9.5 %collective-permute-start.15 = (bf16[392,128]{1,0:T(8,128)(2,1)S(1)}, bf16[392,128]{1,0:T(8,128)(2,1)S(1)}, u32[]{:S(2)}, u32[]{:S(2)}) collective-permute-start(bf16[392,128]{1,0:T(8,128)(2,1)S(1)} %get-tuple-element.83), channel_id=1, source_target_pairs={{0,9},{1,8},{2,11},{3,10},{4,13},{5,12},{6,15},{7,14},{8,1},{9,0},... | collective-permute-start | bytes 301064 | tf_op jit(solution)/shard_map/ppermute | solution.py:423
  58.4 12.3 %collective-permute-start.16 = (bf16[392,128]{1,0:T(8,128)(2,1)S(1)}, bf16[392,128]{1,0:T(8,128)(2,1)S(1)}, u32[]{:S(2)}, u32[]{:S(2)}) collective-permute-start(bf16[392,128]{1,0:T(8,128)(2,1)S(1)} %get-tuple-element.84), channel_id=1, source_target_pairs={{0,10},{1,11},{2,8},{3,9},{4,14},{5,15},{6,12},{7,13},{8,2},{9,3},... | collective-permute-start | bytes 301064 | tf_op jit(solution)/shard_map/ppermute | solution.py:423
  60.9 18.4 %collective-permute-start.26 = (bf16[1536,128]{1,0:T(8,128)(2,1)S(1)}, bf16[1536,128]{1,0:T(8,128)(2,1)S(1)}, u32[]{:S(2)}, u32[]{:S(2)}) collective-permute-start(bf16[1536,128]{1,0:T(8,128)(2,1)S(1)} %shard_map.108), channel_id=1, source_target_pairs={{0,16},{16,0},{1,17},{17,1},{2,18},{18,2},{3,19},{19,3},{4,20},{20... | collective-permute-start | bytes 1179656 | tf_op jit(solution)/shard_map/ppermute | solution.py:452
  62.6 29.6 %collective-permute-start.20 = (bf16[1536,128]{1,0:T(8,128)(2,1)S(1)}, bf16[1536,128]{1,0:T(8,128)(2,1)S(1)}, u32[]{:S(2)}, u32[]{:S(2)}) collective-permute-start(bf16[1536,128]{1,0:T(8,128)(2,1)S(1)} %shard_map.104), channel_id=1, source_target_pairs={{0,16},{16,0},{1,17},{17,1},{2,18},{18,2},{3,19},{19,3},{4,20},{20... | collective-permute-start | bytes 1179656 | tf_op jit(solution)/shard_map/ppermute | solution.py:452
  63.1 9.5 %collective-permute-start.17 = (bf16[392,128]{1,0:T(8,128)(2,1)S(1)}, bf16[392,128]{1,0:T(8,128)(2,1)S(1)}, u32[]{:S(2)}, u32[]{:S(2)}) collective-permute-start(bf16[392,128]{1,0:T(8,128)(2,1)S(1)} %get-tuple-element.85), channel_id=1, source_target_pairs={{0,11},{1,10},{2,9},{3,8},{4,15},{5,14},{6,13},{7,12},{8,3},{9,2},... | collective-permute-start | bytes 301064 | tf_op jit(solution)/shard_map/ppermute | solution.py:423
  63.1 10.3 %collective-permute-start.4 = (bf16[392,128]{1,0:T(8,128)(2,1)S(1)}, bf16[392,128]{1,0:T(8,128)(2,1)S(1)}, u32[]{:S(2)}, u32[]{:S(2)}) collective-permute-start(bf16[392,128]{1,0:T(8,128)(2,1)S(1)} %get-tuple-element.72), channel_id=1, source_target_pairs={{0,2},{1,3},{2,0},{3,1},{4,6},{5,7},{6,4},{7,5},{8,10},{9,11},{10,... | collective-permute-start | bytes 301064 | tf_op jit(solution)/shard_map/ppermute | solution.py:423
  73.5 18.7 %collective-permute-start.22 = (bf16[768,128]{1,0:T(8,128)(2,1)S(1)}, bf16[768,128]{1,0:T(8,128)(2,1)S(1)}, u32[]{:S(2)}, u32[]{:S(2)}) collective-permute-start(bf16[768,128]{1,0:T(8,128)(2,1)S(1)} %shard_map.106), channel_id=1, source_target_pairs={{0,16},{16,0},{1,17},{17,1},{2,18},{18,2},{3,19},{19,3},{4,20},{20... | collective-permute-start | bytes 589832 | tf_op jit(solution)/shard_map/ppermute | solution.py:452
  77.1 15.0 %collective-permute-start.23 = (bf16[768,128]{1,0:T(8,128)(2,1)S(1)}, bf16[768,128]{1,0:T(8,128)(2,1)S(1)}, u32[]{:S(2)}, u32[]{:S(2)}) collective-permute-start(bf16[768,128]{1,0:T(8,128)(2,1)S(1)} %shard_map.107), channel_id=1, source_target_pairs={{0,16},{16,0},{1,17},{17,1},{2,18},{18,2},{3,19},{19,3},{4,20},{20... | collective-permute-start | bytes 589832 | tf_op jit(solution)/shard_map/ppermute | solution.py:452
  78.7 13.5 %collective-permute-start.21 = (bf16[384,128]{1,0:T(8,128)(2,1)S(1)}, bf16[384,128]{1,0:T(8,128)(2,1)S(1)}, u32[]{:S(2)}, u32[]{:S(2)}) collective-permute-start(bf16[384,128]{1,0:T(8,128)(2,1)S(1)} %shard_map.105), channel_id=1, source_target_pairs={{0,16},{16,0},{1,17},{17,1},{2,18},{18,2},{3,19},{19,3},{4,20},{20... | collective-permute-start | bytes 294920 | tf_op jit(solution)/shard_map/ppermute | solution.py:452
  79.3 11.4 %collective-permute-start.24 = (bf16[8,128]{1,0:T(8,128)(2,1)S(1)}, bf16[8,128]{1,0:T(8,128)(2,1)S(1)}, u32[]{:S(2)}, u32[]{:S(2)}) collective-permute-start(bf16[8,128]{1,0:T(8,128)(2,1)S(1)} %get-tuple-element.89.refs_7_), channel_id=1, source_target_pairs={{0,16},{16,0},{1,17},{17,1},{2,18},{18,2},{3,19},{19,3},{4,20},{20... | collective-permute-start | bytes 6152 | tf_op jit(solution)/shard_map/ppermute | solution.py:451
  (3 other events, 18.2 us)

commit v5 on v4

--- a/solution.py
+++ b/solution.py
@@ -13,7 +13,8 @@
 UNROLL = 2
 SPLIT = 4
 MERGES = (
-    ((3, 0), (3, 1), (3, 2), (3, 3)),
+    ((3, 0), (3, 1)),
+    ((3, 2), (3, 3)),
     ((1, 0), (1, 1), (1, 2), (1, 3)),
     ((2, 0),),
     ((2, 1), (0, 1)),
@@ -451,7 +452,7 @@
                 tails = [merged[1], lax.ppermute(merged[1], "dp", cycles[1])]
             passed = lax.ppermute(merged[0], "dp", cycles[1])
             entries.append(([(k, q, 1, j) for j, (k, q) in enumerate(keys)], passed))
-            stage.append(2 if n == len(merges) - 1 else int(n > 0 and len(merges) > 1))
+            stage.append(2 if n == len(merges) - 1 else int(n > len(merges) - 5 and len(merges) > 1))
     else:
         keys = [(k, q) for k in plan.chunks for q in range(plan.near)]
         stacked = jnp.stack([block for k in plan.chunks for block in groups[k]])

time: 98 us -> 111 us (1.13)
  starting transfers between devices: 41 us -> 49.8 us
  waiting for transfers between devices: 27.3 us -> 31.5 us
    ppermute x15, starting transfers between devices: 25.2 us -> 35.6 us  [per_device(): block = lax.ppermute(block, 'shard', plan.pattern(k, q))]
    ppermute x4, waiting for transfers between devices: 13.3 us -> 19.3 us  [per_device(): arrived.setdefault(k, []).append(lax.ppermute(packed, 'dp', cycles[s]))]
    ppermute x15, waiting for transfers between devices: 10.2 us -> 4.32 us  [per_device(): block = lax.ppermute(block, 'shard', plan.pattern(k, q))]
    ppermute x6 -> x7, waiting for transfers between devices: 1.56 us -> 7.08 us  [per_device(): passed = lax.ppermute(merged[0], 'dp', cycles[1])]
    ppermute x1, waiting for transfers between devices: 2.24 us -> 0.73 us  [per_device(): tails = [merged[1], lax.ppermute(merged[1], 'dp', cycles[1])]]
    ppermute x1, starting transfers between devices: 1.58 us -> 0.33 us  [per_device(): tails = [merged[1], lax.ppermute(merged[1], 'dp', cycles[1])]]
    ppermute x6 -> x7, starting transfers between devices: 7.35 us -> 7.13 us  [per_device(): passed = lax.ppermute(merged[0], 'dp', cycles[1])]
  transfers between devices with their start and end apart: 27 -> 28, of which waited for: 8 -> 11; matrix products, arithmetic and copies ran while one was open for 1% -> 0% of each run, Pallas kernels for 25% -> 20%
where the time goes in v5:
time: 111 us
  starting transfers between devices  49.8 us (45%)
  waiting for transfers between devices  31.5 us (28%)
  Pallas kernels  28.1 us (25%)
    ppermute x15, starting transfers between devices, per_device(): block = lax.ppermute(block, 'shard', plan.pattern(k, q))  35.6 us
    ppermute x4, waiting for transfers between devices, per_device(): arrived.setdefault(k, []).append(lax.ppermute(packed, 'dp', cycles[s]))  19.3 us
    pallas_call x4, Pallas kernels, per_device(): pl.pallas_call(functools.partial(pack_kernel, plan, k, s, lead, own, load...  10.6 us
    ppermute x7, starting transfers between devices, per_device(): passed = lax.ppermute(merged[0], 'dp', cycles[1])  7.13 us
    ppermute x7, waiting for transfers between devices, per_device(): passed = lax.ppermute(merged[0], 'dp', cycles[1])  7.08 us
    pallas_call x4, Pallas kernels, per_device(): pl.pallas_call(functools.partial(adam_kernel, plan, k, not news), out_sha...  6.41 us
    pallas_call x3, Pallas kernels, place(): pl.pallas_call(functools.partial(place_kernel, plan, sources, len(group),...  5.89 us
    ppermute x4, starting transfers between devices, per_device(): arrived.setdefault(k, []).append(lax.ppermute(packed, 'dp', cycles[s]))  5.3 us
  transfers between devices with their start and end apart: 28, of which 11 were waited for; matrix products, arithmetic and copies ran while one was open for 0% of the time, Pallas kernels for 20%

profile of v5, /device:TPU:0, one launch (start us, length us, event | category | flops | bytes accessed | tf_op | source)
XLA Modules:
  0.0 110.8 jit_solution(13158488011640001559)
XLA Ops:
  0.6 2.7 %shard_map.92 = (s32[96]{0:T(128)S(1)}, bf16[12,128,128]{2,1,0:T(8,128)(2,1)S(1)}, bf16[48,256,128]{2,1,0:T(8,128)(2,1)S(1)}) custom-call(s32[16,96]{1,0:T(8,128)} %refs_0_.3, bf16[48,256,128]{2,1,0:T(8,128)(2,1)} %bitcast.13), custom_call_target="tpu_custom_call" | custom-call | flops 6000000 | bytes 2097152 | tf_op jit(solution)/shard_map/pallas_call | solution.py:376
  3.3 3.1 %collective-permute-start.3 = (bf16[12,128,128]{2,1,0:T(8,128)(2,1)S(1)}, bf16[12,128,128]{2,1,0:T(8,128)(2,1)S(1)}, u32[]{:S(2)}, u32[]{:S(2)}) collective-permute-start(bf16[12,128,128]{2,1,0:T(8,128)(2,1)S(1)} %get-tuple-element.58), channel_id=1, source_target_pairs={{0,16},{16,0},{1,17},{17,1},{2,18},{18,2},{3,19},{19,3},{4,20},{20... | collective-permute-start | bytes 1179656 | tf_op jit(solution)/shard_map/ppermute | solution.py:397
  6.4 3.1 %shard_map.93 = (bf16[12,128,128]{2,1,0:T(8,128)(2,1)S(1)}, s32[48]{0:T(128)S(1)}, s32[16,128]{1,0:T(8,128)S(1)}, f32[48,128,128]{2,1,0:T(8,128)S(1)}) custom-call(s32[16,96]{1,0:T(8,128)} %refs_0_.3, s32[96]{0:T(128)S(1)} %get-tuple-element.49.refs_1_.refs_0_, bf16[48,256,128]{2,1,0:T(8,128)(2,1)S(1)} %get-tuple-element.50.refs_2_.refs_1_, ...), custom_call_target="tpu_custom_call" | custom-call | flops 6000000 | bytes 2097152 | tf_op jit(solution)/shard_map/pallas_call | solution.py:376
  9.6 2.4 %shard_map.94 = (bf16[12,128,128]{2,1,0:T(8,128)(2,1)S(1)}, f32[48,128,128]{2,1,0:T(8,128)S(1)}) custom-call(s32[96]{0:T(128)S(1)} %get-tuple-element.49.refs_1_.refs_0_, bf16[48,256,128]{2,1,0:T(8,128)(2,1)S(1)} %get-tuple-element.50.refs_2_.refs_1_, f32[48,128,128]{2,1,0:T(8,128)} %bitcast.15), custom_call_target="tpu_custom_call" | custom-call | flops 6000000 | bytes 2097152 | tf_op jit(solution)/shard_map/pallas_call | solution.py:376
  12.0 2.1 %collective-permute-start.1 = (bf16[12,128,128]{2,1,0:T(8,128)(2,1)S(1)}, bf16[12,128,128]{2,1,0:T(8,128)(2,1)S(1)}, u32[]{:S(2)}, u32[]{:S(2)}) collective-permute-start(bf16[12,128,128]{2,1,0:T(8,128)(2,1)S(1)} %get-tuple-element.56), channel_id=1, source_target_pairs={{0,16},{16,0},{1,17},{17,1},{2,18},{18,2},{3,19},{19,3},{4,20},{20... | collective-permute-start | bytes 1179656 | tf_op jit(solution)/shard_map/ppermute | solution.py:397
  14.1 2.4 %shard_map.95 = (bf16[12,128,128]{2,1,0:T(8,128)(2,1)S(1)}, f32[48,128,128]{2,1,0:T(8,128)S(1)}) custom-call(s32[96]{0:T(128)S(1)} %get-tuple-element.49.refs_1_.refs_0_, bf16[48,256,128]{2,1,0:T(8,128)(2,1)S(1)} %get-tuple-element.50.refs_2_.refs_1_, f32[48,128,128]{2,1,0:T(8,128)} %bitcast.16), custom_call_target="tpu_custom_call" | custom-call | flops 6000000 | bytes 2097152 | tf_op jit(solution)/shard_map/pallas_call | solution.py:376
  18.2 6.6 %collective-permute-done.2.refs_5_ = bf16[12,128,128]{2,1,0:T(8,128)(2,1)S(1)} collective-permute-done((bf16[12,128,128]{2,1,0:T(8,128)(2,1)S(1)}, bf16[12,128,128]{2,1,0:T(8,128)(2,1)S(1)}, u32[]{:S(2)}, u32[]{:S(2)}) %collective-permute-start.2) | collective-permute-done | bytes 393248 | tf_op jit(solution)/shard_map/ppermute | solution.py:397
  26.4 6.8 %collective-permute-done.1.refs_5_ = bf16[12,128,128]{2,1,0:T(8,128)(2,1)S(1)} collective-permute-done((bf16[12,128,128]{2,1,0:T(8,128)(2,1)S(1)}, bf16[12,128,128]{2,1,0:T(8,128)(2,1)S(1)}, u32[]{:S(2)}, u32[]{:S(2)}) %collective-permute-start.1) | collective-permute-done | bytes 393248 | tf_op jit(solution)/shard_map/ppermute | solution.py:397
  34.8 6.0 %collective-permute-done.refs_5_ = bf16[12,128,128]{2,1,0:T(8,128)(2,1)S(1)} collective-permute-done((bf16[12,128,128]{2,1,0:T(8,128)(2,1)S(1)}, bf16[12,128,128]{2,1,0:T(8,128)(2,1)S(1)}, u32[]{:S(2)}, u32[]{:S(2)}) %collective-permute-start) | collective-permute-done | bytes 393248 | tf_op jit(solution)/shard_map/ppermute | solution.py:397
  42.4 1.8 %collective-permute-start.4 = (bf16[392,128]{1,0:T(8,128)(2,1)S(1)}, bf16[392,128]{1,0:T(8,128)(2,1)S(1)}, u32[]{:S(2)}, u32[]{:S(2)}) collective-permute-start(bf16[392,128]{1,0:T(8,128)(2,1)S(1)} %get-tuple-element.72), channel_id=1, source_target_pairs={{0,2},{1,3},{2,0},{3,1},{4,6},{5,7},{6,4},{7,5},{8,10},{9,11},{10,... | collective-permute-start | bytes 301064 | tf_op jit(solution)/shard_map/ppermute | solution.py:424
  45.7 2.7 %collective-permute-start.15 = (bf16[392,128]{1,0:T(8,128)(2,1)S(1)}, bf16[392,128]{1,0:T(8,128)(2,1)S(1)}, u32[]{:S(2)}, u32[]{:S(2)}) collective-permute-start(bf16[392,128]{1,0:T(8,128)(2,1)S(1)} %get-tuple-element.83), channel_id=1, source_target_pairs={{0,9},{1,8},{2,11},{3,10},{4,13},{5,12},{6,15},{7,14},{8,1},{9,0},... | collective-permute-start | bytes 301064 | tf_op jit(solution)/shard_map/ppermute | solution.py:424
  53.1 2.2 %collective-permute-start.16 = (bf16[392,128]{1,0:T(8,128)(2,1)S(1)}, bf16[392,128]{1,0:T(8,128)(2,1)S(1)}, u32[]{:S(2)}, u32[]{:S(2)}) collective-permute-start(bf16[392,128]{1,0:T(8,128)(2,1)S(1)} %get-tuple-element.84), channel_id=1, source_target_pairs={{0,10},{1,11},{2,8},{3,9},{4,14},{5,15},{6,12},{7,13},{8,2},{9,3},... | collective-permute-start | bytes 301064 | tf_op jit(solution)/shard_map/ppermute | solution.py:424
  55.3 2.1 %collective-permute-start.6 = (bf16[392,128]{1,0:T(8,128)(2,1)S(1)}, bf16[392,128]{1,0:T(8,128)(2,1)S(1)}, u32[]{:S(2)}, u32[]{:S(2)}) collective-permute-start(bf16[392,128]{1,0:T(8,128)(2,1)S(1)} %get-tuple-element.74), channel_id=1, source_target_pairs={{0,12},{1,13},{2,14},{3,15},{4,8},{5,9},{6,10},{7,11},{8,4},{9,5},... | collective-permute-start | bytes 301064 | tf_op jit(solution)/shard_map/ppermute | solution.py:424
  58.1 2.9 %collective-permute-done.12.refs_8_.refs_2_.refs_7_ = bf16[392,128]{1,0:T(8,128)(2,1)S(1)} collective-permute-done((bf16[392,128]{1,0:T(8,128)(2,1)S(1)}, bf16[392,128]{1,0:T(8,128)(2,1)S(1)}, u32[]{:S(2)}, u32[]{:S(2)}) %collective-permute-start.12) | collective-permute-done | bytes 100384 | tf_op jit(solution)/shard_map/ppermute | solution.py:424
  62.2 3.2 %collective-permute-start.9 = (bf16[392,128]{1,0:T(8,128)(2,1)S(1)}, bf16[392,128]{1,0:T(8,128)(2,1)S(1)}, u32[]{:S(2)}, u32[]{:S(2)}) collective-permute-start(bf16[392,128]{1,0:T(8,128)(2,1)S(1)} %get-tuple-element.77), channel_id=1, source_target_pairs={{0,15},{1,14},{2,13},{3,12},{4,11},{5,10},{6,9},{7,8},{8,7},{9,6},... | collective-permute-start | bytes 301064 | tf_op jit(solution)/shard_map/ppermute | solution.py:424
  66.5 8.3 %collective-permute-start.17 = (bf16[392,128]{1,0:T(8,128)(2,1)S(1)}, bf16[392,128]{1,0:T(8,128)(2,1)S(1)}, u32[]{:S(2)}, u32[]{:S(2)}) collective-permute-start(bf16[392,128]{1,0:T(8,128)(2,1)S(1)} %get-tuple-element.85), channel_id=1, source_target_pairs={{0,11},{1,10},{2,9},{3,8},{4,15},{5,14},{6,13},{7,12},{8,3},{9,2},... | collective-permute-start | bytes 301064 | tf_op jit(solution)/shard_map/ppermute | solution.py:424
  74.8 2.4 %collective-permute-start.5 = (bf16[392,128]{1,0:T(8,128)(2,1)S(1)}, bf16[392,128]{1,0:T(8,128)(2,1)S(1)}, u32[]{:S(2)}, u32[]{:S(2)}) collective-permute-start(bf16[392,128]{1,0:T(8,128)(2,1)S(1)} %get-tuple-element.73), channel_id=1, source_target_pairs={{0,3},{1,2},{2,1},{3,0},{4,7},{5,6},{6,5},{7,4},{8,11},{9,10},{10,... | collective-permute-start | bytes 301064 | tf_op jit(solution)/shard_map/ppermute | solution.py:424
  77.2 7.4 %collective-permute-start.14 = (bf16[392,128]{1,0:T(8,128)(2,1)S(1)}, bf16[392,128]{1,0:T(8,128)(2,1)S(1)}, u32[]{:S(2)}, u32[]{:S(2)}) collective-permute-start(bf16[392,128]{1,0:T(8,128)(2,1)S(1)} %get-tuple-element.82), channel_id=1, source_target_pairs={{0,8},{1,9},{2,10},{3,11},{4,12},{5,13},{6,14},{7,15},{8,0},{9,1},... | collective-permute-start | bytes 301064 | tf_op jit(solution)/shard_map/ppermute | solution.py:424
  89.0 2.2 %collective-permute-done.25.refs_16_ = bf16[768,128]{1,0:T(8,128)(2,1)S(1)} collective-permute-done((bf16[768,128]{1,0:T(8,128)(2,1)S(1)}, bf16[768,128]{1,0:T(8,128)(2,1)S(1)}, u32[]{:S(2)}, u32[]{:S(2)}) %collective-permute-start.25) | collective-permute-done | bytes 196640 | tf_op jit(solution)/shard_map/ppermute | solution.py:453
  91.5 3.8 %collective-permute-done.26.refs_17_ = bf16[768,128]{1,0:T(8,128)(2,1)S(1)} collective-permute-done((bf16[768,128]{1,0:T(8,128)(2,1)S(1)}, bf16[768,128]{1,0:T(8,128)(2,1)S(1)}, u32[]{:S(2)}, u32[]{:S(2)}) %collective-permute-start.26) | collective-permute-done | bytes 196640 | tf_op jit(solution)/shard_map/ppermute | solution.py:453
  99.1 1.7 %shard_map.102 = f32[48,128,128]{2,1,0:T(8,128)} custom-call(f32[48,128,128]{2,1,0:T(8,128)S(1)} %get-tuple-element.70.held), custom_call_target="tpu_custom_call" | custom-call | flops 2000000 | bytes 2097152 | tf_op jit(solution)/shard_map/pallas_call | solution.py:466
  100.8 1.8 %collective-permute-start.19 = (bf16[768,128]{1,0:T(8,128)(2,1)S(1)}, bf16[768,128]{1,0:T(8,128)(2,1)S(1)}, u32[]{:S(2)}, u32[]{:S(2)}) collective-permute-start(bf16[768,128]{1,0:T(8,128)(2,1)S(1)} %get-tuple-element.88), channel_id=1, source_target_pairs={{0,16},{16,0},{1,17},{17,1},{2,18},{18,2},{3,19},{19,3},{4,20},{20... | collective-permute-start | bytes 589832 | tf_op jit(solution)/shard_map/ppermute | solution.py:453
  102.6 2.6 %shard_map.110.refs_8_ = bf16[96,128,128]{2,1,0:T(8,128)(2,1)} custom-call(s32[16,128]{1,0:T(8,128)S(1)} %get-tuple-element.71.refs_0_, bf16[392,128]{1,0:T(8,128)(2,1)S(1)} %collective-permute-done.6.refs_2_.refs_0_.refs_1_, bf16[392,128]{1,0:T(8,128)(2,1)S(1)} %collective-permute-done.7.refs_3_.refs_1_.refs_2_, ...), custom_call_target="tpu_custom_call" | custom-call | flops 5000000 | bytes 2097152 | tf_op jit(solution)/shard_map/pallas_call | solution.py:488
  106.0 1.8 %shard_map.111 = (bf16[96,128,128]{2,1,0:T(8,128)(2,1)}, f32[1,128]{1,0:T(1,128)S(1)}) custom-call(s32[16,128]{1,0:T(8,128)S(1)} %get-tuple-element.71.refs_0_, bf16[392,128]{1,0:T(8,128)(2,1)S(1)} %collective-permute-done.4.refs_0_.refs_16_.refs_1_, ...), custom_call_target="tpu_custom_call", output_to_operand_aliasing={{0}: (8, {})} | custom-call | flops 5000000 | bytes 2097152 | tf_op jit(solution)/shard_map/pallas_call | solution.py:488
  (55 shorter events, 27.9 us)
Async XLA Ops:
  3.3 13.3 %collective-permute-start.3 = (bf16[12,128,128]{2,1,0:T(8,128)(2,1)S(1)}, bf16[12,128,128]{2,1,0:T(8,128)(2,1)S(1)}, u32[]{:S(2)}, u32[]{:S(2)}) collective-permute-start(bf16[12,128,128]{2,1,0:T(8,128)(2,1)S(1)} %get-tuple-element.58), channel_id=1, source_target_pairs={{0,16},{16,0},{1,17},{17,1},{2,18},{18,2},{3,19},{19,3},{4,20},{20... | collective-permute-start | bytes 1179656 | tf_op jit(solution)/shard_map/ppermute | solution.py:397
  9.5 15.3 %collective-permute-start.2 = (bf16[12,128,128]{2,1,0:T(8,128)(2,1)S(1)}, bf16[12,128,128]{2,1,0:T(8,128)(2,1)S(1)}, u32[]{:S(2)}, u32[]{:S(2)}) collective-permute-start(bf16[12,128,128]{2,1,0:T(8,128)(2,1)S(1)} %get-tuple-element.57), channel_id=1, source_target_pairs={{0,16},{16,0},{1,17},{17,1},{2,18},{18,2},{3,19},{19,3},{4,20},{20... | collective-permute-start | bytes 1179656 | tf_op jit(solution)/shard_map/ppermute | solution.py:397
  12.0 21.2 %collective-permute-start.1 = (bf16[12,128,128]{2,1,0:T(8,128)(2,1)S(1)}, bf16[12,128,128]{2,1,0:T(8,128)(2,1)S(1)}, u32[]{:S(2)}, u32[]{:S(2)}) collective-permute-start(bf16[12,128,128]{2,1,0:T(8,128)(2,1)S(1)} %get-tuple-element.56), channel_id=1, source_target_pairs={{0,16},{16,0},{1,17},{17,1},{2,18},{18,2},{3,19},{19,3},{4,20},{20... | collective-permute-start | bytes 1179656 | tf_op jit(solution)/shard_map/ppermute | solution.py:397
  16.5 24.3 %collective-permute-start = (bf16[12,128,128]{2,1,0:T(8,128)(2,1)S(1)}, bf16[12,128,128]{2,1,0:T(8,128)(2,1)S(1)}, u32[]{:S(2)}, u32[]{:S(2)}) collective-permute-start(bf16[12,128,128]{2,1,0:T(8,128)(2,1)S(1)} %get-tuple-element.55), channel_id=1, source_target_pairs={{0,16},{16,0},{1,17},{17,1},{2,18},{18,2},{3,19},{19,3},{4,20},{20... | collective-permute-start | bytes 1179656 | tf_op jit(solution)/shard_map/ppermute | solution.py:397
  42.4 7.6 %collective-permute-start.4 = (bf16[392,128]{1,0:T(8,128)(2,1)S(1)}, bf16[392,128]{1,0:T(8,128)(2,1)S(1)}, u32[]{:S(2)}, u32[]{:S(2)}) collective-permute-start(bf16[392,128]{1,0:T(8,128)(2,1)S(1)} %get-tuple-element.72), channel_id=1, source_target_pairs={{0,2},{1,3},{2,0},{3,1},{4,6},{5,7},{6,4},{7,5},{8,10},{9,11},{10,... | collective-permute-start | bytes 301064 | tf_op jit(solution)/shard_map/ppermute | solution.py:424
  45.7 7.4 %collective-permute-start.15 = (bf16[392,128]{1,0:T(8,128)(2,1)S(1)}, bf16[392,128]{1,0:T(8,128)(2,1)S(1)}, u32[]{:S(2)}, u32[]{:S(2)}) collective-permute-start(bf16[392,128]{1,0:T(8,128)(2,1)S(1)} %get-tuple-element.83), channel_id=1, source_target_pairs={{0,9},{1,8},{2,11},{3,10},{4,13},{5,12},{6,15},{7,14},{8,1},{9,0},... | collective-permute-start | bytes 301064 | tf_op jit(solution)/shard_map/ppermute | solution.py:424
  49.9 7.4 %collective-permute-start.11 = (bf16[392,128]{1,0:T(8,128)(2,1)S(1)}, bf16[392,128]{1,0:T(8,128)(2,1)S(1)}, u32[]{:S(2)}, u32[]{:S(2)}) collective-permute-start(bf16[392,128]{1,0:T(8,128)(2,1)S(1)} %get-tuple-element.79), channel_id=1, source_target_pairs={{0,5},{1,4},{2,7},{3,6},{4,1},{5,0},{6,3},{7,2},{8,13},{9,12},{10,... | collective-permute-start | bytes 301064 | tf_op jit(solution)/shard_map/ppermute | solution.py:424
  50.0 11.1 %collective-permute-start.12 = (bf16[392,128]{1,0:T(8,128)(2,1)S(1)}, bf16[392,128]{1,0:T(8,128)(2,1)S(1)}, u32[]{:S(2)}, u32[]{:S(2)}) collective-permute-start(bf16[392,128]{1,0:T(8,128)(2,1)S(1)} %get-tuple-element.80), channel_id=1, source_target_pairs={{0,6},{1,7},{2,4},{3,5},{4,2},{5,3},{6,0},{7,1},{8,14},{9,15},{10,... | collective-permute-start | bytes 301064 | tf_op jit(solution)/shard_map/ppermute | solution.py:424
  51.3 10.9 %collective-permute-start.13 = (bf16[392,128]{1,0:T(8,128)(2,1)S(1)}, bf16[392,128]{1,0:T(8,128)(2,1)S(1)}, u32[]{:S(2)}, u32[]{:S(2)}) collective-permute-start(bf16[392,128]{1,0:T(8,128)(2,1)S(1)} %get-tuple-element.81), channel_id=1, source_target_pairs={{0,7},{1,6},{2,5},{3,4},{4,3},{5,2},{6,1},{7,0},{8,15},{9,14},{10,... | collective-permute-start | bytes 301064 | tf_op jit(solution)/shard_map/ppermute | solution.py:424
  53.1 12.3 %collective-permute-start.16 = (bf16[392,128]{1,0:T(8,128)(2,1)S(1)}, bf16[392,128]{1,0:T(8,128)(2,1)S(1)}, u32[]{:S(2)}, u32[]{:S(2)}) collective-permute-start(bf16[392,128]{1,0:T(8,128)(2,1)S(1)} %get-tuple-element.84), channel_id=1, source_target_pairs={{0,10},{1,11},{2,8},{3,9},{4,14},{5,15},{6,12},{7,13},{8,2},{9,3},... | collective-permute-start | bytes 301064 | tf_op jit(solution)/shard_map/ppermute | solution.py:424
  55.3 11.2 %collective-permute-start.6 = (bf16[392,128]{1,0:T(8,128)(2,1)S(1)}, bf16[392,128]{1,0:T(8,128)(2,1)S(1)}, u32[]{:S(2)}, u32[]{:S(2)}) collective-permute-start(bf16[392,128]{1,0:T(8,128)(2,1)S(1)} %get-tuple-element.74), channel_id=1, source_target_pairs={{0,12},{1,13},{2,14},{3,15},{4,8},{5,9},{6,10},{7,11},{8,4},{9,5},... | collective-permute-start | bytes 301064 | tf_op jit(solution)/shard_map/ppermute | solution.py:424
  57.4 17.5 %collective-permute-start.7 = (bf16[392,128]{1,0:T(8,128)(2,1)S(1)}, bf16[392,128]{1,0:T(8,128)(2,1)S(1)}, u32[]{:S(2)}, u32[]{:S(2)}) collective-permute-start(bf16[392,128]{1,0:T(8,128)(2,1)S(1)} %get-tuple-element.75), channel_id=1, source_target_pairs={{0,13},{1,12},{2,15},{3,14},{4,9},{5,8},{6,11},{7,10},{8,5},{9,4},... | collective-permute-start | bytes 301064 | tf_op jit(solution)/shard_map/ppermute | solution.py:424
  61.1 16.1 %collective-permute-start.8 = (bf16[392,128]{1,0:T(8,128)(2,1)S(1)}, bf16[392,128]{1,0:T(8,128)(2,1)S(1)}, u32[]{:S(2)}, u32[]{:S(2)}) collective-permute-start(bf16[392,128]{1,0:T(8,128)(2,1)S(1)} %get-tuple-element.76), channel_id=1, source_target_pairs={{0,14},{1,15},{2,12},{3,13},{4,10},{5,11},{6,8},{7,9},{8,6},{9,7},... | collective-permute-start | bytes 301064 | tf_op jit(solution)/shard_map/ppermute | solution.py:424
  62.2 22.4 %collective-permute-start.9 = (bf16[392,128]{1,0:T(8,128)(2,1)S(1)}, bf16[392,128]{1,0:T(8,128)(2,1)S(1)}, u32[]{:S(2)}, u32[]{:S(2)}) collective-permute-start(bf16[392,128]{1,0:T(8,128)(2,1)S(1)} %get-tuple-element.77), channel_id=1, source_target_pairs={{0,15},{1,14},{2,13},{3,12},{4,11},{5,10},{6,9},{7,8},{8,7},{9,6},... | collective-permute-start | bytes 301064 | tf_op jit(solution)/shard_map/ppermute | solution.py:424
  65.5 35.3 %collective-permute-start.27 = (bf16[1536,128]{1,0:T(8,128)(2,1)S(1)}, bf16[1536,128]{1,0:T(8,128)(2,1)S(1)}, u32[]{:S(2)}, u32[]{:S(2)}) collective-permute-start(bf16[1536,128]{1,0:T(8,128)(2,1)S(1)} %shard_map.109), channel_id=1, source_target_pairs={{0,16},{16,0},{1,17},{17,1},{2,18},{18,2},{3,19},{19,3},{4,20},{20... | collective-permute-start | bytes 1179656 | tf_op jit(solution)/shard_map/ppermute | solution.py:453
  66.5 18.7 %collective-permute-start.17 = (bf16[392,128]{1,0:T(8,128)(2,1)S(1)}, bf16[392,128]{1,0:T(8,128)(2,1)S(1)}, u32[]{:S(2)}, u32[]{:S(2)}) collective-permute-start(bf16[392,128]{1,0:T(8,128)(2,1)S(1)} %get-tuple-element.85), channel_id=1, source_target_pairs={{0,11},{1,10},{2,9},{3,8},{4,15},{5,14},{6,13},{7,12},{8,3},{9,2},... | collective-permute-start | bytes 301064 | tf_op jit(solution)/shard_map/ppermute | solution.py:424
  74.8 12.0 %collective-permute-start.5 = (bf16[392,128]{1,0:T(8,128)(2,1)S(1)}, bf16[392,128]{1,0:T(8,128)(2,1)S(1)}, u32[]{:S(2)}, u32[]{:S(2)}) collective-permute-start(bf16[392,128]{1,0:T(8,128)(2,1)S(1)} %get-tuple-element.73), channel_id=1, source_target_pairs={{0,3},{1,2},{2,1},{3,0},{4,7},{5,6},{6,5},{7,4},{8,11},{9,10},{10,... | collective-permute-start | bytes 301064 | tf_op jit(solution)/shard_map/ppermute | solution.py:424
  77.2 10.5 %collective-permute-start.14 = (bf16[392,128]{1,0:T(8,128)(2,1)S(1)}, bf16[392,128]{1,0:T(8,128)(2,1)S(1)}, u32[]{:S(2)}, u32[]{:S(2)}) collective-permute-start(bf16[392,128]{1,0:T(8,128)(2,1)S(1)} %get-tuple-element.82), channel_id=1, source_target_pairs={{0,8},{1,9},{2,10},{3,11},{4,12},{5,13},{6,14},{7,15},{8,0},{9,1},... | collective-permute-start | bytes 301064 | tf_op jit(solution)/shard_map/ppermute | solution.py:424
  85.2 10.2 %collective-permute-start.26 = (bf16[768,128]{1,0:T(8,128)(2,1)S(1)}, bf16[768,128]{1,0:T(8,128)(2,1)S(1)}, u32[]{:S(2)}, u32[]{:S(2)}) collective-permute-start(bf16[768,128]{1,0:T(8,128)(2,1)S(1)} %shard_map.108), channel_id=1, source_target_pairs={{0,16},{16,0},{1,17},{17,1},{2,18},{18,2},{3,19},{19,3},{4,20},{20... | collective-permute-start | bytes 589832 | tf_op jit(solution)/shard_map/ppermute | solution.py:453
  86.9 19.1 %collective-permute-start.21 = (bf16[768,128]{1,0:T(8,128)(2,1)S(1)}, bf16[768,128]{1,0:T(8,128)(2,1)S(1)}, u32[]{:S(2)}, u32[]{:S(2)}) collective-permute-start(bf16[768,128]{1,0:T(8,128)(2,1)S(1)} %shard_map.105), channel_id=1, source_target_pairs={{0,16},{16,0},{1,17},{17,1},{2,18},{18,2},{3,19},{19,3},{4,20},{20... | collective-permute-start | bytes 589832 | tf_op jit(solution)/shard_map/ppermute | solution.py:453
  87.7 18.3 %collective-permute-start.22 = (bf16[768,128]{1,0:T(8,128)(2,1)S(1)}, bf16[768,128]{1,0:T(8,128)(2,1)S(1)}, u32[]{:S(2)}, u32[]{:S(2)}) collective-permute-start(bf16[768,128]{1,0:T(8,128)(2,1)S(1)} %shard_map.106), channel_id=1, source_target_pairs={{0,16},{16,0},{1,17},{17,1},{2,18},{18,2},{3,19},{19,3},{4,20},{20... | collective-permute-start | bytes 589832 | tf_op jit(solution)/shard_map/ppermute | solution.py:453
  91.2 14.8 %collective-permute-start.20 = (bf16[384,128]{1,0:T(8,128)(2,1)S(1)}, bf16[384,128]{1,0:T(8,128)(2,1)S(1)}, u32[]{:S(2)}, u32[]{:S(2)}) collective-permute-start(bf16[384,128]{1,0:T(8,128)(2,1)S(1)} %shard_map.104), channel_id=1, source_target_pairs={{0,16},{16,0},{1,17},{17,1},{2,18},{18,2},{3,19},{19,3},{4,20},{20... | collective-permute-start | bytes 294920 | tf_op jit(solution)/shard_map/ppermute | solution.py:453
  95.4 10.6 %collective-permute-start.23 = (bf16[8,128]{1,0:T(8,128)(2,1)S(1)}, bf16[8,128]{1,0:T(8,128)(2,1)S(1)}, u32[]{:S(2)}, u32[]{:S(2)}) collective-permute-start(bf16[8,128]{1,0:T(8,128)(2,1)S(1)} %get-tuple-element.89.refs_6_), channel_id=1, source_target_pairs={{0,16},{16,0},{1,17},{17,1},{2,18},{18,2},{3,19},{19,3},{4,20},{20... | collective-permute-start | bytes 6152 | tf_op jit(solution)/shard_map/ppermute | solution.py:452
  100.8 8.5 %collective-permute-start.19 = (bf16[768,128]{1,0:T(8,128)(2,1)S(1)}, bf16[768,128]{1,0:T(8,128)(2,1)S(1)}, u32[]{:S(2)}, u32[]{:S(2)}) collective-permute-start(bf16[768,128]{1,0:T(8,128)(2,1)S(1)} %get-tuple-element.88), channel_id=1, source_target_pairs={{0,16},{16,0},{1,17},{17,1},{2,18},{18,2},{3,19},{19,3},{4,20},{20... | collective-permute-start | bytes 589832 | tf_op jit(solution)/shard_map/ppermute | solution.py:453
  (4 other events, 24.9 us)
